TPU v7x, 128 devices: a whole 4x4x4 slice. The times are simulated.
128 devices in a mesh: gx: 4 (over z_hi, core), gy: 4 (over x), gz: 8 (over y, z_lo).
Axes of the slice: x: 4, y: 4, z: 4 (z_hi: 2, z_lo: 2; z = z_hi * 2 + z_lo), core: 2. Of those that a mesh axis runs over, the one named last changes fastest.
Arguments:
- x_a: bfloat16 [32, 8, 64, 1024], P(None, 'gx', 'gy', 'gz'), may hold values from -12 to 12
- x_b: bfloat16 [32, 8, 64, 1024], P(None, 'gx', 'gy', 'gz'), may hold values from -12 to 12
- w_first: bfloat16 [3, 3, 3, 32, 32], replicated, may hold values from -0.21875 to 0.21875
- w_second: bfloat16 [3, 3, 3, 32, 32], replicated, may hold values from -0.21875 to 0.21875
- gain_first: float32 [32], replicated, may hold values from 0.1 to 1.9
- bias_first: float32 [32], replicated, may hold values from -2 to 2
- gain_second: float32 [32], replicated, may hold values from 0.1 to 1.9
- bias_second: float32 [32], replicated, may hold values from -2 to 2
- grad_out: bfloat16 [32, 8, 64, 1024], P(None, 'gx', 'gy', 'gz'), may hold values from -6 to 6
Outputs:
- y_a: bfloat16 [32, 8, 64, 1024], P(None, 'gx', 'gy', 'gz')
- dx_b: bfloat16 [32, 8, 64, 1024], P(None, 'gx', 'gy', 'gz')
- grad_w_first: float32 [3, 3, 3, 32, 32], replicated
- grad_w_second: float32 [3, 3, 3, 32, 32], replicated
- grad_norm: float32 [4, 32], replicated
All inputs are finite; a program needn't handle non-finite values.
Results may differ from a plain program's by a relative error of at most 0.0063.
Values may be sent and summed in bfloat16 or wider, within the bound.
A program may use at most 128 MiB of HBM per device.

v0:
```python
import functools
import math

import jax
import jax.numpy as jnp
from jax import lax
from jax.sharding import Mesh
from jax.sharding import PartitionSpec as P

GX_GY_GZ = ("gx_0", "gx_1", "gy", "gz_0", "gz_1")
GX = ("gx_0", "gx_1")
GZ = ("gz_0", "gz_1")


EPSILON = 1e-05


def by_axis(value, axes):
    return functools.reduce(lax.psum, axes, value)


def extended(block, sides, width):
    for axis, dim in sides:
        count = lax.axis_size(axis)
        forward = [(i, i + 1) for i in range(count - 1)]
        backward = [(target, source) for source, target in forward]
        low = lax.ppermute(
            lax.slice_in_dim(block, block.shape[dim] - width, None, axis=dim), axis, forward
        )
        high = lax.ppermute(lax.slice_in_dim(block, 0, width, axis=dim), axis, backward)
        block = jnp.concatenate([low, block, high], axis=dim)
    return block


def spread(values):
    return values[:, None, None, None]


def silu_slope(value):
    sigma = jax.nn.sigmoid(value)
    return sigma * (1.0 + value * (1.0 - sigma))


def convolve(padded, weight):
    in_chan = padded.shape[0]
    out_chan = weight.shape[3]
    span_x = padded.shape[1] - 2
    span_y = padded.shape[2] - 2
    span_z = padded.shape[3] - 2
    total = jnp.zeros((out_chan, span_x * span_y * span_z), jnp.float32)
    for shift_x in range(3):
        for shift_y in range(3):
            pieces = [
                padded[
                    :,
                    shift_x : shift_x + span_x,
                    shift_y : shift_y + span_y,
                    shift_z : shift_z + span_z,
                ]
                for shift_z in range(3)
            ]
            stacked = jnp.concatenate(pieces, axis=0).reshape(3 * in_chan, -1)
            matrix = weight[shift_x, shift_y].transpose(1, 0, 2).reshape(out_chan, 3 * in_chan)
            total = total + jnp.dot(matrix, stacked, preferred_element_type=jnp.float32)
    return total.reshape(out_chan, span_x, span_y, span_z)


def kernel_grad(padded, upstream):
    in_chan = padded.shape[0]
    out_chan = upstream.shape[0]
    span_x, span_y, span_z = (upstream.shape[1], upstream.shape[2], upstream.shape[3])
    flat = upstream.reshape(out_chan, -1)
    rows = []
    for shift_x in range(3):
        for shift_y in range(3):
            pieces = [
                padded[
                    :,
                    shift_x : shift_x + span_x,
                    shift_y : shift_y + span_y,
                    shift_z : shift_z + span_z,
                ]
                for shift_z in range(3)
            ]
            stacked = jnp.concatenate(pieces, axis=0).reshape(3 * in_chan, -1)
            product = lax.dot_general(
                flat, stacked, (((1,), (1,)), ((), ())), preferred_element_type=jnp.float32
            )
            rows.append(product.reshape(out_chan, 3, in_chan).transpose(1, 0, 2))
    return jnp.stack(rows).reshape(3, 3, 3, out_chan, in_chan)


def flipped(weight):
    return jnp.flip(weight, (0, 1, 2)).transpose(0, 1, 2, 4, 3)


def statistics(blocks, voxels):
    local_sums = jnp.stack([jnp.sum(block, axis=(1, 2, 3)) for block in blocks])
    local_squares = jnp.stack([jnp.sum(jnp.square(block), axis=(1, 2, 3)) for block in blocks])
    sums, squares = (by_axis(local_sums, GX_GY_GZ), by_axis(local_squares, GX_GY_GZ))
    means = sums / voxels
    variance = squares / voxels - means * means
    return (means, lax.rsqrt(variance + EPSILON))


def normalize(block, means, scales, gain, bias):
    normed = (block - spread(means)) * spread(scales)
    return (normed, spread(gain) * normed + spread(bias))


def backward_layer(upstream, preact, normed, scales, gain, voxels):
    slope = upstream * silu_slope(preact)
    sum_d, sum_dx = (
        by_axis(jnp.sum(slope, axis=(1, 2, 3)), GX_GY_GZ),
        by_axis(jnp.sum(slope * normed, axis=(1, 2, 3)), GX_GY_GZ),
    )
    delta = spread(gain * scales) * (
        slope - spread(sum_d / voxels) - normed * spread(sum_dx / voxels)
    )
    return (delta.astype(jnp.bfloat16), sum_d, sum_dx)


def body(x_a, x_b, w_first, w_second, gain_first, bias_first, gain_second, bias_second, grad_out):
    rows_x, rows_y, rows_z = (x_a.shape[1], x_a.shape[2], x_a.shape[3])
    voxels = float(
        rows_x * rows_y * rows_z * lax.axis_size(GX) * lax.axis_size("gy") * lax.axis_size(GZ)
    )
    factor = 1.0 / math.sqrt(voxels)
    volumes = jnp.stack([x_a, x_b])
    padded = extended(volumes, ((GX, 2), ("gy", 3), (GZ, 4)), 1)
    first = [convolve(padded[member], w_first) for member in range(2)]
    means, scales = statistics(first, voxels)
    hidden = []
    for member in range(2):
        normed, preact = normalize(
            first[member], means[member], scales[member], gain_first, bias_first
        )
        hidden.append((preact * jax.nn.sigmoid(preact)).astype(jnp.bfloat16))
    hidden_all = extended(jnp.stack(hidden), ((GX, 2), ("gy", 3), (GZ, 4)), 1)
    hidden_pads = [hidden_all[0], hidden_all[1]]
    input_pad_b = padded[1]
    scale_one = scales[1]
    second = [convolve(hidden_pads[member], w_second) for member in range(2)]
    means_two, scales_two = statistics(second, voxels)
    normed_a, preact_a = normalize(second[0], means_two[0], scales_two[0], gain_second, bias_second)
    y_a = (preact_a * jax.nn.sigmoid(preact_a)).astype(jnp.bfloat16)
    norm_two, pre_two = normalize(second[1], means_two[1], scales_two[1], gain_second, bias_second)
    delta_two, sum_d2, sum_x2 = backward_layer(
        grad_out.astype(jnp.float32), pre_two, norm_two, scales_two[1], gain_second, voxels
    )
    local_second = kernel_grad(hidden_pads[1], delta_two) * factor
    grad_w_second = lax.psum(local_second, GX_GY_GZ)
    delta_pad_two = extended(delta_two, ((GX, 1), ("gy", 2), (GZ, 3)), 1)
    upstream_one = convolve(delta_pad_two, flipped(w_second))
    delta_one, sum_d1, sum_x1 = backward_layer(
        upstream_one, preact, normed, scale_one, gain_first, voxels
    )
    local_first = kernel_grad(input_pad_b, delta_one) * factor
    delta_pad_one = extended(delta_one, ((GX, 1), ("gy", 2), (GZ, 3)), 1)
    dx_b = convolve(delta_pad_one, flipped(w_first)).astype(jnp.bfloat16)
    grad_w_first = lax.psum(local_first, GX_GY_GZ)
    grad_norm = jnp.stack([sum_x1, sum_d1, sum_x2, sum_d2]) * factor
    return (y_a, dx_b, grad_w_first, grad_w_second, grad_norm)


def solution(mesh):
    torus = Mesh(
        mesh.devices.reshape(2, 2, mesh.shape["gy"], 4, 2), ("gx_0", "gx_1", "gy", "gz_0", "gz_1")
    )
    in_specs = (
        P(None, GX, "gy", GZ),
        P(None, GX, "gy", GZ),
        P(),
        P(),
        P(),
        P(),
        P(),
        P(),
        P(None, GX, "gy", GZ),
    )
    out_specs = (P(None, GX, "gy", GZ), P(None, GX, "gy", GZ), P(), P(), P())
    return jax.shard_map(body, mesh=torus, in_specs=in_specs, out_specs=out_specs, check_vma=False)
```

profile of v0, /device:TPU:1, one launch (start us, length us, event | category | flops | bytes accessed | tf_op | source)
XLA Modules:
  0.0 573.7 jit_solution(8080305644700961799)
XLA Ops:
  8.4 6.9 %collective-permute-start = (bf16[2,32,1,16,128]{4,3,2,1,0:T(8,128)(2,1)S(1)}, bf16[2,32,1,16,128]{4,3,2,1,0:T(8,128)(2,1)S(1)}, u32[]{:S(2)}, u32[]{:S(2)}) collective-permute-start(bf16[2,32,1,16,128]{4,3,2,1,0:T(8,128)(2,1)S(1)} %get-tuple-element.259), channel_id=1, source_target_pairs={{0,32},{32,64},{64,96},{1,33},{33,65},{65,97},{2,34},{34,66},{66,9... | collective-permute-start | bytes 786440 | tf_op jit(solution)/shard_map/ppermute | solution.py:27
  15.3 1.9 collective-permute-start.1
  18.6 5.9 %collective-permute-done.1 = bf16[2,32,1,16,128]{4,3,2,1,0:T(8,128)(2,1)S(1)} collective-permute-done((bf16[2,32,1,16,128]{4,3,2,1,0:T(8,128)(2,1)S(1)}, bf16[2,32,1,16,128]{4,3,2,1,0:T(8,128)(2,1)S(1)}, u32[]{:S(2)}, u32[]{:S(2)}) %collective-permute-start.1) | collective-permute-done | bytes 262176 | tf_op jit(solution)/shard_map/ppermute | solution.py:30
  24.7 3.7 copy.460
  29.6 3.1 collective-permute-start.2
  36.1 3.8 collective-permute-done.3
  39.9 6.2 %pad_maximum_fusion = bf16[2,32,4,18,128]{1,2,4,3,0:T(4,128)(2,1)S(1)} fusion(bf16[2,32,4,1,128]{1,2,4,3,0:T(4,128)(2,1)S(1)} %collective-permute-done.3, bf16[2,32,4,16,128]{1,2,4,3,0:T(4,128)(2,1)} %copy.460, bf16[2,32,4,1,128]{1,2,4,3,0:T(4,128)(2,1)S(1)} %collective-permute-done.2), kind=kLoop, calls=%fused_computation | loop fusion | flops 1179648 | bytes 2359296 | tf_op jit(solution)/shard_map/concatenate | solution.py:31
  46.1 2.2 copy-done
  48.3 3.3 collective-permute-start.4
  58.7 6.3 %copy.464 = bf16[2,32,4,18,128]{4,1,3,2,0:T(8,128)(2,1)S(1)} copy(bf16[2,32,4,18,128]{1,2,4,3,0:T(4,128)(2,1)} %copy-done) | data formatting | bytes 2359296 | tf_op jit(solution)/shard_map/concatenate | solution.py:31
  66.0 1.7 copy.463
  72.2 3.3 fusion.175
  99.3 5.3 all-reduce.20
  104.6 2.5 all-reduce.16
  107.0 7.2 %all-reduce.8 = (f32[2,32]{1,0:T(2,128)S(1)}, f32[2,32]{1,0:T(2,128)S(1)}) all-reduce(f32[2,32]{1,0:T(2,128)S(1)} %get-tuple-element.61, f32[2,32]{1,0:T(2,128)S(1)} %get-tuple-element.62), channel_id=1, replica_groups=mesh['gx_0'=2,'gx_1'=2,'gy'=4,'gz_0'=4,'gz_1'=2] {'gy'}, use_global_device_ids=true, to_apply=%region_11.0 | all-reduce | flops 128 | bytes 1024 | tf_op jit(solution)/shard_map/psum | solution.py:19
  114.2 10.4 %all-reduce.4 = (f32[2,32]{1,0:T(2,128)S(1)}, f32[2,32]{1,0:T(2,128)S(1)}) all-reduce(f32[2,32]{1,0:T(2,128)S(1)} %get-tuple-element.45, f32[2,32]{1,0:T(2,128)S(1)} %get-tuple-element.46), channel_id=1, replica_groups=mesh['gx_0'=2,'gx_1'=2,'gy'=4,'gz_0'=4,'gz_1'=2] {'gz_0'}, use_global_device_ids=true, to_apply=%region_12.0 | all-reduce | flops 128 | bytes 1024 | tf_op jit(solution)/shard_map/psum | solution.py:19
  124.6 3.8 all-reduce.12
  130.7 10.1 %collective-permute-start.6 = (bf16[2,32,1,16,128]{4,3,2,1,0:T(8,128)(2,1)S(1)}, bf16[2,32,1,16,128]{4,3,2,1,0:T(8,128)(2,1)S(1)}, u32[]{:S(2)}, u32[]{:S(2)}) collective-permute-start(bf16[2,32,1,16,128]{4,3,2,1,0:T(8,128)(2,1)S(1)} %get-tuple-element.257), channel_id=1, source_target_pairs={{0,32},{32,64},{64,96},{1,33},{33,65},{65,97},{2,34},{34,66},{66,9... | collective-permute-start | bytes 786440 | tf_op jit(solution)/shard_map/ppermute | solution.py:27
  140.7 1.9 collective-permute-start.7
  144.0 5.9 %collective-permute-done.7 = bf16[2,32,1,16,128]{4,3,2,1,0:T(8,128)(2,1)S(1)} collective-permute-done((bf16[2,32,1,16,128]{4,3,2,1,0:T(8,128)(2,1)S(1)}, bf16[2,32,1,16,128]{4,3,2,1,0:T(8,128)(2,1)S(1)}, u32[]{:S(2)}, u32[]{:S(2)}) %collective-permute-start.7) | collective-permute-done | bytes 262176 | tf_op jit(solution)/shard_map/ppermute | solution.py:30
  151.0 5.6 copy.493
  156.7 2.1 fusion.165
  158.7 2.2 collective-permute-start.8
  168.4 6.3 %pad_maximum_fusion.1 = bf16[2,32,4,18,128]{1,2,4,3,0:T(4,128)(2,1)S(1)} fusion(bf16[2,32,4,1,128]{1,2,4,3,0:T(4,128)(2,1)} %collective-permute-done.9, bf16[2,32,4,16,128]{1,2,4,3,0:T(4,128)(2,1)} %copy.493, bf16[2,32,4,1,128]{1,2,4,3,0:T(4,128)(2,1)S(1)} %collective-permute-done.8), kind=kLoop, calls=%fused_computation.1 | loop fusion | flops 1179648 | bytes 2359296 | tf_op jit(solution)/shard_map/concatenate | solution.py:31
  174.7 2.2 copy-done.1
  176.8 1.7 collective-permute-start.10
  182.4 2.2 dot_general.394
  192.0 7.1 %copy.497 = bf16[2,32,4,18,128]{4,1,3,2,0:T(8,128)(2,1)} copy(bf16[2,32,4,18,128]{1,2,4,3,0:T(4,128)(2,1)} %copy-done.1) | data formatting | bytes 2359296 | tf_op jit(solution)/shard_map/concatenate | solution.py:31
  201.1 2.6 pad_maximum_fusion.3
  203.8 1.8 fusion.174
  205.7 3.1 fusion.173
  210.0 3.0 fusion.171
  240.4 2.2 dot_general.408
  246.5 2.2 dot_general.404
  254.1 5.3 all-reduce.19
  259.4 2.5 all-reduce.15
  261.9 8.3 %all-reduce.7 = (f32[2,32]{1,0:T(2,128)S(1)}, f32[2,32]{1,0:T(2,128)S(1)}) all-reduce(f32[2,32]{1,0:T(2,128)S(1)} %get-tuple-element.59, f32[2,32]{1,0:T(2,128)S(1)} %get-tuple-element.60), channel_id=1, replica_groups=mesh['gx_0'=2,'gx_1'=2,'gy'=4,'gz_0'=4,'gz_1'=2] {'gy'}, use_global_device_ids=true, to_apply=%region_25.0 | all-reduce | flops 128 | bytes 1024 | tf_op jit(solution)/shard_map/psum | solution.py:19
  270.2 8.6 %all-reduce.3 = (f32[2,32]{1,0:T(2,128)S(1)}, f32[2,32]{1,0:T(2,128)S(1)}) all-reduce(f32[2,32]{1,0:T(2,128)S(1)} %get-tuple-element.43, f32[2,32]{1,0:T(2,128)S(1)} %get-tuple-element.44), channel_id=1, replica_groups=mesh['gx_0'=2,'gx_1'=2,'gy'=4,'gz_0'=4,'gz_1'=2] {'gz_0'}, use_global_device_ids=true, to_apply=%region_26.0 | all-reduce | flops 128 | bytes 1024 | tf_op jit(solution)/shard_map/psum | solution.py:19
  278.8 3.8 all-reduce.11
  282.8 1.9 fusion.162
  284.6 5.3 all-reduce.18
  289.9 8.6 %all-reduce.14 = (f32[32]{0:T(128)S(1)}, f32[32]{0:T(128)S(1)}) all-reduce(f32[32]{0:T(128)S(1)} %get-tuple-element.65, f32[32]{0:T(128)S(1)} %get-tuple-element.66), channel_id=1, replica_groups=mesh['gx_0'=2,'gx_1'=2,'gy'=4,'gz_0'=4,'gz_1'=2] {'gx_1'}, use_global_device_ids=true, to_apply=%region_36.0 | all-reduce | flops 64 | bytes 512 | tf_op jit(solution)/shard_map/psum | solution.py:19
  298.5 6.1 %all-reduce.6 = (f32[32]{0:T(128)S(1)}, f32[32]{0:T(128)S(1)}) all-reduce(f32[32]{0:T(128)S(1)} %get-tuple-element.57, f32[32]{0:T(128)S(1)} %get-tuple-element.58), channel_id=1, replica_groups=mesh['gx_0'=2,'gx_1'=2,'gy'=4,'gz_0'=4,'gz_1'=2] {'gy'}, use_global_device_ids=true, to_apply=%region_37.0 | all-reduce | flops 64 | bytes 512 | tf_op jit(solution)/shard_map/psum | solution.py:19
  304.6 6.2 %all-reduce.2 = (f32[32]{0:T(128)S(1)}, f32[32]{0:T(128)S(1)}) all-reduce(f32[32]{0:T(128)S(1)} %get-tuple-element.41, f32[32]{0:T(128)S(1)} %get-tuple-element.42), channel_id=1, replica_groups=mesh['gx_0'=2,'gx_1'=2,'gy'=4,'gz_0'=4,'gz_1'=2] {'gz_0'}, use_global_device_ids=true, to_apply=%region_38.0 | all-reduce | flops 64 | bytes 512 | tf_op jit(solution)/shard_map/psum | solution.py:19
  310.7 3.9 all-reduce.10
  318.2 9.4 %collective-permute-start.12 = (bf16[32,1,16,128]{3,0,2,1:T(8,128)(2,1)}, bf16[32,1,16,128]{3,0,2,1:T(8,128)(2,1)S(1)}, u32[]{:S(2)}, u32[]{:S(2)}) collective-permute-start(bf16[32,1,16,128]{3,0,2,1:T(8,128)(2,1)} %get-tuple-element.269), channel_id=1, source_target_pairs={{0,32},{32,64},{64,96},{1,33},{33,65},{65,97},{2,34},{34,66},{66,9... | collective-permute-start | bytes 393224 | tf_op jit(solution)/shard_map/ppermute | solution.py:27
  327.6 2.1 collective-permute-start.13
  336.4 3.4 collective-permute-start.14
  342.8 1.7 collective-permute-done.15
  348.0 4.0 collective-permute-start.16
  355.0 2.2 maximum_maximum_fusion
  366.1 5.4 all-reduce.17
  371.5 5.9 %all-reduce.13 = (f32[32]{0:T(128)S(1)}, f32[32]{0:T(128)S(1)}) all-reduce(f32[32]{0:T(128)S(1)} %get-tuple-element.63, f32[32]{0:T(128)S(1)} %get-tuple-element.64), channel_id=1, replica_groups=mesh['gx_0'=2,'gx_1'=2,'gy'=4,'gz_0'=4,'gz_1'=2] {'gx_1'}, use_global_device_ids=true, to_apply=%region_48.49 | all-reduce | flops 64 | bytes 512 | tf_op jit(solution)/shard_map/psum | solution.py:19
  377.4 6.1 %all-reduce.5 = (f32[32]{0:T(128)S(1)}, f32[32]{0:T(128)S(1)}) all-reduce(f32[32]{0:T(128)S(1)} %get-tuple-element.55, f32[32]{0:T(128)S(1)} %get-tuple-element.56), channel_id=1, replica_groups=mesh['gx_0'=2,'gx_1'=2,'gy'=4,'gz_0'=4,'gz_1'=2] {'gy'}, use_global_device_ids=true, to_apply=%region_49.50 | all-reduce | flops 64 | bytes 512 | tf_op jit(solution)/shard_map/psum | solution.py:19
  383.5 10.0 %all-reduce.1 = (f32[32]{0:T(128)S(1)}, f32[32]{0:T(128)S(1)}) all-reduce(f32[32]{0:T(128)S(1)} %get-tuple-element.39, f32[32]{0:T(128)S(1)} %get-tuple-element.40), channel_id=1, replica_groups=mesh['gx_0'=2,'gx_1'=2,'gy'=4,'gz_0'=4,'gz_1'=2] {'gz_0'}, use_global_device_ids=true, to_apply=%region_50.51 | all-reduce | flops 64 | bytes 512 | tf_op jit(solution)/shard_map/psum | solution.py:19
  393.5 3.8 all-reduce.9
  398.3 10.4 %collective-permute-start.18 = (bf16[32,1,16,128]{3,0,2,1:T(8,128)(2,1)S(1)}, bf16[32,1,16,128]{3,0,2,1:T(8,128)(2,1)S(1)}, u32[]{:S(2)}, u32[]{:S(2)}) collective-permute-start(bf16[32,1,16,128]{3,0,2,1:T(8,128)(2,1)S(1)} %get-tuple-element.264), channel_id=1, source_target_pairs={{0,32},{32,64},{64,96},{1,33},{33,65},{65,97},{2,34},{34,66},{66,9... | collective-permute-start | bytes 393224 | tf_op jit(solution)/shard_map/ppermute | solution.py:27
  408.7 2.3 collective-permute-start.19
  417.4 3.6 collective-permute-start.20
  423.0 2.8 collective-permute-done.21
  428.7 4.0 collective-permute-start.22
  444.8 118.3 %all-reduce.23.cloned.1.call-done = (f32[3,3,3,32,32]{4,3,2,1,0:T(8,128)}, f32[3,3,3,32,32]{4,3,2,1,0:T(8,128)}) async-done(((f32[3,3,3,32,32]{4,3,2,1,0:T(8,128)}, f32[3,3,3,32,32]{4,3,2,1,0:T(8,128)}), (f32[3,3,3,32,32]{4,3,2,1,0:T(8,128)}, f32[3,3,3,32,32]{4,3,2,1,0:T(8,128)})) %all-reduce.23.cloned.1.call-update) | async-done | bytes 221200 | tf_op jit(solution)/shard_map/psum | solution.py:161
  563.0 1.8 copy.917
  564.8 1.8 copy.918
  (639 shorter events, 157.5 us)
Async XLA Ops:
  7.2 17.4 %copy-start.99 = (bf16[32,2,16,128]{3,2,1,0:T(8,128)(2,1)S(1)}, bf16[32,2,16,128]{3,2,1,0:T(8,128)(2,1)}, u32[]{:S(2)}) copy-start(bf16[32,2,16,128]{3,2,1,0:T(8,128)(2,1)} %param.10) | copy-start | bytes 786436
  7.2 17.3 %copy-start.98 = (bf16[32,2,16,128]{3,2,1,0:T(8,128)(2,1)S(1)}, bf16[32,2,16,128]{3,2,1,0:T(8,128)(2,1)}, u32[]{:S(2)}) copy-start(bf16[32,2,16,128]{3,2,1,0:T(8,128)(2,1)} %param.9) | copy-start | bytes 786436
  7.2 555.8 %all-reduce.23.cloned.1.call-start = ((), (), s32[]{:S(2)}) async-start(), calls=%async_computation | async-start | bytes 1769472 | tf_op jit(solution)/shard_map/psum | solution.py:161
  8.4 10.2 %collective-permute-start = (bf16[2,32,1,16,128]{4,3,2,1,0:T(8,128)(2,1)S(1)}, bf16[2,32,1,16,128]{4,3,2,1,0:T(8,128)(2,1)S(1)}, u32[]{:S(2)}, u32[]{:S(2)}) collective-permute-start(bf16[2,32,1,16,128]{4,3,2,1,0:T(8,128)(2,1)S(1)} %get-tuple-element.259), channel_id=1, source_target_pairs={{0,32},{32,64},{64,96},{1,33},{33,65},{65,97},{2,34},{34,66},{66,9... | collective-permute-start | bytes 786440 | tf_op jit(solution)/shard_map/ppermute | solution.py:27
  15.3 9.2 %collective-permute-start.1 = (bf16[2,32,1,16,128]{4,3,2,1,0:T(8,128)(2,1)S(1)}, bf16[2,32,1,16,128]{4,3,2,1,0:T(8,128)(2,1)S(1)}, u32[]{:S(2)}, u32[]{:S(2)}) collective-permute-start(bf16[2,32,1,16,128]{4,3,2,1,0:T(8,128)(2,1)S(1)} %get-tuple-element.260), channel_id=1, source_target_pairs={{32,0},{64,32},{96,64},{33,1},{65,33},{97,65},{34,2},{66,34},{98,6... | collective-permute-start | bytes 786440 | tf_op jit(solution)/shard_map/ppermute | solution.py:30
  24.7 9.4 %copy-start.101 = (bf16[3,3,3,32,32]{4,3,2,1,0:T(8,128)(2,1)S(1)}, bf16[3,3,3,32,32]{4,3,2,1,0:T(8,128)(2,1)}, u32[]{:S(2)}) copy-start(bf16[3,3,3,32,32]{4,3,2,1,0:T(8,128)(2,1)} %param.12) | copy-start | bytes 165892
  29.6 6.4 %collective-permute-start.2 = (bf16[2,32,4,1,128]{1,2,4,3,0:T(4,128)(2,1)S(1)}, bf16[2,32,4,1,128]{1,2,4,3,0:T(4,128)(2,1)S(1)}, u32[]{:S(2)}, u32[]{:S(2)}) collective-permute-start(bf16[2,32,4,1,128]{1,2,4,3,0:T(4,128)(2,1)S(1)} %get-tuple-element.79), channel_id=1, source_target_pairs={{0,8},{8,16},{16,24},{1,9},{9,17},{17,25},{2,10},{10,18},{18,26},{... | collective-permute-start | bytes 196616 | tf_op jit(solution)/shard_map/ppermute | solution.py:27
  32.8 7.1 %collective-permute-start.3 = (bf16[2,32,4,1,128]{1,2,4,3,0:T(4,128)(2,1)S(1)}, bf16[2,32,4,1,128]{1,2,4,3,0:T(4,128)(2,1)S(1)}, u32[]{:S(2)}, u32[]{:S(2)}) collective-permute-start(bf16[2,32,4,1,128]{1,2,4,3,0:T(4,128)(2,1)S(1)} %get-tuple-element.80), channel_id=1, source_target_pairs={{8,0},{16,8},{24,16},{9,1},{17,9},{25,17},{10,2},{18,10},{26,18},{... | collective-permute-start | bytes 196616 | tf_op jit(solution)/shard_map/ppermute | solution.py:30
  34.8 18.0 %copy-start.100 = (bf16[3,3,3,32,32]{4,3,2,1,0:T(8,128)(2,1)S(1)}, bf16[3,3,3,32,32]{4,3,2,1,0:T(8,128)(2,1)}, u32[]{:S(2)}) copy-start(bf16[3,3,3,32,32]{4,3,2,1,0:T(8,128)(2,1)} %param.11) | copy-start | bytes 165892
  48.3 17.7 %collective-permute-start.4 = (bf16[2,32,4,18,1]{1,2,4,3,0:T(4,128)(2,1)S(1)}, bf16[2,32,4,18,1]{1,2,4,3,0:T(4,128)(2,1)}, u32[]{:S(2)}, u32[]{:S(2)}) collective-permute-start(bf16[2,32,4,18,1]{1,2,4,3,0:T(4,128)(2,1)S(1)} %get-tuple-element.75), channel_id=1, source_target_pairs={{0,1},{1,2},{2,3},{3,4},{4,5},{5,6},{6,7},{8,9},{9,10},{10,11},{11... | collective-permute-start | bytes 27656 | tf_op jit(solution)/shard_map/ppermute | solution.py:27
  51.5 13.5 %collective-permute-start.5 = (bf16[2,32,4,18,1]{1,2,4,3,0:T(4,128)(2,1)S(1)}, bf16[2,32,4,18,1]{1,2,4,3,0:T(4,128)(2,1)S(1)}, u32[]{:S(2)}, u32[]{:S(2)}) collective-permute-start(bf16[2,32,4,18,1]{1,2,4,3,0:T(4,128)(2,1)S(1)} %get-tuple-element.76), channel_id=1, source_target_pairs={{1,0},{2,1},{3,2},{4,3},{5,4},{6,5},{7,6},{9,8},{10,9},{11,10},{12... | collective-permute-start | bytes 27656 | tf_op jit(solution)/shard_map/ppermute | solution.py:30
  80.9 5.1 copy-start.4
  81.7 3.4 copy-start.7
  86.7 43.3 %copy-start.21 = (f32[4,8,32,128]{3,2,1,0:T(8,128)}, f32[4,8,32,128]{3,2,1,0:T(8,128)S(1)}, u32[]{:S(2)}) copy-start(f32[4,8,32,128]{3,2,1,0:T(8,128)S(1)} %copy.596) | copy-start | bytes 1572868
  96.7 33.4 %copy-start.147 = (f32[32]{0:T(128)S(1)}, f32[32]{0:T(128)}, u32[]{:S(2)}) copy-start(f32[32]{0:T(128)} %param.14) | copy-start | bytes 388
  96.8 33.4 %copy-start.149 = (f32[32]{0:T(128)S(1)}, f32[32]{0:T(128)}, u32[]{:S(2)}) copy-start(f32[32]{0:T(128)} %param.13) | copy-start | bytes 388
  130.1 12.6 %copy-start.102 = (bf16[3,3,3,32,32]{4,3,2,1,0:T(8,128)(2,1)S(1)}, bf16[3,3,3,32,32]{4,3,2,1,0:T(8,128)(2,1)}, u32[]{:S(2)}) copy-start(bf16[3,3,3,32,32]{4,3,2,1,0:T(8,128)(2,1)} %param.12) | copy-start | bytes 165892
  130.1 12.6 %copy-start.103 = (bf16[3,3,3,32,32]{3,4,2,1,0:T(8,128)(2,1)S(1)}, bf16[3,3,3,32,32]{3,4,2,1,0:T(8,128)(2,1)}, u32[]{:S(2)}) copy-start(bf16[3,3,3,32,32]{3,4,2,1,0:T(8,128)(2,1)} %reverse_bitcast_fusion) | copy-start | bytes 165892
  130.7 13.4 %collective-permute-start.6 = (bf16[2,32,1,16,128]{4,3,2,1,0:T(8,128)(2,1)S(1)}, bf16[2,32,1,16,128]{4,3,2,1,0:T(8,128)(2,1)S(1)}, u32[]{:S(2)}, u32[]{:S(2)}) collective-permute-start(bf16[2,32,1,16,128]{4,3,2,1,0:T(8,128)(2,1)S(1)} %get-tuple-element.257), channel_id=1, source_target_pairs={{0,32},{32,64},{64,96},{1,33},{33,65},{65,97},{2,34},{34,66},{66,9... | collective-permute-start | bytes 786440 | tf_op jit(solution)/shard_map/ppermute | solution.py:27
  140.7 9.2 %collective-permute-start.7 = (bf16[2,32,1,16,128]{4,3,2,1,0:T(8,128)(2,1)S(1)}, bf16[2,32,1,16,128]{4,3,2,1,0:T(8,128)(2,1)S(1)}, u32[]{:S(2)}, u32[]{:S(2)}) collective-permute-start(bf16[2,32,1,16,128]{4,3,2,1,0:T(8,128)(2,1)S(1)} %get-tuple-element.258), channel_id=1, source_target_pairs={{32,0},{64,32},{96,64},{33,1},{65,33},{97,65},{34,2},{66,34},{98,6... | collective-permute-start | bytes 786440 | tf_op jit(solution)/shard_map/ppermute | solution.py:30
  156.6 10.6 %copy-start.126 = (bf16[32,3,32]{2,0,1:T(8,128)(2,1)S(1)}, bf16[32,3,32]{2,0,1:T(8,128)(2,1)}, u32[]{:S(2)}) copy-start(bf16[32,3,32]{2,0,1:T(8,128)(2,1)} %get-tuple-element.292) | copy-start | bytes 18436
  156.6 10.7 %copy-start.125 = (bf16[32,3,32]{2,0,1:T(8,128)(2,1)S(1)}, bf16[32,3,32]{2,0,1:T(8,128)(2,1)}, u32[]{:S(2)}) copy-start(bf16[32,3,32]{2,0,1:T(8,128)(2,1)} %get-tuple-element.293) | copy-start | bytes 18436
  156.6 10.9 %copy-start.124 = (bf16[32,3,32]{2,0,1:T(8,128)(2,1)S(1)}, bf16[32,3,32]{2,0,1:T(8,128)(2,1)}, u32[]{:S(2)}) copy-start(bf16[32,3,32]{2,0,1:T(8,128)(2,1)} %get-tuple-element.294) | copy-start | bytes 18436
  156.6 11.0 %copy-start.123 = (bf16[32,3,32]{2,0,1:T(8,128)(2,1)S(1)}, bf16[32,3,32]{2,0,1:T(8,128)(2,1)}, u32[]{:S(2)}) copy-start(bf16[32,3,32]{2,0,1:T(8,128)(2,1)} %get-tuple-element.295) | copy-start | bytes 18436
  156.6 11.1 %copy-start.122 = (bf16[32,3,32]{2,0,1:T(8,128)(2,1)S(1)}, bf16[32,3,32]{2,0,1:T(8,128)(2,1)}, u32[]{:S(2)}) copy-start(bf16[32,3,32]{2,0,1:T(8,128)(2,1)} %get-tuple-element.296) | copy-start | bytes 18436
  156.6 11.2 %copy-start.121 = (bf16[32,3,32]{2,0,1:T(8,128)(2,1)S(1)}, bf16[32,3,32]{2,0,1:T(8,128)(2,1)}, u32[]{:S(2)}) copy-start(bf16[32,3,32]{2,0,1:T(8,128)(2,1)} %get-tuple-element.297) | copy-start | bytes 18436
  158.7 9.2 %collective-permute-start.8 = (bf16[2,32,4,1,128]{1,2,4,3,0:T(4,128)(2,1)}, bf16[2,32,4,1,128]{1,2,4,3,0:T(4,128)(2,1)S(1)}, u32[]{:S(2)}, u32[]{:S(2)}) collective-permute-start(bf16[2,32,4,1,128]{1,2,4,3,0:T(4,128)(2,1)} %get-tuple-element.77), channel_id=1, source_target_pairs={{0,8},{8,16},{16,24},{1,9},{9,17},{17,25},{2,10},{10,18},{18,26},{... | collective-permute-start | bytes 196616 | tf_op jit(solution)/shard_map/ppermute | solution.py:27
  160.9 7.4 %collective-permute-start.9 = (bf16[2,32,4,1,128]{1,2,4,3,0:T(4,128)(2,1)}, bf16[2,32,4,1,128]{1,2,4,3,0:T(4,128)(2,1)}, u32[]{:S(2)}, u32[]{:S(2)}) collective-permute-start(bf16[2,32,4,1,128]{1,2,4,3,0:T(4,128)(2,1)} %get-tuple-element.78), channel_id=1, source_target_pairs={{8,0},{16,8},{24,16},{9,1},{17,9},{25,17},{10,2},{18,10},{26,18},{... | collective-permute-start | bytes 196616 | tf_op jit(solution)/shard_map/ppermute | solution.py:30
  168.0 12.0 %copy-start.146 = (f32[2,32]{1,0:T(2,128)S(1)}, f32[2,32]{1,0:T(2,128)}, u32[]{:S(2)}) copy-start(f32[2,32]{1,0:T(2,128)} %copy-done.145) | copy-start | bytes 772
  168.0 12.0 %copy-start.150 = (f32[32]{0:T(128)S(1)}, f32[32]{0:T(128)}, u32[]{:S(2)}) copy-start(f32[32]{0:T(128)} %param.13) | copy-start | bytes 388
  176.8 23.2 %collective-permute-start.10 = (bf16[2,32,4,18,1]{1,2,4,3,0:T(4,128)(2,1)S(1)}, bf16[2,32,4,18,1]{1,2,4,3,0:T(4,128)(2,1)S(1)}, u32[]{:S(2)}, u32[]{:S(2)}) collective-permute-start(bf16[2,32,4,18,1]{1,2,4,3,0:T(4,128)(2,1)S(1)} %get-tuple-element.73), channel_id=1, source_target_pairs={{0,1},{1,2},{2,3},{3,4},{4,5},{5,6},{6,7},{8,9},{9,10},{10,11},{11... | collective-permute-start | bytes 27656 | tf_op jit(solution)/shard_map/ppermute | solution.py:27
  178.6 20.5 %collective-permute-start.11 = (bf16[2,32,4,18,1]{1,2,4,3,0:T(4,128)(2,1)S(1)}, bf16[2,32,4,18,1]{1,2,4,3,0:T(4,128)(2,1)S(1)}, u32[]{:S(2)}, u32[]{:S(2)}) collective-permute-start(bf16[2,32,4,18,1]{1,2,4,3,0:T(4,128)(2,1)S(1)} %get-tuple-element.74), channel_id=1, source_target_pairs={{1,0},{2,1},{3,2},{4,3},{5,4},{6,5},{7,6},{9,8},{10,9},{11,10},{12... | collective-permute-start | bytes 27656 | tf_op jit(solution)/shard_map/ppermute | solution.py:30
  181.2 3.4 copy-start.3
  239.1 3.4 copy-start.61
  239.2 3.4 copy-start.62
  245.2 3.5 copy-start.56
  245.2 3.5 copy-start.57
  253.4 29.2 %copy-start.152 = (f32[32]{0:T(128)S(1)}, f32[32]{0:T(128)}, u32[]{:S(2)}) copy-start(f32[32]{0:T(128)} %param.15) | copy-start | bytes 388
  253.4 29.3 %copy-start.106 = (bf16[32,2,16,128]{3,2,1,0:T(8,128)(2,1)S(1)}, bf16[32,2,16,128]{3,2,1,0:T(8,128)(2,1)}, u32[]{:S(2)}) copy-start(bf16[32,2,16,128]{3,2,1,0:T(8,128)(2,1)} %param.17) | copy-start | bytes 786436
  253.4 29.3 %copy-start.151 = (f32[32]{0:T(128)S(1)}, f32[32]{0:T(128)}, u32[]{:S(2)}) copy-start(f32[32]{0:T(128)} %param.16) | copy-start | bytes 388
  254.0 28.8 %copy-start.43 = (f32[4,8,32,128]{3,2,1,0:T(8,128)S(1)}, f32[4,8,32,128]{3,2,1,0:T(8,128)}, u32[]{:S(2)}) copy-start(f32[4,8,32,128]{3,2,1,0:T(8,128)} %copy.606) | copy-start | bytes 1572868
  316.8 14.5 %copy-start.33 = (bf16[3,32,4096]{2,1,0:T(8,128)(2,1)S(1)}, bf16[3,32,4096]{2,1,0:T(8,128)(2,1)}, u32[]{:S(2)}) copy-start(bf16[3,32,4096]{2,1,0:T(8,128)(2,1)} %dot_general.398) | copy-start | bytes 2359300
  318.1 13.9 %copy-start.36 = (bf16[3,32,4096]{2,1,0:T(8,128)(2,1)S(1)}, bf16[3,32,4096]{2,1,0:T(8,128)(2,1)}, u32[]{:S(2)}) copy-start(bf16[3,32,4096]{2,1,0:T(8,128)(2,1)} %dot_general.400) | copy-start | bytes 2359300
  318.2 18.2 %collective-permute-start.12 = (bf16[32,1,16,128]{3,0,2,1:T(8,128)(2,1)}, bf16[32,1,16,128]{3,0,2,1:T(8,128)(2,1)S(1)}, u32[]{:S(2)}, u32[]{:S(2)}) collective-permute-start(bf16[32,1,16,128]{3,0,2,1:T(8,128)(2,1)} %get-tuple-element.269), channel_id=1, source_target_pairs={{0,32},{32,64},{64,96},{1,33},{33,65},{65,97},{2,34},{34,66},{66,9... | collective-permute-start | bytes 393224 | tf_op jit(solution)/shard_map/ppermute | solution.py:27
  327.6 5.0 copy-start.40
  327.6 8.8 %collective-permute-start.13 = (bf16[32,1,16,128]{3,0,2,1:T(8,128)(2,1)S(1)}, bf16[32,1,16,128]{3,0,2,1:T(8,128)(2,1)S(1)}, u32[]{:S(2)}, u32[]{:S(2)}) collective-permute-start(bf16[32,1,16,128]{3,0,2,1:T(8,128)(2,1)S(1)} %get-tuple-element.270), channel_id=1, source_target_pairs={{32,0},{64,32},{96,64},{33,1},{65,33},{97,65},{34,2},{66,34},{98,6... | collective-permute-start | bytes 393224 | tf_op jit(solution)/shard_map/ppermute | solution.py:30
  335.1 6.8 %copy-start.97 = (bf16[32,2,16,128]{3,0,2,1:T(8,128)(2,1)S(1)}, bf16[32,2,16,128]{3,0,2,1:T(8,128)(2,1)}, u32[]{:S(2)}) copy-start(bf16[32,2,16,128]{3,0,2,1:T(8,128)(2,1)} %get-tuple-element.307) | copy-start | bytes 786436
  336.4 6.3 %collective-permute-start.14 = (bf16[32,4,1,128]{3,0,2,1:T(8,128)(2,1)S(1)}, bf16[32,4,1,128]{3,0,2,1:T(8,128)(2,1)S(1)}, u32[]{:S(2)}, u32[]{:S(2)}) collective-permute-start(bf16[32,4,1,128]{3,0,2,1:T(8,128)(2,1)S(1)} %get-tuple-element.255), channel_id=1, source_target_pairs={{0,8},{8,16},{16,24},{1,9},{9,17},{17,25},{2,10},{10,18},{18,26},{... | collective-permute-start | bytes 98312 | tf_op jit(solution)/shard_map/ppermute | solution.py:27
  339.8 4.7 collective-permute-start.15
  342.8 9.3 %copy-start.104 = (bf16[32,4,1,128]{3,0,2,1:T(8,128)(2,1)}, bf16[32,4,1,128]{3,0,2,1:T(8,128)(2,1)S(1)}, u32[]{:S(2)}) copy-start(bf16[32,4,1,128]{3,0,2,1:T(8,128)(2,1)S(1)} %collective-permute-done.14) | copy-start | bytes 98308
  344.5 7.6 %copy-start.105 = (bf16[32,4,1,128]{3,0,2,1:T(8,128)(2,1)}, bf16[32,4,1,128]{3,0,2,1:T(8,128)(2,1)S(1)}, u32[]{:S(2)}) copy-start(bf16[32,4,1,128]{3,0,2,1:T(8,128)(2,1)S(1)} %collective-permute-done.15) | copy-start | bytes 98308
  346.7 7.0 %collective-permute-start.17 = (bf16[32,4,18,1]{0,2,3,1:T(8,128)(2,1)S(1)}, bf16[32,4,18,1]{0,2,3,1:T(8,128)(2,1)}, u32[]{:S(2)}, u32[]{:S(2)}) collective-permute-start(bf16[32,4,18,1]{0,2,3,1:T(8,128)(2,1)S(1)} %copy.531), channel_id=1, source_target_pairs={{1,0},{2,1},{3,2},{4,3},{5,4},{6,5},{7,6},{9,8},{10,9},{11,10},{12... | collective-permute-start | bytes 13832 | tf_op jit(solution)/shard_map/ppermute | solution.py:30
  348.0 5.1 collective-permute-start.16
  366.1 31.5 %copy-start.22 = (f32[4,8,32,128]{3,2,1,0:T(8,128)S(1)}, f32[4,8,32,128]{3,2,1,0:T(8,128)}, u32[]{:S(2)}) copy-start(f32[4,8,32,128]{3,2,1,0:T(8,128)} %copy-done.21) | copy-start | bytes 1572868
  397.3 13.6 %copy-start.28 = (bf16[3,32,4096]{2,1,0:T(8,128)(2,1)S(1)}, bf16[3,32,4096]{2,1,0:T(8,128)(2,1)}, u32[]{:S(2)}) copy-start(bf16[3,32,4096]{2,1,0:T(8,128)(2,1)} %dot_general.378) | copy-start | bytes 2359300
  397.5 14.0 %copy-start.29 = (bf16[3,32,4096]{2,1,0:T(8,128)(2,1)S(1)}, bf16[3,32,4096]{2,1,0:T(8,128)(2,1)}, u32[]{:S(2)}) copy-start(bf16[3,32,4096]{2,1,0:T(8,128)(2,1)} %dot_general.380) | copy-start | bytes 2359300
  398.3 13.9 %copy-start.30 = (bf16[3,32,4096]{2,1,0:T(8,128)(2,1)S(1)}, bf16[3,32,4096]{2,1,0:T(8,128)(2,1)}, u32[]{:S(2)}) copy-start(bf16[3,32,4096]{2,1,0:T(8,128)(2,1)} %dot_general.382) | copy-start | bytes 2359300
  398.3 19.1 %collective-permute-start.18 = (bf16[32,1,16,128]{3,0,2,1:T(8,128)(2,1)S(1)}, bf16[32,1,16,128]{3,0,2,1:T(8,128)(2,1)S(1)}, u32[]{:S(2)}, u32[]{:S(2)}) collective-permute-start(bf16[32,1,16,128]{3,0,2,1:T(8,128)(2,1)S(1)} %get-tuple-element.264), channel_id=1, source_target_pairs={{0,32},{32,64},{64,96},{1,33},{33,65},{65,97},{2,34},{34,66},{66,9... | collective-permute-start | bytes 393224 | tf_op jit(solution)/shard_map/ppermute | solution.py:27
  408.7 4.1 copy-start.32
  408.7 8.7 %collective-permute-start.19 = (bf16[32,1,16,128]{3,0,2,1:T(8,128)(2,1)S(1)}, bf16[32,1,16,128]{3,0,2,1:T(8,128)(2,1)S(1)}, u32[]{:S(2)}, u32[]{:S(2)}) collective-permute-start(bf16[32,1,16,128]{3,0,2,1:T(8,128)(2,1)S(1)} %get-tuple-element.265), channel_id=1, source_target_pairs={{32,0},{64,32},{96,64},{33,1},{65,33},{97,65},{34,2},{66,34},{98,6... | collective-permute-start | bytes 393224 | tf_op jit(solution)/shard_map/ppermute | solution.py:30
  417.4 5.5 collective-permute-start.20
  421.1 4.7 collective-permute-start.21
  427.4 6.8 %collective-permute-start.23 = (bf16[32,4,18,1]{0,2,3,1:T(8,128)(2,1)S(1)}, bf16[32,4,18,1]{0,2,3,1:T(8,128)(2,1)S(1)}, u32[]{:S(2)}, u32[]{:S(2)}) collective-permute-start(bf16[32,4,18,1]{0,2,3,1:T(8,128)(2,1)S(1)} %copy.546), channel_id=1, source_target_pairs={{1,0},{2,1},{3,2},{4,3},{5,4},{6,5},{7,6},{9,8},{10,9},{11,10},{12... | collective-permute-start | bytes 13832 | tf_op jit(solution)/shard_map/ppermute | solution.py:30
  428.7 4.9 collective-permute-start.22
  (114 other events, 149.4 us)
Sparse Core Ops, SparseCore 0:
  417.5 145.4 all-reduce.22
where the time goes:
time: 580 us; the launch traced here: 574 us
  waiting for transfers between devices  142 us (24%)
  local copies, waits for them, and re-layouts  139 us (24%)
  blocking collectives  119 us (21%)
  starting transfers between devices  80.6 us (14%)
  other arithmetic  40.1 us (7%)
  matrix products  36.2 us (6%)
  between operations  17.5 us (3%)
    psum x20, blocking collectives, by_axis(): return functools.reduce(lax.psum, axes, value)  119 us
    psum x1, waiting for transfers between devices, body(): grad_w_first = lax.psum(local_first, GX_GY_GZ)  118 us
    ppermute x12, starting transfers between devices, extended(): lax.ppermute(lax.slice_in_dim(block, block.shape[dim] - width, None, axis...  62 us
    dot_general x18, local copies, waits for them, and re-layouts, kernel_grad(): lax.dot_general(flat, stacked, (((1,), (1,)), ((), ())), preferred_elemen...  25.1 us
    dot_general x54, matrix products, convolve(): total = total + jnp.dot(matrix, stacked, preferred_element_type=jnp.float32)  24.7 us
    unnamed x315, local copies, waits for them, and re-layouts  23.5 us
    concatenate x4, local copies, waits for them, and re-layouts, extended(): block = jnp.concatenate([low, block, high], axis=dim)  22.8 us
    concatenate x12, other arithmetic, extended(): block = jnp.concatenate([low, block, high], axis=dim)  21.5 us
  transfers between devices with their start and end apart: 25, of which 12 were waited for; matrix products, arithmetic and copies ran while one was open for 12% of the time, Pallas kernels for 0%

commit v1 on v0

v1 whole, which is shorter than its diff:
```python
import functools
import math

import jax
import jax.numpy as jnp
from jax import lax
from jax.experimental import pallas as pl
from jax.experimental.pallas import tpu as pltpu
from jax.sharding import PartitionSpec as P

F32 = jnp.float32
BF16 = jnp.bfloat16
EPSILON = 1e-05
C = 32
LANES = 128
SPAN_X, SPAN_Y = 2, 16
PAD_X, PAD_Y = SPAN_X + 2, SPAN_Y + 2
TAPS = 3 * C
DEPTH = PAD_X * 3 * TAPS
FLAT = 9 * TAPS
GROUP = 4
AXES = ("gx", "gy", "gz")
MESH = pl.DeviceIdType.MESH


def sigmoid(value):
    return 0.5 + 0.5 * jnp.tanh(0.5 * value)


class Halo:
    def __init__(self, rows, near, far_y, turn, far_x, edge, send, recv, place, volumes):
        self.rows, self.near, self.far_y, self.turn, self.far_x = rows, near, far_y, turn, far_x
        self.edge, self.send, self.recv, self.place, self.volumes = edge, send, recv, place, volumes
        self.count = 0
        self.sent = []

    def has(self, axis, step):
        me, size = self.place[axis]
        return me > 0 if step < 0 else me < size - 1

    def push(self, source, target, axis, step):
        me, size = self.place[axis]
        index = self.count
        self.count += 1
        copy = pltpu.make_async_remote_copy(
            src_ref=source,
            dst_ref=target,
            send_sem=self.send.at[index],
            recv_sem=self.recv.at[index],
            device_id={axis: lax.rem(me + step + size, size)},
            device_id_type=MESH,
        )

        @pl.when(self.has(axis, step))
        def _():
            copy.start()

        self.sent.append((copy, self.has(axis, step)))
        return copy, self.has(axis, -step)

    def faces_x(self, volume):
        rows = self.rows
        inner = pl.ds(1, SPAN_Y)
        down = self.push(
            rows.at[volume, 1, inner], rows.at[volume, PAD_X - 1, inner], "gx", -1
        )
        up = self.push(rows.at[volume, SPAN_X, inner], rows.at[volume, 0, inner], "gx", 1)
        return [down, up]

    def faces_y(self):
        rows, inner, every = self.rows, pl.ds(1, SPAN_X), pl.ds(0, self.volumes)
        down = self.push(
            rows.at[every, inner, 1], rows.at[every, inner, PAD_Y - 1], "gy", -1
        )
        up = self.push(rows.at[every, inner, SPAN_Y], rows.at[every, inner, 0], "gy", 1)
        return [down, up]

    def columns_z(self):
        down = self.push(self.edge.at[0], self.near.at[1], "gz", -1)
        up = self.push(self.edge.at[1], self.near.at[0], "gz", 1)
        return [down, up]

    def columns_y(self):
        down = self.push(self.near, self.far_y.at[1], "gy", -1)
        up = self.push(self.near, self.far_y.at[0], "gy", 1)
        return [down, up]

    def columns_x(self, lane):
        inside = lax.rem(lane, 32)
        for side in range(2):
            for volume in range(self.volumes):
                own = self.near[side, volume].astype(F32)
                low = pltpu.roll(self.far_y[0, side, volume].astype(F32), LANES - 16, 1)
                high = pltpu.roll(self.far_y[1, side, volume].astype(F32), 16, 1)
                own = jnp.where(inside == 0, low, jnp.where(inside == PAD_Y - 1, high, own))
                self.turn[side, volume] = own.astype(BF16)
        down = self.push(self.turn, self.far_x.at[1], "gx", -1)
        up = self.push(self.turn, self.far_x.at[0], "gx", 1)
        return [down, up]

    def corners_x(self):
        rows, every = self.rows, pl.ds(0, self.volumes)
        result = []
        for at in (0, PAD_Y - 1):
            result.append(
                self.push(rows.at[every, 1, at], rows.at[every, PAD_X - 1, at], "gx", -1)
            )
            result.append(
                self.push(rows.at[every, SPAN_X, at], rows.at[every, 0, at], "gx", 1)
            )
        return result

    def merged(self, side, volume, lane):
        own = self.turn[side, volume].astype(F32)
        low = pltpu.roll(self.far_x[0, side, volume].astype(F32), LANES - 64, 1)
        high = pltpu.roll(self.far_x[1, side, volume].astype(F32), 64, 1)
        return jnp.where(lane < 32, low, jnp.where(lane >= 96, high, own))

    @staticmethod
    def arrive(pushes):
        for copy, present in pushes:

            @pl.when(present)
            def _(copy=copy):
                copy.wait_recv()

    def drain(self):
        for copy, present in self.sent:

            @pl.when(present)
            def _(copy=copy):
                copy.wait_send()


class Fan:
    def __init__(self, place, axis, send, recv, first):
        self.me, self.size = place[axis]
        self.axis, self.send, self.recv, self.first = axis, send, recv, first
        self.copies = []

    def start(self, source_of, target):
        for step in range(1, self.size):
            to = lax.rem(self.me + step, self.size)
            copy = pltpu.make_async_remote_copy(
                src_ref=source_of(to),
                dst_ref=target,
                send_sem=self.send.at[self.first + step - 1],
                recv_sem=self.recv.at[self.first + step - 1],
                device_id={self.axis: to},
                device_id_type=MESH,
            )
            copy.start()
            self.copies.append(copy)

    def arrive(self):
        for copy in self.copies:
            copy.wait_recv()

    def drain(self):
        for copy in self.copies:
            copy.wait_send()


def kernel(
    voxels,
    x_a, x_b, grad, weights, params,
    y_out, dx_out, gw_out, norm_out,
    taps_x, taps_h, taps_d2, taps_d1,
    rows_x, rows_1, rows_2, rows_e,
    near_x, near_1, near_2, near_e,
    fary_x, fary_1, fary_2, fary_e,
    turn_x, turn_1, turn_2, turn_e,
    farx_x, farx_1, farx_2, farx_e,
    edge_x, edge_1, edge_2, edge_e,
    side_x, side_1, side_2, side_e,
    conv_1, conv_2, back_1,
    sums_x, sums_z, sums_y,
    gw_local, gw_a, gw_sa, gw_b, gw_sb, gw_c, gw_sc, gw_d, gw_e,
    halo_send, halo_recv, sums_send, sums_recv, gw_send, gw_recv,
):
    place = {axis: (lax.axis_index(axis), lax.axis_size(axis)) for axis in AXES}
    for near in (near_x, near_1, near_2, near_e):
        near[...] = jnp.zeros_like(near)
    barrier = pltpu.get_barrier_semaphore()
    partners = 0
    for axis in AXES:
        me, size = place[axis]
        for step in range(1, size):
            pl.semaphore_signal(
                barrier, inc=1, device_id={axis: lax.rem(me + step, size)}, device_id_type=MESH
            )
            partners += 1

    lane = lax.broadcasted_iota(jnp.int32, (C, LANES), 1)
    halos = []
    for index, (rows, near, fary, turn, farx, edge, volumes) in enumerate((
        (rows_x, near_x, fary_x, turn_x, farx_x, edge_x, 3),
        (rows_1, near_1, fary_1, turn_1, farx_1, edge_1, 2),
        (rows_2, near_2, fary_2, turn_2, farx_2, edge_2, 1),
        (rows_e, near_e, fary_e, turn_e, farx_e, edge_e, 1),
    )):
        halos.append(
            Halo(rows, near, fary, turn, farx, edge, halo_send.at[index], halo_recv.at[index],
                 place, volumes)
        )
    halo_x, halo_1, halo_2, halo_e = halos

    low_x, high_x = place["gx"][0] > 0, place["gx"][0] < place["gx"][1] - 1
    low_y, high_y = place["gy"][0] > 0, place["gy"][0] < place["gy"][1] - 1
    low_z, high_z = place["gz"][0] > 0, place["gz"][0] < place["gz"][1] - 1

    def keep(at_x, at_y):
        held_x = low_x if at_x == 0 else high_x if at_x == PAD_X - 1 else None
        if isinstance(at_y, int):
            held_y = low_y if at_y == 0 else high_y if at_y == PAD_Y - 1 else None
        else:
            held_y = jnp.logical_and(
                jnp.logical_or(at_y > 0, low_y), jnp.logical_or(at_y < PAD_Y - 1, high_y)
            )
        if held_x is None:
            return held_y
        return held_x if held_y is None else jnp.logical_and(held_x, held_y)

    def lane_keep(side):
        spot_x, spot_y = lane // 32, lax.rem(lane, 32)
        bad = jnp.zeros((C, LANES), jnp.int32)
        for hit, present in (
            (spot_x == 0, low_x), (spot_x == PAD_X - 1, high_x),
            (spot_y == 0, low_y), (spot_y == PAD_Y - 1, high_y),
        ):
            missing = jnp.where(present, 0, 1)
            bad = bad + jnp.where(hit, missing, 0)
        bad = bad + jnp.where(low_z if side == 0 else high_z, 0, 1)
        return bad == 0

    def extract(tile, spot, carry):
        first, last = carry
        first = jnp.where(lane == spot, pltpu.roll(tile, spot, 1), first)
        last = jnp.where(lane == spot, pltpu.roll(tile, lax.rem(spot + 1, LANES), 1), last)
        return first, last

    def put_taps(taps, volume, at_x, at_y, tile, side_lo, side_hi):
        spot = at_x * 32 + at_y
        left = jnp.where(
            lane == 0,
            pltpu.roll(side_lo, lax.rem(LANES - spot, LANES), 1),
            pltpu.roll(tile, 1, 1),
        )
        right = jnp.where(
            lane == LANES - 1,
            pltpu.roll(side_hi, LANES - 1 - spot, 1),
            pltpu.roll(tile, LANES - 1, 1),
        )
        taps[volume, at_x, at_y, 0:C] = left.astype(BF16)
        taps[volume, at_x, at_y, C : 2 * C] = tile.astype(BF16)
        taps[volume, at_x, at_y, 2 * C : 3 * C] = right.astype(BF16)

    def build(taps, volume, outer, inner, sides):
        low, high = sides
        zero = jnp.zeros((C, LANES), F32)

        def held(at_x, at_y):
            tile = outer(at_x, at_y)
            return jnp.where(keep(at_x, at_y), tile, zero)

        for at_x in (1, 2):

            def step(block, carry, at_x=at_x):
                for k in range(8):
                    at_y = block * 8 + k
                    put_taps(
                        taps, volume, at_x, at_y + 1, inner(at_x - 1, at_y), low[...], high[...]
                    )
                return carry

            lax.fori_loop(0, 2, step, 0)
            for at_y in (0, PAD_Y - 1):
                put_taps(taps, volume, at_x, at_y, held(at_x, at_y), low[...], high[...])
        for at_x in (0, PAD_X - 1):

            def step(block, carry, at_x=at_x):
                for k in range(6):
                    at_y = block * 6 + k
                    put_taps(taps, volume, at_x, at_y, held(at_x, at_y), low[...], high[...])
                return carry

            lax.fori_loop(0, 3, step, 0)

    def convolve(taps, volume, weight, emit, carry):
        def step(block, carry):
            first = block * GROUP
            columns = [
                taps[volume, :, pl.ds(first + k, 3)].reshape(DEPTH, LANES) for k in range(GROUP)
            ]
            total = jnp.dot(
                weights[weight],
                jnp.concatenate(columns, axis=1),
                preferred_element_type=F32,
            )
            for k in range(GROUP):
                for at_x in range(SPAN_X):
                    tile = total[at_x * C : (at_x + 1) * C, k * LANES : (k + 1) * LANES]
                    carry = emit(at_x, first + k, tile, carry)
            return carry

        return lax.fori_loop(0, SPAN_Y // GROUP, step, carry)

    def kernel_grad(taps, volume, upstream, index):
        def step(block, total):
            first = block * GROUP
            left, right = [], []
            for k in range(GROUP):
                left.append(
                    upstream[0, pl.ds(1, SPAN_X), first + k + 1, C : 2 * C].reshape(
                        SPAN_X * C, LANES
                    )
                )
                right.append(taps[volume, :, pl.ds(first + k, 3)].reshape(DEPTH, LANES))
            return total + lax.dot_general(
                jnp.concatenate(left, axis=1),
                jnp.concatenate(right, axis=1),
                (((1,), (1,)), ((), ())),
                preferred_element_type=F32,
            )

        total = lax.fori_loop(
            0, SPAN_Y // GROUP, step, jnp.zeros((SPAN_X * C, DEPTH), F32)
        )
        both = total[0:C, 0:FLAT] + total[C : 2 * C, 3 * TAPS : 3 * TAPS + FLAT]
        both = jnp.concatenate([both, jnp.zeros((C, 1024 - FLAT), F32)], axis=1)
        for j in range(4):
            for k in range(8):
                gw_local[j, index, k] = both[8 * j : 8 * j + 8, LANES * k : LANES * (k + 1)]

    def pack(columns):
        whole = jnp.zeros((C, LANES), F32)
        for k, column in enumerate(columns):
            whole = whole + jnp.where(lane == k, column, 0.0)
        tile = whole[0:8]
        for j in range(1, 4):
            tile = tile + pltpu.roll(whole[8 * j : 8 * j + 8], 4 * j, 1)
        return tile

    def unpack(tile, count):
        parts = [tile] + [pltpu.roll(tile, LANES - 4 * j, 1) for j in range(1, 4)]
        whole = jnp.concatenate(parts, axis=0)
        return [whole[:, k : k + 1] for k in range(count)]

    class Total:
        def __init__(self, index):
            self.fans = {}
            first = 0
            for axis, slots in (("gx", sums_x), ("gz", sums_z), ("gy", sums_y)):
                fan = Fan(place, axis, sums_send.at[index], sums_recv.at[index], first)
                first += fan.size - 1
                self.fans[axis] = (fan, slots.at[index])

        def start(self, axis, tile):
            fan, slots = self.fans[axis]
            slots[fan.me] = tile
            mine = slots.at[fan.me]
            fan.start(lambda to: mine, mine)

        def finish(self, axis):
            fan, slots = self.fans[axis]
            fan.arrive()
            tile = slots[0]
            for k in range(1, fan.size):
                tile = tile + slots[k]
            return tile

        def drain(self):
            for fan, slots in self.fans.values():
                fan.drain()

    totals = [Total(index) for index in range(4)]

    def reduce_with(total, tile, halo, waits):
        total.start("gx", tile)
        phase_1 = waits + halo.faces_y() + halo.columns_z()
        tile = total.finish("gx")
        total.start("gz", tile)
        halo.arrive(phase_1[-4:])
        phase_2 = halo.columns_y()
        corners = halo.corners_x()
        tile = total.finish("gz")
        total.start("gy", tile)
        halo.arrive(phase_2)
        last = halo.columns_x(lane)
        tile = total.finish("gy")
        return tile, waits + corners + last

    gain_1, bias_1, gain_2, bias_2 = (params[:, k : k + 1] for k in range(4))

    zero = jnp.zeros((C, LANES), F32)
    for volume, source in enumerate((x_a, x_b, grad)):
        for at_x in range(SPAN_X):

            def step(block, carry, source=source, at_x=at_x, volume=volume):
                for k in range(8):
                    at_y = block * 8 + k
                    row = source[at_x, at_y]
                    rows_x[volume, at_x + 1, at_y + 1] = row
                    carry = extract(
                        row.astype(F32), (at_x + 1) * 32 + at_y + 1, carry
                    )
                return carry

            carry = lax.fori_loop(0, 2, step, (zero, zero) if at_x == 0 else carry)
        edge_x[0, volume] = carry[0].astype(BF16)
        edge_x[1, volume] = carry[1].astype(BF16)

    pl.semaphore_wait(barrier, partners)

    waits_x = [halo_x.faces_x(0), halo_x.faces_x(1)]
    phase_1 = halo_x.faces_y() + halo_x.columns_z()
    waits_g = halo_x.faces_x(2)
    halo_x.arrive(phase_1)
    phase_2 = halo_x.columns_y()
    corners = halo_x.corners_x()
    halo_x.arrive(phase_2)
    halo_x.arrive(halo_x.columns_x(lane))
    halo_x.arrive(corners)
    ok = [lane_keep(side) for side in range(2)]
    for side in range(2):
        for volume in range(3):
            tile = halo_x.merged(side, volume, lane)
            side_x[volume, side] = jnp.where(ok[side], tile, 0.0)

    def stats_emit(keep_f32, halo, volume):
        def emit(at_x, at_y, tile, carry):
            total, squares, first, last = carry
            keep_f32[volume, at_x, at_y] = tile
            halo.rows[halo_of[volume], at_x + 1, at_y + 1] = tile.astype(BF16)
            first, last = extract(tile, (at_x + 1) * 32 + at_y + 1, (first, last))
            return total + tile, squares + tile * tile, first, last

        halo_of = {0: 0, 1: 1}
        return emit

    columns = []
    waits = []
    for volume in range(2):
        halo_x.arrive(waits_x[volume])
        build(
            taps_x, volume,
            lambda at_x, at_y, volume=volume: rows_x[volume, at_x, at_y].astype(F32),
            lambda at_x, at_y, volume=volume: rows_x[volume, at_x + 1, at_y + 1].astype(F32),
            (side_x.at[volume, 0], side_x.at[volume, 1]),
        )
        total, squares, first, last = convolve(
            taps_x, volume, 0, stats_emit(conv_1, halo_1, volume), (zero,) * 4
        )
        edge_1[0, volume] = first.astype(BF16)
        edge_1[1, volume] = last.astype(BF16)
        waits += halo_1.faces_x(volume)
        columns += [
            jnp.sum(total, axis=1, keepdims=True), jnp.sum(squares, axis=1, keepdims=True)
        ]
    tile, arrivals = reduce_with(totals[0], pack(columns), halo_1, waits)
    sums = unpack(tile, 4)
    halo_1.arrive(arrivals)

    def moments(total, squares):
        mean = total / voxels
        scale = lax.rsqrt(squares / voxels - mean * mean + EPSILON)
        return mean, scale

    columns = []
    affine_1 = None
    for volume in range(2):
        mean, scale = moments(sums[2 * volume], sums[2 * volume + 1])
        slope = jnp.broadcast_to(gain_1 * scale, (C, LANES))
        shift = jnp.broadcast_to(bias_1 - mean * gain_1 * scale, (C, LANES))

        def active(value, slope=slope, shift=shift):
            pre = value * slope + shift
            return pre * sigmoid(pre)

        for side in range(2):
            tile = active(halo_1.merged(side, volume, lane))
            side_1[volume, side] = jnp.where(ok[side], tile, 0.0)
        build(
            taps_h, volume,
            lambda at_x, at_y, volume=volume: active(rows_1[volume, at_x, at_y].astype(F32)),
            lambda at_x, at_y, volume=volume: active(conv_1[volume, at_x, at_y]),
            (side_1.at[volume, 0], side_1.at[volume, 1]),
        )
        if volume == 0:

            def emit(at_x, at_y, tile, carry):
                total, squares = carry
                conv_2[0, at_x, at_y] = tile
                return total + tile, squares + tile * tile

            total, squares = convolve(taps_h, 0, 1, emit, (zero,) * 2)
        else:

            def emit(at_x, at_y, tile, carry):
                total, squares, first, last = carry
                conv_2[1, at_x, at_y] = tile
                rows_2[0, at_x + 1, at_y + 1] = tile.astype(BF16)
                first, last = extract(tile, (at_x + 1) * 32 + at_y + 1, (first, last))
                return total + tile, squares + tile * tile, first, last

            total, squares, first, last = convolve(taps_h, 1, 1, emit, (zero,) * 4)
            edge_2[0, 0] = first.astype(BF16)
            edge_2[1, 0] = last.astype(BF16)
            waits = halo_2.faces_x(0)
        columns += [
            jnp.sum(total, axis=1, keepdims=True), jnp.sum(squares, axis=1, keepdims=True)
        ]
    mean_1, scale_1 = mean, scale
    tile, arrivals = reduce_with(totals[1], pack(columns), halo_2, waits)
    sums = unpack(tile, 4)

    mean_2, scale_2 = moments(sums[2], sums[3])

    def layer_of(mean, scale, gain, bias):
        norm_slope = jnp.broadcast_to(scale, (C, LANES))
        norm_shift = jnp.broadcast_to(-mean * scale, (C, LANES))
        wide_gain = jnp.broadcast_to(gain, (C, LANES))
        wide_bias = jnp.broadcast_to(bias, (C, LANES))

        def slope_of(value, upstream):
            normed = value * norm_slope + norm_shift
            pre = wide_gain * normed + wide_bias
            sigma = sigmoid(pre)
            return upstream * (sigma * (1.0 + pre * (1.0 - sigma))), normed

        return slope_of

    def delta_of(slope_of, sum_d, sum_x, gain, scale):
        wide_d = jnp.broadcast_to(sum_d / voxels, (C, LANES))
        wide_x = jnp.broadcast_to(sum_x / voxels, (C, LANES))
        factor = jnp.broadcast_to(gain * scale, (C, LANES))

        def delta(value, upstream):
            slope, normed = slope_of(value, upstream)
            return factor * (slope - wide_d - normed * wide_x)

        return delta

    slope_2 = layer_of(mean_2, scale_2, gain_2, bias_2)

    def sum_rows(slope_of, value_of, upstream_of):
        carry = (zero, zero)
        for at_x in range(SPAN_X):

            def step(block, carry, at_x=at_x):
                total, weighted = carry
                for k in range(8):
                    at_y = block * 8 + k
                    slope, normed = slope_of(value_of(at_x, at_y), upstream_of(at_x, at_y))
                    total, weighted = total + slope, weighted + slope * normed
                return total, weighted

            carry = lax.fori_loop(0, 2, step, carry)
        return [jnp.sum(part, axis=1, keepdims=True) for part in carry]

    columns = sum_rows(
        slope_2,
        lambda at_x, at_y: conv_2[1, at_x, at_y],
        lambda at_x, at_y: rows_x[2, at_x + 1, at_y + 1].astype(F32),
    )
    totals[2].start("gx", pack(columns))

    mean_a, scale_a = moments(sums[0], sums[1])
    slope_a = jnp.broadcast_to(gain_2 * scale_a, (C, LANES))
    shift_a = jnp.broadcast_to(bias_2 - mean_a * gain_2 * scale_a, (C, LANES))
    for at_x in range(SPAN_X):

        def step(block, carry, at_x=at_x):
            for k in range(8):
                at_y = block * 8 + k
                pre = conv_2[0, at_x, at_y] * slope_a + shift_a
                y_out[at_x, at_y] = (pre * sigmoid(pre)).astype(BF16)
            return carry

        lax.fori_loop(0, 2, step, 0)

    totals[2].start("gz", totals[2].finish("gx"))
    totals[2].start("gy", totals[2].finish("gz"))
    halo_2.arrive(arrivals)
    halo_x.arrive(waits_g)
    sum_d2, sum_x2 = unpack(totals[2].finish("gy"), 2)

    delta_2 = delta_of(slope_2, sum_d2, sum_x2, gain_2, scale_2)
    for side in range(2):
        tile = delta_2(halo_2.merged(side, 0, lane), side_x[2, side])
        side_2[0, side] = jnp.where(ok[side], tile, 0.0)
    build(
        taps_d2, 0,
        lambda at_x, at_y: delta_2(
            rows_2[0, at_x, at_y].astype(F32), rows_x[2, at_x, at_y].astype(F32)
        ),
        lambda at_x, at_y: delta_2(
            conv_2[1, at_x, at_y], rows_x[2, at_x + 1, at_y + 1].astype(F32)
        ),
        (side_2.at[0, 0], side_2.at[0, 1]),
    )
    slope_1 = layer_of(mean_1, scale_1, gain_1, bias_1)

    def emit(at_x, at_y, tile, carry):
        total, weighted, first, last = carry
        back_1[at_x, at_y] = tile
        rows_e[0, at_x + 1, at_y + 1] = tile.astype(BF16)
        first, last = extract(tile, (at_x + 1) * 32 + at_y + 1, (first, last))
        slope, normed = slope_1(conv_1[1, at_x, at_y], tile)
        return total + slope, weighted + slope * normed, first, last

    total, weighted, first, last = convolve(taps_d2, 0, 2, emit, (zero,) * 4)
    edge_e[0, 0] = first.astype(BF16)
    edge_e[1, 0] = last.astype(BF16)
    waits = halo_e.faces_x(0)
    columns = [
        jnp.sum(total, axis=1, keepdims=True), jnp.sum(weighted, axis=1, keepdims=True)
    ]
    tile, arrivals = reduce_with(totals[3], pack(columns), halo_e, waits)
    kernel_grad(taps_h, 1, taps_d2, 1)
    sum_d1, sum_x1 = unpack(tile, 2)
    halo_e.arrive(arrivals)

    delta_1 = delta_of(slope_1, sum_d1, sum_x1, gain_1, scale_1)
    for side in range(2):
        tile = delta_1(halo_1.merged(side, 1, lane), halo_e.merged(side, 0, lane))
        side_e[0, side] = jnp.where(ok[side], tile, 0.0)
    build(
        taps_d1, 0,
        lambda at_x, at_y: delta_1(
            rows_1[1, at_x, at_y].astype(F32), rows_e[0, at_x, at_y].astype(F32)
        ),
        lambda at_x, at_y: delta_1(conv_1[1, at_x, at_y], back_1[at_x, at_y]),
        (side_e.at[0, 0], side_e.at[0, 1]),
    )
    kernel_grad(taps_x, 1, taps_d1, 0)

    fan_a = Fan(place, "gx", gw_send, gw_recv, 0)
    fan_b = Fan(place, "gz", gw_send, gw_recv, 3)
    fan_c = Fan(place, "gy", gw_send, gw_recv, 10)
    fan_d = Fan(place, "gz", gw_send, gw_recv, 13)
    fan_e = Fan(place, "gx", gw_send, gw_recv, 20)
    fan_a.start(lambda to: gw_local.at[to], gw_a.at[fan_a.me])

    def emit(at_x, at_y, tile, carry):
        dx_out[at_x, at_y] = tile.astype(BF16)
        return carry

    convolve(taps_d1, 0, 3, emit, 0)

    fan_a.arrive()
    gw_a[fan_a.me] = gw_local[fan_a.me]
    for index in range(2):
        for k in range(8):
            tile = gw_a[0, index, k]
            for j in range(1, 4):
                tile = tile + gw_a[j, index, k]
            gw_sa[k, index] = tile
    fan_b.start(lambda to: gw_sa.at[to], gw_b.at[fan_b.me])
    fan_b.arrive()
    gw_b[fan_b.me] = gw_sa[fan_b.me]
    for index in range(2):
        tile = gw_b[0, index]
        for j in range(1, 8):
            tile = tile + gw_b[j, index]
        gw_c[fan_c.me, index] = tile
    fan_c.start(lambda to: gw_c.at[fan_c.me], gw_c.at[fan_c.me])
    fan_c.arrive()
    for index in range(2):
        tile = gw_c[0, index]
        for j in range(1, 4):
            tile = tile + gw_c[j, index]
        gw_d[fan_d.me, index] = tile * (1.0 / math.sqrt(voxels))
    fan_d.start(lambda to: gw_d.at[fan_d.me], gw_d.at[fan_d.me])
    fan_d.arrive()
    fan_e.start(lambda to: gw_d, gw_e.at[fan_e.me])
    gw_e[fan_e.me] = gw_d[...]
    norms = [sum_x1, sum_d1, sum_x2, sum_d2]
    whole = jnp.zeros((C, LANES), F32)
    for k, column in enumerate(norms):
        whole = whole + jnp.where(lane == k, column, 0.0)
    norm_out[...] = whole * (1.0 / math.sqrt(voxels))
    fan_e.arrive()
    for j in range(4):
        for index in range(2):
            for k in range(8):
                gw_out[index, 8 * j : 8 * j + 8, LANES * k : LANES * (k + 1)] = gw_e[j, k, index]

    for halo in halos:
        halo.drain()
    for total in totals:
        total.drain()
    for fan in (fan_a, fan_b, fan_c, fan_d, fan_e):
        fan.drain()


def stacked(weight):
    flat = weight.transpose(3, 0, 1, 2, 4).reshape(C, FLAT)
    slab = 3 * TAPS
    return jnp.concatenate(
        [jnp.pad(flat, ((0, 0), (0, slab))), jnp.pad(flat, ((0, 0), (slab, 0)))], axis=0
    )


def flipped(weight):
    return jnp.flip(weight, (0, 1, 2)).transpose(0, 1, 2, 4, 3)


def body(voxels, x_a, x_b, w_first, w_second, gain_first, bias_first, gain_second, bias_second,
         grad_out):
    weights = jnp.stack(
        [stacked(w_first), stacked(w_second), stacked(flipped(w_second)), stacked(flipped(w_first))]
    )
    params = jnp.stack([gain_first, bias_first, gain_second, bias_second], axis=1)

    def by_rows(block):
        return block.transpose(1, 2, 0, 3)

    def sized(*shape, kind=BF16):
        return pltpu.VMEM(shape, kind)

    volumes = (3, 2, 1, 1)
    scratch = [sized(count, PAD_X, PAD_Y, TAPS, LANES) for count in (2, 2, 1, 1)]
    scratch += [sized(count, PAD_X, PAD_Y, C, LANES) for count in volumes]
    scratch += [sized(2, count, C, LANES) for count in volumes]
    scratch += [sized(2, 2, count, C, LANES) for count in volumes]
    scratch += [sized(2, count, C, LANES) for count in volumes]
    scratch += [sized(2, 2, count, C, LANES) for count in volumes]
    scratch += [sized(2, count, C, LANES) for count in volumes]
    scratch += [sized(count, 2, C, LANES, kind=F32) for count in volumes]
    scratch += [
        sized(2, SPAN_X, SPAN_Y, C, LANES, kind=F32),
        sized(2, SPAN_X, SPAN_Y, C, LANES, kind=F32),
        sized(SPAN_X, SPAN_Y, C, LANES, kind=F32),
        sized(4, 4, 8, LANES, kind=F32),
        sized(4, 8, 8, LANES, kind=F32),
        sized(4, 4, 8, LANES, kind=F32),
        sized(4, 2, 8, 8, LANES, kind=F32),
        sized(4, 2, 8, 8, LANES, kind=F32),
        sized(8, 2, 8, LANES, kind=F32),
        sized(8, 2, 8, LANES, kind=F32),
        sized(2, 8, LANES, kind=F32),
        sized(4, 2, 8, LANES, kind=F32),
        sized(2, 8, LANES, kind=F32),
        sized(8, 2, 8, LANES, kind=F32),
        sized(4, 8, 2, 8, LANES, kind=F32),
        pltpu.SemaphoreType.DMA((4, 24)),
        pltpu.SemaphoreType.DMA((4, 24)),
        pltpu.SemaphoreType.DMA((4, 16)),
        pltpu.SemaphoreType.DMA((4, 16)),
        pltpu.SemaphoreType.DMA((24,)),
        pltpu.SemaphoreType.DMA((24,)),
    ]
    in_vmem = pl.BlockSpec(memory_space=pltpu.VMEM)
    y_a, dx_b, kernels, norms = pl.pallas_call(
        functools.partial(kernel, voxels),
        out_shape=(
            jax.ShapeDtypeStruct((SPAN_X, SPAN_Y, C, LANES), BF16),
            jax.ShapeDtypeStruct((SPAN_X, SPAN_Y, C, LANES), BF16),
            jax.ShapeDtypeStruct((2, C, 1024), F32),
            jax.ShapeDtypeStruct((C, LANES), F32),
        ),
        in_specs=[in_vmem] * 5,
        out_specs=(in_vmem,) * 4,
        scratch_shapes=scratch,
        compiler_params=pltpu.CompilerParams(
            collective_id=0, has_side_effects=True, vmem_limit_bytes=60 * 1024 * 1024
        ),
    )(by_rows(x_a), by_rows(x_b), by_rows(grad_out), weights, params)

    def by_channels(block):
        return block.transpose(2, 0, 1, 3)

    grads = kernels[:, :, :FLAT].reshape(2, C, 3, 3, 3, C).transpose(0, 2, 3, 4, 1, 5)
    return (by_channels(y_a), by_channels(dx_b), grads[0], grads[1], norms[:, :4].T)


def solution(mesh):
    split = P(None, "gx", "gy", "gz")
    voxels = float(SPAN_X * SPAN_Y * LANES * mesh.size)
    return jax.shard_map(
        functools.partial(body, voxels),
        mesh=mesh,
        in_specs=(split, split, P(), P(), P(), P(), P(), P(), split),
        out_specs=(split, split, P(), P(), P()),
        check_vma=False,
    )
```

time: 580 us -> 135 us (0.23); the launches traced: 574 us -> 135 us
  waiting for transfers between devices: 142 us -> 0 us
  local copies, waits for them, and re-layouts: 139 us -> 12.8 us
  Pallas kernels: 0 us -> 119 us
  blocking collectives: 119 us -> 0 us
  starting transfers between devices: 80.6 us -> 0 us
  other arithmetic: 40.1 us -> 1.87 us
  matrix products: 36.2 us -> 0 us
  between operations: 17.5 us -> 0.76 us
    pallas_call x0 -> x1, Pallas kernels: none -> 119 us  [body(): pl.pallas_call(functools.partial(kernel, voxels), out_shape=(jax.ShapeDty...]
    psum x20 -> x0, blocking collectives: 119 us -> none  [by_axis(): return functools.reduce(lax.psum, axes, value)]
    psum x1 -> x0, waiting for transfers between devices: 118 us -> none  [body(): grad_w_first = lax.psum(local_first, GX_GY_GZ)]
    ppermute x24 -> x0, starting transfers between devices: 80.5 us -> none  [the longest x12 62 us: extended(): lax.ppermute(lax.slice_in_dim(block, block.shape[dim] - width, None, axis...]
    concatenate x58 -> x0, local copies, waits for them, and re-layouts: 42 us -> none  [the longest x4 22.8 us: extended(): block = jnp.concatenate([low, block, high], axis=dim)]
    dot_general x72 -> x0, matrix products: 36.2 us -> none  [the longest x54 24.7 us: convolve(): total = total + jnp.dot(matrix, stacked, preferred_element_type=jnp.float32)]
    concatenate x56 -> x0, other arithmetic: 30.2 us -> none  [the longest x12 21.5 us: extended(): block = jnp.concatenate([low, block, high], axis=dim)]
    slice x29 -> x1, local copies, waits for them, and re-layouts: 27.6 us -> 0.02 us  [body(): kernels[:, :, :FLAT].reshape(2, C, 3, 3, 3, C).transpose(0, 2, 3, 4, 1, 5)]
  transfers between devices with their start and end apart: 25 -> 0, of which waited for: 12 -> 0; matrix products, arithmetic and copies ran while one was open for 12% -> 0% of each run, Pallas kernels for 0% -> 0%
where the time goes in v1:
time: 135 us
  Pallas kernels  119 us (88%)
  local copies, waits for them, and re-layouts  12.8 us (9%)
  other arithmetic  1.87 us (1%)
    pallas_call x1, Pallas kernels, body(): pl.pallas_call(functools.partial(kernel, voxels), out_shape=(jax.ShapeDty...  119 us
    unnamed x18, local copies, waits for them, and re-layouts  6.68 us

profile of v1, /device:TPU:1, one launch (start us, length us, event | category | flops | bytes accessed | tf_op | source)
XLA Modules:
  0.0 134.9 jit_solution(2891319653294218628)
XLA Ops:
  0.6 0.0 copy-start.2
  0.6 0.8 pad_maximum_fusion.1
  1.4 0.7 copy.52.params
  2.1 0.0 copy-start
  2.1 1.0 rev.8
  3.1 0.1 copy.59
  3.2 0.0 copy-start.1
  3.2 1.0 rev.7
  4.2 0.1 copy.58
  4.4 0.1 fusion.13
  4.5 0.0 copy-done.2
  4.5 0.8 copy.63
  5.3 0.0 copy-done
  5.3 0.2 copy.49
  5.4 0.2 reshape.26
  5.6 0.0 copy-done.1
  5.7 0.0 copy-start.3
  5.7 0.0 copy-start.4
  5.7 0.2 copy.48
  5.8 0.2 reshape.25
  6.0 0.1 fusion.9
  6.1 0.9 pad_maximum_fusion.weights
  7.1 0.0 copy-done.3
  7.1 0.0 copy-done.4
  7.1 1.0 copy_bitcast_fusion
  8.1 119.5 %shard_map.128 = (bf16[2,16,32,128]{3,2,1,0:T(8,128)(2,1)}, bf16[2,16,32,128]{3,2,1,0:T(8,128)(2,1)}, f32[2,32,1024]{2,1,0:T(8,128)}, f32[32,128]{1,0:T(8,128)}) custom-call(bf16[2,16,32,128]{3,2,1,0:T(8,128)(2,1)} %bitcast.37, bf16[2,16,32,128]{3,2,1,0:T(8,128)(2,1)} %get-tuple-element.35.x_b, bf16[2,16,32,128]{3,2,1,0:T(8,128)(2,1)} %get-tuple-element.34.grad, ...), custom_call_target="tpu_custom_call" | custom-call | tf_op jit(solution)/shard_map/pallas_call | solution.py:755
  127.5 0.0 copy-start.5
  127.6 1.8 %copy.53 = bf16[32,2,16,128]{3,2,1,0:T(8,128)(2,1)} copy(bf16[32,2,16,128]{3,0,2,1:T(8,128)(2,1)} %bitcast.43) | data formatting | bytes 524288
  129.4 1.8 %copy.54 = bf16[32,2,16,128]{3,2,1,0:T(8,128)(2,1)} copy(bf16[32,2,16,128]{3,0,2,1:T(8,128)(2,1)} %bitcast.42) | data formatting | bytes 524288
  131.1 0.7 slice_bitcast_fusion.2
  131.8 0.7 copy.57
  132.5 0.0 copy-done.5
  132.5 0.6 reshape.29
  133.1 0.2 slice_bitcast_fusion
  133.3 0.8 copy.56
  134.1 0.8 copy.55
  (1 shorter events, 0.0 us)
Async XLA Ops:
  0.6 3.8 %copy-start.2 = (bf16[32,2,16,128]{3,2,1,0:T(8,128)(2,1)S(1)}, bf16[32,2,16,128]{3,2,1,0:T(8,128)(2,1)}, u32[]{:S(2)}) copy-start(bf16[32,2,16,128]{3,2,1,0:T(8,128)(2,1)} %param.9) | copy-start | bytes 786436
  2.1 3.2 %copy-start = (bf16[3,3,3,32,32]{4,3,2,1,0:T(8,128)(2,1)S(1)}, bf16[3,3,3,32,32]{4,3,2,1,0:T(8,128)(2,1)}, u32[]{:S(2)}) copy-start(bf16[3,3,3,32,32]{4,3,2,1,0:T(8,128)(2,1)} %param.12) | copy-start | bytes 165892
  3.2 2.4 %copy-start.1 = (bf16[3,3,3,32,32]{4,3,2,1,0:T(8,128)(2,1)S(1)}, bf16[3,3,3,32,32]{4,3,2,1,0:T(8,128)(2,1)}, u32[]{:S(2)}) copy-start(bf16[3,3,3,32,32]{4,3,2,1,0:T(8,128)(2,1)} %param.11) | copy-start | bytes 165892
  5.7 1.4 %copy-start.3 = (bf16[32,2,16,128]{3,2,1,0:T(8,128)(2,1)S(1)}, bf16[32,2,16,128]{3,2,1,0:T(8,128)(2,1)}, u32[]{:S(2)}) copy-start(bf16[32,2,16,128]{3,2,1,0:T(8,128)(2,1)} %param.17) | copy-start | bytes 786436
  5.7 1.4 %copy-start.4 = (bf16[32,2,16,128]{3,2,1,0:T(8,128)(2,1)S(1)}, bf16[32,2,16,128]{3,2,1,0:T(8,128)(2,1)}, u32[]{:S(2)}) copy-start(bf16[32,2,16,128]{3,2,1,0:T(8,128)(2,1)} %param.10) | copy-start | bytes 786436
  127.5 4.9 %copy-start.5 = (f32[2,32,1024]{2,1,0:T(8,128)S(1)}, f32[2,32,1024]{2,1,0:T(8,128)}, u32[]{:S(2)}) copy-start(f32[2,32,1024]{2,1,0:T(8,128)} %get-tuple-element.11) | copy-start | bytes 786436

commit v2 on v1

--- a/solution.py
+++ b/solution.py
@@ -27,9 +27,17 @@
     return 0.5 + 0.5 * jnp.tanh(0.5 * value)
 
 
+def rolled(tile, shift):
+    shift = shift % LANES
+    return pltpu.roll(tile, shift, 1) if shift else tile
+
+
 class Halo:
-    def __init__(self, rows, near, far_y, turn, far_x, edge, send, recv, place, volumes):
+    def __init__(
+        self, rows, near, far_y, turn, far_x, edge, side, send, recv, place, volumes
+    ):
         self.rows, self.near, self.far_y, self.turn, self.far_x = rows, near, far_y, turn, far_x
+        self.side = side
         self.edge, self.send, self.recv, self.place, self.volumes = edge, send, recv, place, volumes
         self.count = 0
         self.sent = []
@@ -87,15 +95,23 @@
 
     def columns_x(self, lane):
         inside = lax.rem(lane, 32)
+        down = jnp.zeros((C, LANES), F32)
+        up = jnp.zeros((C, LANES), F32)
         for side in range(2):
             for volume in range(self.volumes):
                 own = self.near[side, volume].astype(F32)
                 low = pltpu.roll(self.far_y[0, side, volume].astype(F32), LANES - 16, 1)
                 high = pltpu.roll(self.far_y[1, side, volume].astype(F32), 16, 1)
                 own = jnp.where(inside == 0, low, jnp.where(inside == PAD_Y - 1, high, own))
-                self.turn[side, volume] = own.astype(BF16)
-        down = self.push(self.turn, self.far_x.at[1], "gx", -1)
-        up = self.push(self.turn, self.far_x.at[0], "gx", 1)
+                self.side[volume, side] = own
+                at = 32 * (side * self.volumes + volume)
+                here = lane // 32 == at // 32
+                down = jnp.where(here, rolled(own, at - 32), down)
+                up = jnp.where(here, rolled(own, at - 64), up)
+        self.turn[0] = down.astype(BF16)
+        self.turn[1] = up.astype(BF16)
+        down = self.push(self.turn.at[0], self.far_x.at[1], "gx", -1)
+        up = self.push(self.turn.at[1], self.far_x.at[0], "gx", 1)
         return [down, up]
 
     def corners_x(self):
@@ -111,10 +127,10 @@
         return result
 
     def merged(self, side, volume, lane):
-        own = self.turn[side, volume].astype(F32)
-        low = pltpu.roll(self.far_x[0, side, volume].astype(F32), LANES - 64, 1)
-        high = pltpu.roll(self.far_x[1, side, volume].astype(F32), 64, 1)
-        return jnp.where(lane < 32, low, jnp.where(lane >= 96, high, own))
+        at = 32 * (side * self.volumes + volume)
+        low = rolled(self.far_x[0].astype(F32), -at)
+        high = rolled(self.far_x[1].astype(F32), 96 - at)
+        return jnp.where(lane < 32, low, jnp.where(lane >= 96, high, self.side[volume, side]))
 
     @staticmethod
     def arrive(pushes):
@@ -166,44 +182,51 @@
     x_a, x_b, grad, weights, params,
     y_out, dx_out, gw_out, norm_out,
     taps_x, taps_h, taps_d2, taps_d1,
-    rows_x, rows_1, rows_2, rows_e,
-    near_x, near_1, near_2, near_e,
-    fary_x, fary_1, fary_2, fary_e,
-    turn_x, turn_1, turn_2, turn_e,
-    farx_x, farx_1, farx_2, farx_e,
-    edge_x, edge_1, edge_2, edge_e,
-    side_x, side_1, side_2, side_e,
+    rows_x, rows_g, rows_1, rows_2, rows_e,
+    near_x, near_g, near_1, near_2, near_e,
+    fary_x, fary_g, fary_1, fary_2, fary_e,
+    turn_x, turn_g, turn_1, turn_2, turn_e,
+    farx_x, farx_g, farx_1, farx_2, farx_e,
+    edge_x, edge_g, edge_1, edge_2, edge_e,
+    side_x, side_g, side_1, side_2, side_e,
+    side_h,
     conv_1, conv_2, back_1,
-    sums_x, sums_z, sums_y,
+    sums,
     gw_local, gw_a, gw_sa, gw_b, gw_sb, gw_c, gw_sc, gw_d, gw_e,
     halo_send, halo_recv, sums_send, sums_recv, gw_send, gw_recv,
 ):
     place = {axis: (lax.axis_index(axis), lax.axis_size(axis)) for axis in AXES}
-    for near in (near_x, near_1, near_2, near_e):
+    for near in (near_x, near_g, near_1, near_2, near_e):
         near[...] = jnp.zeros_like(near)
     barrier = pltpu.get_barrier_semaphore()
-    partners = 0
-    for axis in AXES:
-        me, size = place[axis]
-        for step in range(1, size):
-            pl.semaphore_signal(
-                barrier, inc=1, device_id={axis: lax.rem(me + step, size)}, device_id_type=MESH
-            )
-            partners += 1
+    count = place["gx"][1] * place["gy"][1] * place["gz"][1]
+    flat = (place["gx"][0] * place["gy"][1] + place["gy"][0]) * place["gz"][1] + place["gz"][0]
+
+    def other(step):
+        return lax.rem(flat + step, count)
+
+    def greet(step, carry):
+        pl.semaphore_signal(
+            barrier, inc=1, device_id=other(step), device_id_type=pl.DeviceIdType.LOGICAL
+        )
+        return carry
+
+    lax.fori_loop(1, count, greet, 0)
 
     lane = lax.broadcasted_iota(jnp.int32, (C, LANES), 1)
     halos = []
-    for index, (rows, near, fary, turn, farx, edge, volumes) in enumerate((
-        (rows_x, near_x, fary_x, turn_x, farx_x, edge_x, 3),
-        (rows_1, near_1, fary_1, turn_1, farx_1, edge_1, 2),
-        (rows_2, near_2, fary_2, turn_2, farx_2, edge_2, 1),
-        (rows_e, near_e, fary_e, turn_e, farx_e, edge_e, 1),
+    for index, (rows, near, fary, turn, farx, edge, side, volumes) in enumerate((
+        (rows_x, near_x, fary_x, turn_x, farx_x, edge_x, side_x, 2),
+        (rows_g, near_g, fary_g, turn_g, farx_g, edge_g, side_g, 1),
+        (rows_1, near_1, fary_1, turn_1, farx_1, edge_1, side_1, 2),
+        (rows_2, near_2, fary_2, turn_2, farx_2, edge_2, side_2, 1),
+        (rows_e, near_e, fary_e, turn_e, farx_e, edge_e, side_e, 1),
     )):
         halos.append(
-            Halo(rows, near, fary, turn, farx, edge, halo_send.at[index], halo_recv.at[index],
-                 place, volumes)
-        )
-    halo_x, halo_1, halo_2, halo_e = halos
+            Halo(rows, near, fary, turn, farx, edge, side, halo_send.at[index],
+                 halo_recv.at[index], place, volumes)
+        )
+    halo_x, halo_g, halo_1, halo_2, halo_e = halos
 
     low_x, high_x = place["gx"][0] > 0, place["gx"][0] < place["gx"][1] - 1
     low_y, high_y = place["gy"][0] > 0, place["gy"][0] < place["gy"][1] - 1
@@ -332,98 +355,96 @@
             for k in range(8):
                 gw_local[j, index, k] = both[8 * j : 8 * j + 8, LANES * k : LANES * (k + 1)]
 
+    channel = lax.broadcasted_iota(jnp.int32, (C, LANES), 0)
+
     def pack(columns):
         whole = jnp.zeros((C, LANES), F32)
         for k, column in enumerate(columns):
-            whole = whole + jnp.where(lane == k, column, 0.0)
-        tile = whole[0:8]
-        for j in range(1, 4):
-            tile = tile + pltpu.roll(whole[8 * j : 8 * j + 8], 4 * j, 1)
-        return tile
-
-    def unpack(tile, count):
-        parts = [tile] + [pltpu.roll(tile, LANES - 4 * j, 1) for j in range(1, 4)]
-        whole = jnp.concatenate(parts, axis=0)
-        return [whole[:, k : k + 1] for k in range(count)]
+            whole = whole + jnp.where(lane == channel + 32 * k, column, 0.0)
+        return jnp.sum(whole, axis=0, keepdims=True)
+
+    def unpack(row, number):
+        return [
+            jnp.sum(jnp.where(lane == channel + 32 * k, row, 0.0), axis=1, keepdims=True)
+            for k in range(number)
+        ]
 
     class Total:
         def __init__(self, index):
-            self.fans = {}
-            first = 0
-            for axis, slots in (("gx", sums_x), ("gz", sums_z), ("gy", sums_y)):
-                fan = Fan(place, axis, sums_send.at[index], sums_recv.at[index], first)
-                first += fan.size - 1
-                self.fans[axis] = (fan, slots.at[index])
-
-        def start(self, axis, tile):
-            fan, slots = self.fans[axis]
-            slots[fan.me] = tile
-            mine = slots.at[fan.me]
-            fan.start(lambda to: mine, mine)
-
-        def finish(self, axis):
-            fan, slots = self.fans[axis]
-            fan.arrive()
-            tile = slots[0]
-            for k in range(1, fan.size):
-                tile = tile + slots[k]
-            return tile
+            self.slots, self.index = sums.at[index], index
+
+        def start(self, row):
+            mine = self.slots.at[flat]
+            mine[...] = row
+
+            def send(step, carry):
+                pltpu.make_async_remote_copy(
+                    src_ref=mine,
+                    dst_ref=mine,
+                    send_sem=sums_send.at[self.index],
+                    recv_sem=sums_recv.at[self.index],
+                    device_id=other(step),
+                    device_id_type=pl.DeviceIdType.LOGICAL,
+                ).start()
+                return carry
+
+            lax.fori_loop(1, count, send, 0)
+
+        def others(self, semaphore):
+            part = self.slots.at[pl.ds(0, count - 1)]
+            pltpu.make_async_copy(part, part, semaphore.at[self.index]).wait()
+
+        def finish(self):
+            self.others(sums_recv)
+            return jnp.sum(self.slots[...], axis=0)
 
         def drain(self):
-            for fan, slots in self.fans.values():
-                fan.drain()
+            self.others(sums_send)
 
     totals = [Total(index) for index in range(4)]
 
-    def reduce_with(total, tile, halo, waits):
-        total.start("gx", tile)
-        phase_1 = waits + halo.faces_y() + halo.columns_z()
-        tile = total.finish("gx")
-        total.start("gz", tile)
-        halo.arrive(phase_1[-4:])
-        phase_2 = halo.columns_y()
-        corners = halo.corners_x()
-        tile = total.finish("gz")
-        total.start("gy", tile)
-        halo.arrive(phase_2)
-        last = halo.columns_x(lane)
-        tile = total.finish("gy")
-        return tile, waits + corners + last
+    def second(halo, phase):
+        halo.arrive(phase)
+        return halo.columns_y(), halo.corners_x()
+
+    def third(halo, phase):
+        halo.arrive(phase)
+        return halo.columns_x(lane)
 
     gain_1, bias_1, gain_2, bias_2 = (params[:, k : k + 1] for k in range(4))
 
     zero = jnp.zeros((C, LANES), F32)
-    for volume, source in enumerate((x_a, x_b, grad)):
+    for source, rows, edge, at in (
+        (x_a, rows_x, edge_x, 0), (x_b, rows_x, edge_x, 1), (grad, rows_g, edge_g, 0)
+    ):
         for at_x in range(SPAN_X):
 
-            def step(block, carry, source=source, at_x=at_x, volume=volume):
+            def step(block, carry, source=source, rows=rows, at_x=at_x, at=at):
                 for k in range(8):
                     at_y = block * 8 + k
                     row = source[at_x, at_y]
-                    rows_x[volume, at_x + 1, at_y + 1] = row
+                    rows[at, at_x + 1, at_y + 1] = row
                     carry = extract(
                         row.astype(F32), (at_x + 1) * 32 + at_y + 1, carry
                     )
                 return carry
 
             carry = lax.fori_loop(0, 2, step, (zero, zero) if at_x == 0 else carry)
-        edge_x[0, volume] = carry[0].astype(BF16)
-        edge_x[1, volume] = carry[1].astype(BF16)
-
-    pl.semaphore_wait(barrier, partners)
-
-    waits_x = [halo_x.faces_x(0), halo_x.faces_x(1)]
-    phase_1 = halo_x.faces_y() + halo_x.columns_z()
-    waits_g = halo_x.faces_x(2)
-    halo_x.arrive(phase_1)
-    phase_2 = halo_x.columns_y()
-    corners = halo_x.corners_x()
-    halo_x.arrive(phase_2)
-    halo_x.arrive(halo_x.columns_x(lane))
+        edge[0, at] = carry[0].astype(BF16)
+        edge[1, at] = carry[1].astype(BF16)
+
+    pl.semaphore_wait(barrier, count - 1)
+
+    phase = halo_x.columns_z() + halo_x.faces_y()
+    waits_x = [halo_x.faces_x(0)]
+    phase, corners = second(halo_x, phase)
+    last = third(halo_x, phase)
+    waits_x.append(halo_x.faces_x(1))
     halo_x.arrive(corners)
+    halo_x.arrive(last)
     ok = [lane_keep(side) for side in range(2)]
     for side in range(2):
-        for volume in range(3):
+        for volume in range(2):
             tile = halo_x.merged(side, volume, lane)
             side_x[volume, side] = jnp.where(ok[side], tile, 0.0)
 
@@ -453,13 +474,21 @@
         )
         edge_1[0, volume] = first.astype(BF16)
         edge_1[1, volume] = last.astype(BF16)
-        waits += halo_1.faces_x(volume)
+        if volume == 0:
+            waits += halo_1.faces_x(volume)
         columns += [
             jnp.sum(total, axis=1, keepdims=True), jnp.sum(squares, axis=1, keepdims=True)
         ]
-    tile, arrivals = reduce_with(totals[0], pack(columns), halo_1, waits)
-    sums = unpack(tile, 4)
-    halo_1.arrive(arrivals)
+    totals[0].start(pack(columns))
+    phase = halo_1.columns_z() + halo_1.faces_y()
+    waits += halo_1.faces_x(1)
+    phase, corners = second(halo_1, phase)
+    last = third(halo_1, phase)
+    row = totals[0].finish()
+    halo_1.arrive(waits + corners + last)
+    phase_g = halo_g.columns_z() + halo_g.faces_y()
+    waits_g = halo_g.faces_x(0)
+    stats = unpack(row, 4)
 
     def moments(total, squares):
         mean = total / voxels
@@ -469,7 +498,7 @@
     columns = []
     affine_1 = None
     for volume in range(2):
-        mean, scale = moments(sums[2 * volume], sums[2 * volume + 1])
+        mean, scale = moments(stats[2 * volume], stats[2 * volume + 1])
         slope = jnp.broadcast_to(gain_1 * scale, (C, LANES))
         shift = jnp.broadcast_to(bias_1 - mean * gain_1 * scale, (C, LANES))
 
@@ -478,13 +507,14 @@
             return pre * sigmoid(pre)
 
         for side in range(2):
-            tile = active(halo_1.merged(side, volume, lane))
-            side_1[volume, side] = jnp.where(ok[side], tile, 0.0)
+            tile = halo_1.merged(side, volume, lane)
+            side_1[volume, side] = tile
+            side_h[volume, side] = jnp.where(ok[side], active(tile), 0.0)
         build(
             taps_h, volume,
             lambda at_x, at_y, volume=volume: active(rows_1[volume, at_x, at_y].astype(F32)),
             lambda at_x, at_y, volume=volume: active(conv_1[volume, at_x, at_y]),
-            (side_1.at[volume, 0], side_1.at[volume, 1]),
+            (side_h.at[volume, 0], side_h.at[volume, 1]),
         )
         if volume == 0:
 
@@ -494,6 +524,7 @@
                 return total + tile, squares + tile * tile
 
             total, squares = convolve(taps_h, 0, 1, emit, (zero,) * 2)
+            phase_g, corners_g = second(halo_g, phase_g)
         else:
 
             def emit(at_x, at_y, tile, carry):
@@ -506,15 +537,17 @@
             total, squares, first, last = convolve(taps_h, 1, 1, emit, (zero,) * 4)
             edge_2[0, 0] = first.astype(BF16)
             edge_2[1, 0] = last.astype(BF16)
-            waits = halo_2.faces_x(0)
         columns += [
             jnp.sum(total, axis=1, keepdims=True), jnp.sum(squares, axis=1, keepdims=True)
         ]
     mean_1, scale_1 = mean, scale
-    tile, arrivals = reduce_with(totals[1], pack(columns), halo_2, waits)
-    sums = unpack(tile, 4)
-
-    mean_2, scale_2 = moments(sums[2], sums[3])
+    totals[1].start(pack(columns))
+    phase = halo_2.columns_z() + halo_2.faces_y()
+    waits = halo_2.faces_x(0)
+    last_g = third(halo_g, phase_g)
+    stats = unpack(totals[1].finish(), 4)
+
+    mean_2, scale_2 = moments(stats[2], stats[3])
 
     def layer_of(mean, scale, gain, bias):
         norm_slope = jnp.broadcast_to(scale, (C, LANES))
@@ -561,11 +594,12 @@
     columns = sum_rows(
         slope_2,
         lambda at_x, at_y: conv_2[1, at_x, at_y],
-        lambda at_x, at_y: rows_x[2, at_x + 1, at_y + 1].astype(F32),
+        lambda at_x, at_y: rows_g[0, at_x + 1, at_y + 1].astype(F32),
     )
-    totals[2].start("gx", pack(columns))
-
-    mean_a, scale_a = moments(sums[0], sums[1])
+    totals[2].start(pack(columns))
+    phase, corners = second(halo_2, phase)
+
+    mean_a, scale_a = moments(stats[0], stats[1])
     slope_a = jnp.broadcast_to(gain_2 * scale_a, (C, LANES))
     shift_a = jnp.broadcast_to(bias_2 - mean_a * gain_2 * scale_a, (C, LANES))
     for at_x in range(SPAN_X):
@@ -579,23 +613,22 @@
 
         lax.fori_loop(0, 2, step, 0)
 
-    totals[2].start("gz", totals[2].finish("gx"))
-    totals[2].start("gy", totals[2].finish("gz"))
-    halo_2.arrive(arrivals)
-    halo_x.arrive(waits_g)
-    sum_d2, sum_x2 = unpack(totals[2].finish("gy"), 2)
+    last = third(halo_2, phase)
+    halo_g.arrive(waits_g + corners_g + last_g)
+    halo_2.arrive(waits + corners + last)
+    sum_d2, sum_x2 = unpack(totals[2].finish(), 2)
 
     delta_2 = delta_of(slope_2, sum_d2, sum_x2, gain_2, scale_2)
     for side in range(2):
-        tile = delta_2(halo_2.merged(side, 0, lane), side_x[2, side])
+        tile = delta_2(halo_2.merged(side, 0, lane), halo_g.merged(side, 0, lane))
         side_2[0, side] = jnp.where(ok[side], tile, 0.0)
     build(
         taps_d2, 0,
         lambda at_x, at_y: delta_2(
-            rows_2[0, at_x, at_y].astype(F32), rows_x[2, at_x, at_y].astype(F32)
+            rows_2[0, at_x, at_y].astype(F32), rows_g[0, at_x, at_y].astype(F32)
         ),
         lambda at_x, at_y: delta_2(
-            conv_2[1, at_x, at_y], rows_x[2, at_x + 1, at_y + 1].astype(F32)
+            conv_2[1, at_x, at_y], rows_g[0, at_x + 1, at_y + 1].astype(F32)
         ),
         (side_2.at[0, 0], side_2.at[0, 1]),
     )
@@ -612,18 +645,21 @@
     total, weighted, first, last = convolve(taps_d2, 0, 2, emit, (zero,) * 4)
     edge_e[0, 0] = first.astype(BF16)
     edge_e[1, 0] = last.astype(BF16)
-    waits = halo_e.faces_x(0)
     columns = [
         jnp.sum(total, axis=1, keepdims=True), jnp.sum(weighted, axis=1, keepdims=True)
     ]
-    tile, arrivals = reduce_with(totals[3], pack(columns), halo_e, waits)
+    totals[3].start(pack(columns))
+    phase = halo_e.columns_z() + halo_e.faces_y()
+    waits = halo_e.faces_x(0)
     kernel_grad(taps_h, 1, taps_d2, 1)
-    sum_d1, sum_x1 = unpack(tile, 2)
-    halo_e.arrive(arrivals)
+    phase, corners = second(halo_e, phase)
+    last = third(halo_e, phase)
+    sum_d1, sum_x1 = unpack(totals[3].finish(), 2)
+    halo_e.arrive(waits + corners + last)
 
     delta_1 = delta_of(slope_1, sum_d1, sum_x1, gain_1, scale_1)
     for side in range(2):
-        tile = delta_1(halo_1.merged(side, 1, lane), halo_e.merged(side, 0, lane))
+        tile = delta_1(side_1[1, side], halo_e.merged(side, 0, lane))
         side_e[0, side] = jnp.where(ok[side], tile, 0.0)
     build(
         taps_d1, 0,
@@ -719,22 +755,22 @@
     def sized(*shape, kind=BF16):
         return pltpu.VMEM(shape, kind)
 
-    volumes = (3, 2, 1, 1)
+    volumes = (2, 1, 2, 1, 1)
+    devices = math.prod(lax.axis_size(axis) for axis in AXES)
     scratch = [sized(count, PAD_X, PAD_Y, TAPS, LANES) for count in (2, 2, 1, 1)]
     scratch += [sized(count, PAD_X, PAD_Y, C, LANES) for count in volumes]
     scratch += [sized(2, count, C, LANES) for count in volumes]
     scratch += [sized(2, 2, count, C, LANES) for count in volumes]
-    scratch += [sized(2, count, C, LANES) for count in volumes]
-    scratch += [sized(2, 2, count, C, LANES) for count in volumes]
+    scratch += [sized(2, C, LANES) for count in volumes]
+    scratch += [sized(2, C, LANES) for count in volumes]
     scratch += [sized(2, count, C, LANES) for count in volumes]
     scratch += [sized(count, 2, C, LANES, kind=F32) for count in volumes]
+    scratch += [sized(2, 2, C, LANES, kind=F32)]
     scratch += [
         sized(2, SPAN_X, SPAN_Y, C, LANES, kind=F32),
         sized(2, SPAN_X, SPAN_Y, C, LANES, kind=F32),
         sized(SPAN_X, SPAN_Y, C, LANES, kind=F32),
-        sized(4, 4, 8, LANES, kind=F32),
-        sized(4, 8, 8, LANES, kind=F32),
-        sized(4, 4, 8, LANES, kind=F32),
+        sized(4, devices, 1, LANES, kind=F32),
         sized(4, 2, 8, 8, LANES, kind=F32),
         sized(4, 2, 8, 8, LANES, kind=F32),
         sized(8, 2, 8, LANES, kind=F32),
@@ -744,10 +780,10 @@
         sized(2, 8, LANES, kind=F32),
         sized(8, 2, 8, LANES, kind=F32),
         sized(4, 8, 2, 8, LANES, kind=F32),
-        pltpu.SemaphoreType.DMA((4, 24)),
-        pltpu.SemaphoreType.DMA((4, 24)),
-        pltpu.SemaphoreType.DMA((4, 16)),
-        pltpu.SemaphoreType.DMA((4, 16)),
+        pltpu.SemaphoreType.DMA((5, 24)),
+        pltpu.SemaphoreType.DMA((5, 24)),
+        pltpu.SemaphoreType.DMA((4,)),
+        pltpu.SemaphoreType.DMA((4,)),
         pltpu.SemaphoreType.DMA((24,)),
         pltpu.SemaphoreType.DMA((24,)),
     ]

time: 135 us -> 119 us (0.88)
  Pallas kernels: 119 us -> 103 us
    pallas_call x1, Pallas kernels: 119 us -> 103 us  [body(): pl.pallas_call(functools.partial(kernel, voxels), out_shape=(jax.ShapeDty...]
where the time goes in v2:
time: 119 us; the launch traced here: 118 us
  Pallas kernels  103 us (87%)
  local copies, waits for them, and re-layouts  12.8 us (11%)
  other arithmetic  1.87 us (2%)
    pallas_call x1, Pallas kernels, body(): pl.pallas_call(functools.partial(kernel, voxels), out_shape=(jax.ShapeDty...  103 us
    unnamed x18, local copies, waits for them, and re-layouts  6.68 us

profile of v2, /device:TPU:1, one launch (start us, length us, event | category | flops | bytes accessed | tf_op | source)
XLA Modules:
  0.0 118.3 jit_solution(242704556509190162)
XLA Ops:
  0.6 0.0 copy-start.2
  0.6 0.8 pad_maximum_fusion.1
  1.4 0.7 copy.52.params
  2.1 0.0 copy-start
  2.1 1.0 rev.8
  3.1 0.1 copy.59
  3.2 0.0 copy-start.1
  3.2 1.0 rev.7
  4.2 0.1 copy.58
  4.4 0.1 fusion.13
  4.5 0.0 copy-done.2
  4.5 0.8 copy.63
  5.3 0.0 copy-done
  5.3 0.2 copy.49
  5.4 0.2 reshape.26
  5.6 0.0 copy-done.1
  5.7 0.0 copy-start.3
  5.7 0.0 copy-start.4
  5.7 0.2 copy.48
  5.8 0.2 reshape.25
  6.0 0.1 fusion.9
  6.1 0.9 pad_maximum_fusion.weights
  7.1 0.0 copy-done.3
  7.1 0.0 copy-done.4
  7.1 1.0 copy_bitcast_fusion
  8.1 102.8 %shard_map.128 = (bf16[2,16,32,128]{3,2,1,0:T(8,128)(2,1)}, bf16[2,16,32,128]{3,2,1,0:T(8,128)(2,1)}, f32[2,32,1024]{2,1,0:T(8,128)}, f32[32,128]{1,0:T(8,128)}) custom-call(bf16[2,16,32,128]{3,2,1,0:T(8,128)(2,1)} %bitcast.37, bf16[2,16,32,128]{3,2,1,0:T(8,128)(2,1)} %get-tuple-element.35.x_b, bf16[2,16,32,128]{3,2,1,0:T(8,128)(2,1)} %get-tuple-element.34.grad, ...), custom_call_target="tpu_custom_call" | custom-call | tf_op jit(solution)/shard_map/pallas_call | solution.py:791
  110.9 0.0 copy-start.5
  110.9 1.8 %copy.53 = bf16[32,2,16,128]{3,2,1,0:T(8,128)(2,1)} copy(bf16[32,2,16,128]{3,0,2,1:T(8,128)(2,1)} %bitcast.43) | data formatting | bytes 524288
  112.7 1.8 %copy.54 = bf16[32,2,16,128]{3,2,1,0:T(8,128)(2,1)} copy(bf16[32,2,16,128]{3,0,2,1:T(8,128)(2,1)} %bitcast.42) | data formatting | bytes 524288
  114.5 0.7 slice_bitcast_fusion.2
  115.2 0.7 copy.57
  115.8 0.0 copy-done.5
  115.9 0.6 reshape.29
  116.5 0.2 slice_bitcast_fusion
  116.7 0.8 copy.56
  117.5 0.8 copy.55
  (1 shorter events, 0.0 us)
Async XLA Ops:
  0.6 3.8 %copy-start.2 = (bf16[32,2,16,128]{3,2,1,0:T(8,128)(2,1)S(1)}, bf16[32,2,16,128]{3,2,1,0:T(8,128)(2,1)}, u32[]{:S(2)}) copy-start(bf16[32,2,16,128]{3,2,1,0:T(8,128)(2,1)} %param.9) | copy-start | bytes 786436
  2.1 3.2 %copy-start = (bf16[3,3,3,32,32]{4,3,2,1,0:T(8,128)(2,1)S(1)}, bf16[3,3,3,32,32]{4,3,2,1,0:T(8,128)(2,1)}, u32[]{:S(2)}) copy-start(bf16[3,3,3,32,32]{4,3,2,1,0:T(8,128)(2,1)} %param.12) | copy-start | bytes 165892
  3.2 2.4 %copy-start.1 = (bf16[3,3,3,32,32]{4,3,2,1,0:T(8,128)(2,1)S(1)}, bf16[3,3,3,32,32]{4,3,2,1,0:T(8,128)(2,1)}, u32[]{:S(2)}) copy-start(bf16[3,3,3,32,32]{4,3,2,1,0:T(8,128)(2,1)} %param.11) | copy-start | bytes 165892
  5.7 1.4 %copy-start.3 = (bf16[32,2,16,128]{3,2,1,0:T(8,128)(2,1)S(1)}, bf16[32,2,16,128]{3,2,1,0:T(8,128)(2,1)}, u32[]{:S(2)}) copy-start(bf16[32,2,16,128]{3,2,1,0:T(8,128)(2,1)} %param.17) | copy-start | bytes 786436
  5.7 1.4 %copy-start.4 = (bf16[32,2,16,128]{3,2,1,0:T(8,128)(2,1)S(1)}, bf16[32,2,16,128]{3,2,1,0:T(8,128)(2,1)}, u32[]{:S(2)}) copy-start(bf16[32,2,16,128]{3,2,1,0:T(8,128)(2,1)} %param.10) | copy-start | bytes 786436
  110.9 4.9 %copy-start.5 = (f32[2,32,1024]{2,1,0:T(8,128)S(1)}, f32[2,32,1024]{2,1,0:T(8,128)}, u32[]{:S(2)}) copy-start(f32[2,32,1024]{2,1,0:T(8,128)} %get-tuple-element.11) | copy-start | bytes 786436

commit v3 on v2

--- a/solution.py
+++ b/solution.py
@@ -148,35 +148,6 @@
                 copy.wait_send()
 
 
-class Fan:
-    def __init__(self, place, axis, send, recv, first):
-        self.me, self.size = place[axis]
-        self.axis, self.send, self.recv, self.first = axis, send, recv, first
-        self.copies = []
-
-    def start(self, source_of, target):
-        for step in range(1, self.size):
-            to = lax.rem(self.me + step, self.size)
-            copy = pltpu.make_async_remote_copy(
-                src_ref=source_of(to),
-                dst_ref=target,
-                send_sem=self.send.at[self.first + step - 1],
-                recv_sem=self.recv.at[self.first + step - 1],
-                device_id={self.axis: to},
-                device_id_type=MESH,
-            )
-            copy.start()
-            self.copies.append(copy)
-
-    def arrive(self):
-        for copy in self.copies:
-            copy.wait_recv()
-
-    def drain(self):
-        for copy in self.copies:
-            copy.wait_send()
-
-
 def kernel(
     voxels,
     x_a, x_b, grad, weights, params,
@@ -192,18 +163,56 @@
     side_h,
     conv_1, conv_2, back_1,
     sums,
-    gw_local, gw_a, gw_sa, gw_b, gw_sb, gw_c, gw_sc, gw_d, gw_e,
+    norms, slopes, early_out, early_in, late_out, late_in, gathered, pairs,
     halo_send, halo_recv, sums_send, sums_recv, gw_send, gw_recv,
 ):
     place = {axis: (lax.axis_index(axis), lax.axis_size(axis)) for axis in AXES}
     for near in (near_x, near_g, near_1, near_2, near_e):
         near[...] = jnp.zeros_like(near)
+    for chunks in (early_out, late_out):
+        for j in range(4):
+            chunks[32 * j + 28 : 32 * j + 32] = jnp.zeros((4, 4, LANES), F32)
     barrier = pltpu.get_barrier_semaphore()
     count = place["gx"][1] * place["gy"][1] * place["gz"][1]
     flat = (place["gx"][0] * place["gy"][1] + place["gy"][0]) * place["gz"][1] + place["gz"][0]
 
+    chip_x, chip_y = place["gy"][0], place["gz"][0] // 2
+    chip_z = place["gx"][0] // 2 * 2 + lax.rem(place["gz"][0], 2)
+    core = lax.rem(place["gx"][0], 2)
+
     def other(step):
         return lax.rem(flat + step, count)
+
+    def fan_out(source_of, target, send, recv):
+        spots = []
+        for step_z, step_core in ((2, 1), (2, 0), (1, 1), (3, 1), (1, 0), (3, 0), (0, 1), (0, 0)):
+            to_z, to_core = lax.rem(chip_z + step_z, 4), lax.rem(core + step_core, 2)
+            spots.append(to_z // 2 * 64 + to_core * 32 + lax.rem(to_z, 2))
+
+        def copies(plane, chosen):
+            to_x = lax.rem(chip_x + plane // 4 + 1, 4)
+            to_y = lax.rem(chip_y + lax.rem(plane, 4) + 1, 4)
+            for spot in chosen:
+                to = spot + to_x * 8 + to_y * 2
+                pltpu.make_async_remote_copy(
+                    src_ref=source_of(to), dst_ref=target, send_sem=send, recv_sem=recv,
+                    device_id=to, device_id_type=pl.DeviceIdType.LOGICAL,
+                ).start()
+
+        def most(plane, carry):
+            copies(plane, spots[:-1])
+            return carry
+
+        def rest(plane, carry):
+            copies(plane, spots[-1:])
+            return carry
+
+        lax.fori_loop(0, 16, most, 0)
+        lax.fori_loop(0, 15, rest, 0)
+
+    def fan_in(slots, semaphore):
+        part = slots.at[pl.ds(0, count - 1)]
+        pltpu.make_async_copy(part, part, semaphore).wait()
 
     def greet(step, carry):
         pl.semaphore_signal(
@@ -328,16 +337,17 @@
 
         return lax.fori_loop(0, SPAN_Y // GROUP, step, carry)
 
-    def kernel_grad(taps, volume, upstream, index):
+    def kernel_grad(taps, volume, row_of, out, first_row, plain=False):
+        high = SPAN_X * C + (16 if plain else 0)
+
         def step(block, total):
             first = block * GROUP
             left, right = [], []
             for k in range(GROUP):
-                left.append(
-                    upstream[0, pl.ds(1, SPAN_X), first + k + 1, C : 2 * C].reshape(
-                        SPAN_X * C, LANES
-                    )
-                )
+                rows = [row_of(at_x, first + k) for at_x in range(SPAN_X)]
+                if plain:
+                    rows.append(jnp.ones((16, LANES), BF16))
+                left.append(jnp.concatenate(rows, axis=0))
                 right.append(taps[volume, :, pl.ds(first + k, 3)].reshape(DEPTH, LANES))
             return total + lax.dot_general(
                 jnp.concatenate(left, axis=1),
@@ -346,14 +356,25 @@
                 preferred_element_type=F32,
             )
 
-        total = lax.fori_loop(
-            0, SPAN_Y // GROUP, step, jnp.zeros((SPAN_X * C, DEPTH), F32)
-        )
-        both = total[0:C, 0:FLAT] + total[C : 2 * C, 3 * TAPS : 3 * TAPS + FLAT]
-        both = jnp.concatenate([both, jnp.zeros((C, 1024 - FLAT), F32)], axis=1)
-        for j in range(4):
-            for k in range(8):
-                gw_local[j, index, k] = both[8 * j : 8 * j + 8, LANES * k : LANES * (k + 1)]
+        total = lax.fori_loop(0, SPAN_Y // GROUP, step, jnp.zeros((high, DEPTH), F32))
+        slab = 3 * TAPS
+
+        def wide(value):
+            return jnp.concatenate(
+                [value, jnp.zeros((value.shape[0], 7 * LANES - FLAT), F32)], axis=1
+            )
+
+        both = wide(total[0:C, 0:FLAT] + total[C : 2 * C, slab : slab + FLAT])
+        if plain:
+            alone = total[2 * C : 2 * C + 1]
+            alone = wide(alone[:, 0:FLAT] + alone[:, slab : slab + FLAT])
+        for k in range(7):
+            lanes = slice(LANES * k, LANES * (k + 1))
+            for pair in range(16):
+                spot = (pair // 4 * 8 + k) * 4 + pair % 4
+                out[spot, first_row : first_row + 2] = both[2 * pair : 2 * pair + 2, lanes]
+                if plain:
+                    out[spot, 2:3] = alone[:, lanes]
 
     channel = lax.broadcasted_iota(jnp.int32, (C, LANES), 0)
 
@@ -377,29 +398,16 @@
             mine = self.slots.at[flat]
             mine[...] = row
 
-            def send(step, carry):
-                pltpu.make_async_remote_copy(
-                    src_ref=mine,
-                    dst_ref=mine,
-                    send_sem=sums_send.at[self.index],
-                    recv_sem=sums_recv.at[self.index],
-                    device_id=other(step),
-                    device_id_type=pl.DeviceIdType.LOGICAL,
-                ).start()
-                return carry
-
-            lax.fori_loop(1, count, send, 0)
-
-        def others(self, semaphore):
-            part = self.slots.at[pl.ds(0, count - 1)]
-            pltpu.make_async_copy(part, part, semaphore.at[self.index]).wait()
+            fan_out(
+                lambda to: mine, mine, sums_send.at[self.index], sums_recv.at[self.index]
+            )
 
         def finish(self):
-            self.others(sums_recv)
+            fan_in(self.slots, sums_recv.at[self.index])
             return jnp.sum(self.slots[...], axis=0)
 
         def drain(self):
-            self.others(sums_send)
+            fan_in(self.slots, sums_send.at[self.index])
 
     totals = [Total(index) for index in range(4)]
 
@@ -506,6 +514,15 @@
             pre = value * slope + shift
             return pre * sigmoid(pre)
 
+        norm_slope = jnp.broadcast_to(scale, (C, LANES))
+        norm_shift = jnp.broadcast_to(-mean * scale, (C, LANES))
+
+        def own_row(at_x, at_y, volume, active, norm_slope=norm_slope, norm_shift=norm_shift):
+            value = conv_1[volume, at_x, at_y]
+            if volume == 1:
+                norms[at_x, at_y] = (value * norm_slope + norm_shift).astype(BF16)
+            return active(value)
+
         for side in range(2):
             tile = halo_1.merged(side, volume, lane)
             side_1[volume, side] = tile
@@ -513,7 +530,7 @@
         build(
             taps_h, volume,
             lambda at_x, at_y, volume=volume: active(rows_1[volume, at_x, at_y].astype(F32)),
-            lambda at_x, at_y, volume=volume: active(conv_1[volume, at_x, at_y]),
+            functools.partial(own_row, volume=volume, active=active),
             (side_h.at[volume, 0], side_h.at[volume, 1]),
         )
         if volume == 0:
@@ -545,6 +562,11 @@
     phase = halo_2.columns_z() + halo_2.faces_y()
     waits = halo_2.faces_x(0)
     last_g = third(halo_g, phase_g)
+    kernel_grad(taps_x, 1, lambda at_x, at_y: norms[at_x, at_y], early_out, 0, plain=True)
+    fan_out(
+        lambda to: early_out.at[to], early_in.at[flat], gw_send.at[0], gw_recv.at[0]
+    )
+    early_in[flat] = early_out[flat]
     stats = unpack(totals[1].finish(), 4)
 
     mean_2, scale_2 = moments(stats[2], stats[3])
@@ -640,6 +662,7 @@
         rows_e[0, at_x + 1, at_y + 1] = tile.astype(BF16)
         first, last = extract(tile, (at_x + 1) * 32 + at_y + 1, (first, last))
         slope, normed = slope_1(conv_1[1, at_x, at_y], tile)
+        slopes[at_x, at_y] = slope.astype(BF16)
         return total + slope, weighted + slope * normed, first, last
 
     total, weighted, first, last = convolve(taps_d2, 0, 2, emit, (zero,) * 4)
@@ -651,9 +674,14 @@
     totals[3].start(pack(columns))
     phase = halo_e.columns_z() + halo_e.faces_y()
     waits = halo_e.faces_x(0)
-    kernel_grad(taps_h, 1, taps_d2, 1)
+    kernel_grad(taps_x, 1, lambda at_x, at_y: slopes[at_x, at_y], late_out, 0)
     phase, corners = second(halo_e, phase)
+    kernel_grad(
+        taps_h, 1, lambda at_x, at_y: taps_d2[0, at_x + 1, at_y + 1, C : 2 * C], late_out, 2
+    )
     last = third(halo_e, phase)
+    fan_out(lambda to: late_out.at[to], late_in.at[flat], gw_send.at[1], gw_recv.at[1])
+    late_in[flat] = late_out[flat]
     sum_d1, sum_x1 = unpack(totals[3].finish(), 2)
     halo_e.arrive(waits + corners + last)
 
@@ -669,14 +697,24 @@
         lambda at_x, at_y: delta_1(conv_1[1, at_x, at_y], back_1[at_x, at_y]),
         (side_e.at[0, 0], side_e.at[0, 1]),
     )
-    kernel_grad(taps_x, 1, taps_d1, 0)
-
-    fan_a = Fan(place, "gx", gw_send, gw_recv, 0)
-    fan_b = Fan(place, "gz", gw_send, gw_recv, 3)
-    fan_c = Fan(place, "gy", gw_send, gw_recv, 10)
-    fan_d = Fan(place, "gz", gw_send, gw_recv, 13)
-    fan_e = Fan(place, "gx", gw_send, gw_recv, 20)
-    fan_a.start(lambda to: gw_local.at[to], gw_a.at[fan_a.me])
+    whole = 1.0 / math.sqrt(voxels)
+    for k, column in enumerate(
+        (gain_1 * scale_1 * whole, sum_d1 / voxels, sum_x1 / voxels)
+    ):
+        tile = jnp.broadcast_to(column, (C, LANES))
+        for pair in range(16):
+            pairs[k, pair] = tile[2 * pair : 2 * pair + 2]
+    fan_in(early_in, gw_recv.at[0])
+    early = jnp.sum(early_in[...], axis=0)
+    at = flat // 32 * 4 + lax.rem(flat, 4)
+    fan_in(late_in, gw_recv.at[1])
+    late = jnp.sum(late_in[...], axis=0)
+    gathered[flat, 0:2] = pairs[0, at] * (
+        late[0:2] - pairs[1, at] * early[2:3] - pairs[2, at] * early[0:2]
+    )
+    gathered[flat, 2:4] = late[2:4] * whole
+    mine = gathered.at[flat]
+    fan_out(lambda to: mine, mine, gw_send.at[2], gw_recv.at[2])
 
     def emit(at_x, at_y, tile, carry):
         dx_out[at_x, at_y] = tile.astype(BF16)
@@ -684,50 +722,19 @@
 
     convolve(taps_d1, 0, 3, emit, 0)
 
-    fan_a.arrive()
-    gw_a[fan_a.me] = gw_local[fan_a.me]
-    for index in range(2):
-        for k in range(8):
-            tile = gw_a[0, index, k]
-            for j in range(1, 4):
-                tile = tile + gw_a[j, index, k]
-            gw_sa[k, index] = tile
-    fan_b.start(lambda to: gw_sa.at[to], gw_b.at[fan_b.me])
-    fan_b.arrive()
-    gw_b[fan_b.me] = gw_sa[fan_b.me]
-    for index in range(2):
-        tile = gw_b[0, index]
-        for j in range(1, 8):
-            tile = tile + gw_b[j, index]
-        gw_c[fan_c.me, index] = tile
-    fan_c.start(lambda to: gw_c.at[fan_c.me], gw_c.at[fan_c.me])
-    fan_c.arrive()
-    for index in range(2):
-        tile = gw_c[0, index]
-        for j in range(1, 4):
-            tile = tile + gw_c[j, index]
-        gw_d[fan_d.me, index] = tile * (1.0 / math.sqrt(voxels))
-    fan_d.start(lambda to: gw_d.at[fan_d.me], gw_d.at[fan_d.me])
-    fan_d.arrive()
-    fan_e.start(lambda to: gw_d, gw_e.at[fan_e.me])
-    gw_e[fan_e.me] = gw_d[...]
-    norms = [sum_x1, sum_d1, sum_x2, sum_d2]
-    whole = jnp.zeros((C, LANES), F32)
-    for k, column in enumerate(norms):
-        whole = whole + jnp.where(lane == k, column, 0.0)
-    norm_out[...] = whole * (1.0 / math.sqrt(voxels))
-    fan_e.arrive()
-    for j in range(4):
-        for index in range(2):
-            for k in range(8):
-                gw_out[index, 8 * j : 8 * j + 8, LANES * k : LANES * (k + 1)] = gw_e[j, k, index]
+    tile = jnp.zeros((C, LANES), F32)
+    for k, column in enumerate((sum_x1, sum_d1, sum_x2, sum_d2)):
+        tile = tile + jnp.where(lane == k, column, 0.0)
+    norm_out[...] = tile * whole
+    fan_in(gathered, gw_recv.at[2])
+    gw_out[...] = gathered[...]
 
     for halo in halos:
         halo.drain()
     for total in totals:
         total.drain()
-    for fan in (fan_a, fan_b, fan_c, fan_d, fan_e):
-        fan.drain()
+    for k, chunks in enumerate((early_out, late_out, gathered)):
+        fan_in(chunks, gw_send.at[k])
 
 
 def stacked(weight):
@@ -771,21 +778,20 @@
         sized(2, SPAN_X, SPAN_Y, C, LANES, kind=F32),
         sized(SPAN_X, SPAN_Y, C, LANES, kind=F32),
         sized(4, devices, 1, LANES, kind=F32),
-        sized(4, 2, 8, 8, LANES, kind=F32),
-        sized(4, 2, 8, 8, LANES, kind=F32),
-        sized(8, 2, 8, LANES, kind=F32),
-        sized(8, 2, 8, LANES, kind=F32),
-        sized(2, 8, LANES, kind=F32),
-        sized(4, 2, 8, LANES, kind=F32),
-        sized(2, 8, LANES, kind=F32),
-        sized(8, 2, 8, LANES, kind=F32),
-        sized(4, 8, 2, 8, LANES, kind=F32),
+        sized(SPAN_X, SPAN_Y, C, LANES),
+        sized(SPAN_X, SPAN_Y, C, LANES),
+        sized(devices, 4, LANES, kind=F32),
+        sized(devices, 4, LANES, kind=F32),
+        sized(devices, 4, LANES, kind=F32),
+        sized(devices, 4, LANES, kind=F32),
+        sized(devices, 4, LANES, kind=F32),
+        sized(3, 16, 2, LANES, kind=F32),
         pltpu.SemaphoreType.DMA((5, 24)),
         pltpu.SemaphoreType.DMA((5, 24)),
         pltpu.SemaphoreType.DMA((4,)),
         pltpu.SemaphoreType.DMA((4,)),
-        pltpu.SemaphoreType.DMA((24,)),
-        pltpu.SemaphoreType.DMA((24,)),
+        pltpu.SemaphoreType.DMA((3,)),
+        pltpu.SemaphoreType.DMA((3,)),
     ]
     in_vmem = pl.BlockSpec(memory_space=pltpu.VMEM)
     y_a, dx_b, kernels, norms = pl.pallas_call(
@@ -793,7 +799,7 @@
         out_shape=(
             jax.ShapeDtypeStruct((SPAN_X, SPAN_Y, C, LANES), BF16),
             jax.ShapeDtypeStruct((SPAN_X, SPAN_Y, C, LANES), BF16),
-            jax.ShapeDtypeStruct((2, C, 1024), F32),
+            jax.ShapeDtypeStruct((devices, 4, LANES), F32),
             jax.ShapeDtypeStruct((C, LANES), F32),
         ),
         in_specs=[in_vmem] * 5,
@@ -807,7 +813,8 @@
     def by_channels(block):
         return block.transpose(2, 0, 1, 3)
 
-    grads = kernels[:, :, :FLAT].reshape(2, C, 3, 3, 3, C).transpose(0, 2, 3, 4, 1, 5)
+    kernels = kernels.reshape(4, 8, 4, 2, 2, LANES).transpose(3, 0, 2, 4, 1, 5)
+    grads = kernels.reshape(2, C, 8 * LANES)[:, :, :FLAT].reshape(2, C, 3, 3, 3, C).transpose(0, 2, 3, 4, 1, 5)
     return (by_channels(y_a), by_channels(dx_b), grads[0], grads[1], norms[:, :4].T)
 
 

time: 119 us -> 103 us (0.87)
  Pallas kernels: 103 us -> 87 us
    pallas_call x1, Pallas kernels: 103 us -> 87 us  [body(): pl.pallas_call(functools.partial(kernel, voxels), out_shape=(jax.ShapeDty...]
where the time goes in v3:
time: 103 us
  Pallas kernels  87 us (84%)
  local copies, waits for them, and re-layouts  13 us (13%)
  other arithmetic  1.87 us (2%)
    pallas_call x1, Pallas kernels, body(): pl.pallas_call(functools.partial(kernel, voxels), out_shape=(jax.ShapeDty...  87 us
    unnamed x18, local copies, waits for them, and re-layouts  6.68 us

profile of v3, /device:TPU:1, one launch (start us, length us, event | category | flops | bytes accessed | tf_op | source)
XLA Modules:
  0.0 102.6 jit_solution(12883740008166426447)
XLA Ops:
  0.6 0.0 copy-start.2
  0.6 0.8 pad_maximum_fusion.1
  1.4 0.7 copy.52.params
  2.1 0.0 copy-start
  2.1 1.0 rev.8
  3.1 0.1 copy.60
  3.2 0.0 copy-start.1
  3.2 1.0 rev.7
  4.2 0.1 copy.59
  4.4 0.1 fusion.13
  4.5 0.0 copy-done.2
  4.5 0.8 copy.66
  5.3 0.0 copy-done
  5.3 0.2 copy.49
  5.4 0.2 reshape.32
  5.6 0.0 copy-done.1
  5.7 0.0 copy-start.4
  5.7 0.0 copy-start.5
  5.7 0.2 copy.48
  5.8 0.2 reshape.31
  6.0 0.1 fusion.9
  6.1 0.9 pad_maximum_fusion.weights
  7.1 0.0 copy-done.4
  7.1 0.0 copy-done.5
  7.1 1.0 copy_bitcast_fusion.1
  8.1 87.0 %shard_map.128 = (bf16[2,16,32,128]{3,2,1,0:T(8,128)(2,1)}, bf16[2,16,32,128]{3,2,1,0:T(8,128)(2,1)}, f32[128,4,128]{2,1,0:T(4,128)}, f32[32,128]{1,0:T(8,128)}) custom-call(bf16[2,16,32,128]{3,2,1,0:T(8,128)(2,1)} %bitcast.44, bf16[2,16,32,128]{3,2,1,0:T(8,128)(2,1)} %get-tuple-element.35.x_b, bf16[2,16,32,128]{3,2,1,0:T(8,128)(2,1)} %get-tuple-element.34.grad, ...), custom_call_target="tpu_custom_call" | custom-call | tf_op jit(solution)/shard_map/pallas_call | solution.py:797
  95.0 0.0 copy-start.3
  95.0 1.8 %copy.54 = bf16[32,2,16,128]{3,2,1,0:T(8,128)(2,1)} copy(bf16[32,2,16,128]{3,0,2,1:T(8,128)(2,1)} %bitcast.51) | data formatting | bytes 524288
  96.8 1.8 %copy.55 = bf16[32,2,16,128]{3,2,1,0:T(8,128)(2,1)} copy(bf16[32,2,16,128]{3,0,2,1:T(8,128)(2,1)} %bitcast.50) | data formatting | bytes 524288
  98.6 0.7 slice_bitcast_fusion.2
  99.3 0.7 copy.58
  100.0 0.0 copy-done.3
  100.0 0.1 copy.65
  100.1 0.6 reshape.37
  100.7 0.2 slice_bitcast_fusion
  100.9 0.8 copy.57
  101.8 0.8 copy.56
  (2 shorter events, 0.1 us)
Async XLA Ops:
  0.6 3.8 %copy-start.2 = (bf16[32,2,16,128]{3,2,1,0:T(8,128)(2,1)S(1)}, bf16[32,2,16,128]{3,2,1,0:T(8,128)(2,1)}, u32[]{:S(2)}) copy-start(bf16[32,2,16,128]{3,2,1,0:T(8,128)(2,1)} %param.9) | copy-start | bytes 786436
  2.1 3.2 %copy-start = (bf16[3,3,3,32,32]{4,3,2,1,0:T(8,128)(2,1)S(1)}, bf16[3,3,3,32,32]{4,3,2,1,0:T(8,128)(2,1)}, u32[]{:S(2)}) copy-start(bf16[3,3,3,32,32]{4,3,2,1,0:T(8,128)(2,1)} %param.12) | copy-start | bytes 165892
  3.2 2.4 %copy-start.1 = (bf16[3,3,3,32,32]{4,3,2,1,0:T(8,128)(2,1)S(1)}, bf16[3,3,3,32,32]{4,3,2,1,0:T(8,128)(2,1)}, u32[]{:S(2)}) copy-start(bf16[3,3,3,32,32]{4,3,2,1,0:T(8,128)(2,1)} %param.11) | copy-start | bytes 165892
  5.7 1.4 %copy-start.4 = (bf16[32,2,16,128]{3,2,1,0:T(8,128)(2,1)S(1)}, bf16[32,2,16,128]{3,2,1,0:T(8,128)(2,1)}, u32[]{:S(2)}) copy-start(bf16[32,2,16,128]{3,2,1,0:T(8,128)(2,1)} %param.17) | copy-start | bytes 786436
  5.7 1.4 %copy-start.5 = (bf16[32,2,16,128]{3,2,1,0:T(8,128)(2,1)S(1)}, bf16[32,2,16,128]{3,2,1,0:T(8,128)(2,1)}, u32[]{:S(2)}) copy-start(bf16[32,2,16,128]{3,2,1,0:T(8,128)(2,1)} %param.10) | copy-start | bytes 786436
  95.0 4.9 %copy-start.3 = (f32[128,4,128]{2,1,0:T(4,128)S(1)}, f32[128,4,128]{2,1,0:T(4,128)}, u32[]{:S(2)}) copy-start(f32[128,4,128]{2,1,0:T(4,128)} %get-tuple-element.11) | copy-start | bytes 786436

commit v4 on v3

--- a/solution.py
+++ b/solution.py
@@ -150,8 +150,9 @@
 
 def kernel(
     voxels,
-    x_a, x_b, grad, weights, params,
-    y_out, dx_out, gw_out, norm_out,
+    x_a, x_b, grad, w_first, w_second, gain_first, bias_first, gain_second, bias_second,
+    y_out, dx_out, gw_first, gw_second, norm_out,
+    block_a, block_b, block_g, block_y, block_dx, kernel_1, kernel_2, weights, stage,
     taps_x, taps_h, taps_d2, taps_d1,
     rows_x, rows_g, rows_1, rows_2, rows_e,
     near_x, near_g, near_1, near_2, near_e,
@@ -164,8 +165,17 @@
     conv_1, conv_2, back_1,
     sums,
     norms, slopes, early_out, early_in, late_out, late_in, gathered, pairs,
-    halo_send, halo_recv, sums_send, sums_recv, gw_send, gw_recv,
+    halo_send, halo_recv, sums_send, sums_recv, gw_send, gw_recv, local,
 ):
+    loads = [
+        pltpu.make_async_copy(source, target, local.at[index])
+        for index, (source, target) in enumerate((
+            (x_a, block_a), (x_b, block_b), (grad, block_g), (w_first, kernel_1),
+            (w_second, kernel_2),
+        ))
+    ]
+    for load in loads:
+        load.start()
     place = {axis: (lax.axis_index(axis), lax.axis_size(axis)) for axis in AXES}
     for near in (near_x, near_g, near_1, near_2, near_e):
         near[...] = jnp.zeros_like(near)
@@ -419,21 +429,57 @@
         halo.arrive(phase)
         return halo.columns_x(lane)
 
-    gain_1, bias_1, gain_2, bias_2 = (params[:, k : k + 1] for k in range(4))
+    small_lane = lax.broadcasted_iota(jnp.int32, (C, C), 1)
+    small_row = lax.broadcasted_iota(jnp.int32, (C, C), 0)
+
+    def column(row):
+        return jnp.sum(jnp.where(small_lane == small_row, row[...], 0.0), axis=1, keepdims=True)
+
+    gain_1, bias_1, gain_2, bias_2 = (
+        column(row) for row in (gain_first, bias_first, gain_second, bias_second)
+    )
+
+    def stack_weights(source, forward, backward):
+        tiles = [
+            jnp.concatenate(
+                [source[tap].astype(F32) for tap in range(4 * k, min(4 * k + 4, 27))]
+                + ([jnp.zeros((C, C), F32)] if k == 6 else []),
+                axis=1,
+            )
+            for k in range(7)
+        ]
+        turned = [tile.T for tile in tiles]
+        pieces = [turned[tap // 4][C * (tap % 4) : C * (tap % 4) + C] for tap in range(26, -1, -1)]
+        back = [jnp.concatenate((pieces + pieces[:1])[4 * k : 4 * k + 4], axis=1) for k in range(7)]
+        for index, parts in ((forward, tiles), (backward, back)):
+            last = jnp.where(lane < 96, parts[6], 0.0)
+            empty = jnp.zeros((C, LANES), F32)
+            top = parts[:6] + [last, empty, empty]
+            moved = [pltpu.roll(part, 32, 1) for part in parts[:6] + [last]]
+            low = [empty, empty]
+            for k in range(7):
+                low.append(jnp.where(lane < 32, moved[k - 1] if k else empty, moved[k]))
+            for k in range(9):
+                weights[index, 0:C, LANES * k : LANES * (k + 1)] = top[k].astype(BF16)
+                weights[index, C : 2 * C, LANES * k : LANES * (k + 1)] = low[k].astype(BF16)
 
     zero = jnp.zeros((C, LANES), F32)
-    for source, rows, edge, at in (
-        (x_a, rows_x, edge_x, 0), (x_b, rows_x, edge_x, 1), (grad, rows_g, edge_g, 0)
-    ):
+
+    def take(load, source, rows, edge, at):
+        load.wait()
         for at_x in range(SPAN_X):
-
-            def step(block, carry, source=source, rows=rows, at_x=at_x, at=at):
+            rows[at, at_x + 1, 1 : SPAN_Y + 1] = jnp.swapaxes(
+                source[:, at_x].astype(F32), 0, 1
+            ).astype(BF16)
+        for at_x in range(SPAN_X):
+
+            def step(block, carry, at_x=at_x):
                 for k in range(8):
                     at_y = block * 8 + k
-                    row = source[at_x, at_y]
-                    rows[at, at_x + 1, at_y + 1] = row
                     carry = extract(
-                        row.astype(F32), (at_x + 1) * 32 + at_y + 1, carry
+                        rows[at, at_x + 1, at_y + 1].astype(F32),
+                        (at_x + 1) * 32 + at_y + 1,
+                        carry,
                     )
                 return carry
 
@@ -441,11 +487,19 @@
         edge[0, at] = carry[0].astype(BF16)
         edge[1, at] = carry[1].astype(BF16)
 
+    take(loads[0], block_a, rows_x, edge_x, 0)
+    take(loads[1], block_b, rows_x, edge_x, 1)
+
     pl.semaphore_wait(barrier, count - 1)
 
     phase = halo_x.columns_z() + halo_x.faces_y()
     waits_x = [halo_x.faces_x(0)]
+    loads[3].wait()
+    loads[4].wait()
+    stack_weights(kernel_1, 0, 3)
+    stack_weights(kernel_2, 1, 2)
     phase, corners = second(halo_x, phase)
+    take(loads[2], block_g, rows_g, edge_g, 0)
     last = third(halo_x, phase)
     waits_x.append(halo_x.faces_x(1))
     halo_x.arrive(corners)
@@ -630,10 +684,13 @@
             for k in range(8):
                 at_y = block * 8 + k
                 pre = conv_2[0, at_x, at_y] * slope_a + shift_a
-                y_out[at_x, at_y] = (pre * sigmoid(pre)).astype(BF16)
+                stage[at_x, at_y] = pre * sigmoid(pre)
             return carry
 
         lax.fori_loop(0, 2, step, 0)
+        block_y[:, at_x] = jnp.swapaxes(stage[at_x], 0, 1).astype(BF16)
+    store_y = pltpu.make_async_copy(block_y, y_out, local.at[5])
+    store_y.start()
 
     last = third(halo_2, phase)
     halo_g.arrive(waits_g + corners_g + last_g)
@@ -698,10 +755,10 @@
         (side_e.at[0, 0], side_e.at[0, 1]),
     )
     whole = 1.0 / math.sqrt(voxels)
-    for k, column in enumerate(
+    for k, factor in enumerate(
         (gain_1 * scale_1 * whole, sum_d1 / voxels, sum_x1 / voxels)
     ):
-        tile = jnp.broadcast_to(column, (C, LANES))
+        tile = jnp.broadcast_to(factor, (C, LANES))
         for pair in range(16):
             pairs[k, pair] = tile[2 * pair : 2 * pair + 2]
     fan_in(early_in, gw_recv.at[0])
@@ -717,18 +774,34 @@
     fan_out(lambda to: mine, mine, gw_send.at[2], gw_recv.at[2])
 
     def emit(at_x, at_y, tile, carry):
-        dx_out[at_x, at_y] = tile.astype(BF16)
+        stage[at_x, at_y] = tile
         return carry
 
     convolve(taps_d1, 0, 3, emit, 0)
-
-    tile = jnp.zeros((C, LANES), F32)
-    for k, column in enumerate((sum_x1, sum_d1, sum_x2, sum_d2)):
-        tile = tile + jnp.where(lane == k, column, 0.0)
-    norm_out[...] = tile * whole
+    for at_x in range(SPAN_X):
+        block_dx[:, at_x] = jnp.swapaxes(stage[at_x], 0, 1).astype(BF16)
+    store_dx = pltpu.make_async_copy(block_dx, dx_out, local.at[6])
+    store_dx.start()
+
+    for k, total in enumerate((sum_x1, sum_d1, sum_x2, sum_d2)):
+        norm_out[k : k + 1] = whole * jnp.sum(
+            jnp.where(small_lane == small_row, total, 0.0), axis=0, keepdims=True
+        )
     fan_in(gathered, gw_recv.at[2])
-    gw_out[...] = gathered[...]
-
+    for member, out in ((0, gw_first), (1, gw_second)):
+        for k in range(7):
+            tile = jnp.concatenate(
+                [
+                    gathered[(pair // 4 * 8 + k) * 4 + pair % 4, 2 * member : 2 * member + 2]
+                    for pair in range(16)
+                ],
+                axis=0,
+            )
+            for tap in range(4 * k, min(4 * k + 4, 27)):
+                out[tap] = tile[:, C * (tap % 4) : C * (tap % 4) + C]
+
+    store_y.wait()
+    store_dx.wait()
     for halo in halos:
         halo.drain()
     for total in totals:
@@ -737,34 +810,19 @@
         fan_in(chunks, gw_send.at[k])
 
 
-def stacked(weight):
-    flat = weight.transpose(3, 0, 1, 2, 4).reshape(C, FLAT)
-    slab = 3 * TAPS
-    return jnp.concatenate(
-        [jnp.pad(flat, ((0, 0), (0, slab))), jnp.pad(flat, ((0, 0), (slab, 0)))], axis=0
-    )
-
-
-def flipped(weight):
-    return jnp.flip(weight, (0, 1, 2)).transpose(0, 1, 2, 4, 3)
-
-
 def body(voxels, x_a, x_b, w_first, w_second, gain_first, bias_first, gain_second, bias_second,
          grad_out):
-    weights = jnp.stack(
-        [stacked(w_first), stacked(w_second), stacked(flipped(w_second)), stacked(flipped(w_first))]
-    )
-    params = jnp.stack([gain_first, bias_first, gain_second, bias_second], axis=1)
-
-    def by_rows(block):
-        return block.transpose(1, 2, 0, 3)
-
     def sized(*shape, kind=BF16):
         return pltpu.VMEM(shape, kind)
 
     volumes = (2, 1, 2, 1, 1)
     devices = math.prod(lax.axis_size(axis) for axis in AXES)
-    scratch = [sized(count, PAD_X, PAD_Y, TAPS, LANES) for count in (2, 2, 1, 1)]
+    block = (C, SPAN_X, SPAN_Y, LANES)
+    scratch = [sized(*block)] * 5 + [sized(27, C, C)] * 2
+    scratch += [
+        sized(4, SPAN_X * C, DEPTH), sized(SPAN_X, SPAN_Y, C, LANES, kind=F32)
+    ]
+    scratch += [sized(count, PAD_X, PAD_Y, TAPS, LANES) for count in (2, 2, 1, 1)]
     scratch += [sized(count, PAD_X, PAD_Y, C, LANES) for count in volumes]
     scratch += [sized(2, count, C, LANES) for count in volumes]
     scratch += [sized(2, 2, count, C, LANES) for count in volumes]
@@ -792,30 +850,33 @@
         pltpu.SemaphoreType.DMA((4,)),
         pltpu.SemaphoreType.DMA((3,)),
         pltpu.SemaphoreType.DMA((3,)),
+        pltpu.SemaphoreType.DMA((7,)),
     ]
     in_vmem = pl.BlockSpec(memory_space=pltpu.VMEM)
-    y_a, dx_b, kernels, norms = pl.pallas_call(
+    anywhere = pl.BlockSpec(memory_space=pl.ANY)
+    taps = jax.ShapeDtypeStruct((27, C, C), F32)
+    y_a, dx_b, grad_first, grad_second, norms = pl.pallas_call(
         functools.partial(kernel, voxels),
         out_shape=(
-            jax.ShapeDtypeStruct((SPAN_X, SPAN_Y, C, LANES), BF16),
-            jax.ShapeDtypeStruct((SPAN_X, SPAN_Y, C, LANES), BF16),
-            jax.ShapeDtypeStruct((devices, 4, LANES), F32),
-            jax.ShapeDtypeStruct((C, LANES), F32),
+            jax.ShapeDtypeStruct(block, BF16),
+            jax.ShapeDtypeStruct(block, BF16),
+            taps,
+            taps,
+            jax.ShapeDtypeStruct((4, C), F32),
         ),
-        in_specs=[in_vmem] * 5,
-        out_specs=(in_vmem,) * 4,
+        in_specs=[anywhere] * 5 + [in_vmem] * 4,
+        out_specs=(anywhere,) * 2 + (in_vmem,) * 3,
         scratch_shapes=scratch,
         compiler_params=pltpu.CompilerParams(
             collective_id=0, has_side_effects=True, vmem_limit_bytes=60 * 1024 * 1024
         ),
-    )(by_rows(x_a), by_rows(x_b), by_rows(grad_out), weights, params)
-
-    def by_channels(block):
-        return block.transpose(2, 0, 1, 3)
-
-    kernels = kernels.reshape(4, 8, 4, 2, 2, LANES).transpose(3, 0, 2, 4, 1, 5)
-    grads = kernels.reshape(2, C, 8 * LANES)[:, :, :FLAT].reshape(2, C, 3, 3, 3, C).transpose(0, 2, 3, 4, 1, 5)
-    return (by_channels(y_a), by_channels(dx_b), grads[0], grads[1], norms[:, :4].T)
+    )(
+        x_a, x_b, grad_out, w_first.reshape(27, C, C), w_second.reshape(27, C, C),
+        *(row.reshape(1, C) for row in (gain_first, bias_first, gain_second, bias_second)),
+    )
+    return (
+        y_a, dx_b, grad_first.reshape(3, 3, 3, C, C), grad_second.reshape(3, 3, 3, C, C), norms
+    )
 
 
 def solution(mesh):

time: 103 us -> 92.4 us (0.90)
  local copies, waits for them, and re-layouts: 13 us -> 4.96 us
  other arithmetic: 1.87 us -> 0 us
    transpose x4 -> x0, local copies, waits for them, and re-layouts: 2.02 us -> none  [the longest x1 0.99 us: by_rows(): return block.transpose(1, 2, 0, 3)]
    rev x2 -> x0, local copies, waits for them, and re-layouts: 1.98 us -> none  [flipped(): return jnp.flip(weight, (0, 1, 2)).transpose(0, 1, 2, 4, 3)]
    another operation x4 -> x0, other arithmetic: 1.87 us -> none  [the longest x3 1.11 us: body(): jnp.stack([stacked(w_first), stacked(w_second), stacked(flipped(w_second)...]
    unnamed x18 -> x13, local copies, waits for them, and re-layouts: 6.68 us -> 4.96 us
    reshape x7 -> x0, local copies, waits for them, and re-layouts: 1.36 us -> none  [the longest x4 0.64 us: stacked(): flat = weight.transpose(3, 0, 1, 2, 4).reshape(C, FLAT)]
where the time goes in v4:
time: 92.4 us; the launch traced here: 92.2 us
  Pallas kernels  86.5 us (94%)
  local copies, waits for them, and re-layouts  4.96 us (5%)
    pallas_call x1, Pallas kernels, body(): pl.pallas_call(functools.partial(kernel, voxels), out_shape=(jax.ShapeDty...  86.5 us
    unnamed x13, local copies, waits for them, and re-layouts  4.96 us

profile of v4, /device:TPU:1, one launch (start us, length us, event | category | flops | bytes accessed | tf_op | source)
XLA Modules:
  0.0 92.2 jit_solution(10032705964249188997)
XLA Ops:
  0.6 86.5 %shard_map.128 = (bf16[32,2,16,128]{3,2,1,0:T(8,128)(2,1)}, bf16[32,2,16,128]{3,2,1,0:T(8,128)(2,1)}, f32[27,32,32]{2,1,0:T(8,128)}, f32[27,32,32]{2,1,0:T(8,128)}, f32[4,32]{1,0:T(4,128)}) custom-call(bf16[32,2,16,128]{3,2,1,0:T(8,128)(2,1)} %x_a.1, bf16[32,2,16,128]{3,2,1,0:T(8,128)(2,1)} %x_b.1, bf16[32,2,16,128]{3,2,1,0:T(8,128)(2,1)} %grad.1, ...), custom_call_target="tpu_custom_call" | custom-call | tf_op jit(solution)/shard_map/pallas_call | solution.py:858
  87.2 0.0 copy-start.2
  87.2 0.0 copy-start.1
  87.2 1.7 %copy.19 = bf16[32,2,16,128]{3,2,1,0:T(8,128)(2,1)} copy(bf16[32,2,16,128]{3,2,1,0:T(8,128)(2,1)} %get-tuple-element.20) | data formatting | bytes 524288
  88.9 0.0 copy-done.2
  88.9 0.7 copy.20
  89.6 0.0 copy-done.1
  89.6 0.0 copy-start
  89.6 0.8 copy.21
  90.4 0.4 copy-done
  90.8 0.0 copy-start.3
  90.8 0.8 copy.22
  91.6 0.0 copy-done.3
  91.6 0.6 copy.23
Async XLA Ops:
  87.2 1.8 %copy-start.2 = (bf16[32,2,16,128]{3,2,1,0:T(8,128)(2,1)S(1)}, bf16[32,2,16,128]{3,2,1,0:T(8,128)(2,1)}, u32[]{:S(2)}) copy-start(bf16[32,2,16,128]{3,2,1,0:T(8,128)(2,1)} %get-tuple-element.21) | copy-start | bytes 786436
  87.2 2.5 %copy-start.1 = (f32[27,32,32]{2,1,0:T(8,128)S(1)}, f32[27,32,32]{2,1,0:T(8,128)}, u32[]{:S(2)}) copy-start(f32[27,32,32]{2,1,0:T(8,128)} %get-tuple-element.12) | copy-start | bytes 331780
  89.6 1.2 %copy-start = (f32[27,32,32]{2,1,0:T(8,128)S(1)}, f32[27,32,32]{2,1,0:T(8,128)}, u32[]{:S(2)}) copy-start(f32[27,32,32]{2,1,0:T(8,128)} %get-tuple-element.13) | copy-start | bytes 331780
  90.8 0.8 copy-start.3

commit v5 on v4

--- a/solution.py
+++ b/solution.py
@@ -152,7 +152,7 @@
     voxels,
     x_a, x_b, grad, w_first, w_second, gain_first, bias_first, gain_second, bias_second,
     y_out, dx_out, gw_first, gw_second, norm_out,
-    block_a, block_b, block_g, block_y, block_dx, kernel_1, kernel_2, weights, stage,
+    block_a, block_b, block_g, kernel_1, kernel_2, row_1, row_2, row_3, row_4, weights, stage,
     taps_x, taps_h, taps_d2, taps_d1,
     rows_x, rows_g, rows_1, rows_2, rows_e,
     near_x, near_g, near_1, near_2, near_e,
@@ -171,7 +171,8 @@
         pltpu.make_async_copy(source, target, local.at[index])
         for index, (source, target) in enumerate((
             (x_a, block_a), (x_b, block_b), (grad, block_g), (w_first, kernel_1),
-            (w_second, kernel_2),
+            (w_second, kernel_2), (gain_first, row_1), (bias_first, row_2), (gain_second, row_3),
+            (bias_second, row_4),
         ))
     ]
     for load in loads:
@@ -435,9 +436,9 @@
     def column(row):
         return jnp.sum(jnp.where(small_lane == small_row, row[...], 0.0), axis=1, keepdims=True)
 
-    gain_1, bias_1, gain_2, bias_2 = (
-        column(row) for row in (gain_first, bias_first, gain_second, bias_second)
-    )
+    for load in loads[5:]:
+        load.wait()
+    gain_1, bias_1, gain_2, bias_2 = (column(row) for row in (row_1, row_2, row_3, row_4))
 
     def stack_weights(source, forward, backward):
         tiles = [
@@ -688,9 +689,7 @@
             return carry
 
         lax.fori_loop(0, 2, step, 0)
-        block_y[:, at_x] = jnp.swapaxes(stage[at_x], 0, 1).astype(BF16)
-    store_y = pltpu.make_async_copy(block_y, y_out, local.at[5])
-    store_y.start()
+        y_out[:, at_x] = jnp.swapaxes(stage[at_x], 0, 1).astype(BF16)
 
     last = third(halo_2, phase)
     halo_g.arrive(waits_g + corners_g + last_g)
@@ -779,9 +778,7 @@
 
     convolve(taps_d1, 0, 3, emit, 0)
     for at_x in range(SPAN_X):
-        block_dx[:, at_x] = jnp.swapaxes(stage[at_x], 0, 1).astype(BF16)
-    store_dx = pltpu.make_async_copy(block_dx, dx_out, local.at[6])
-    store_dx.start()
+        dx_out[:, at_x] = jnp.swapaxes(stage[at_x], 0, 1).astype(BF16)
 
     for k, total in enumerate((sum_x1, sum_d1, sum_x2, sum_d2)):
         norm_out[k : k + 1] = whole * jnp.sum(
@@ -800,8 +797,6 @@
             for tap in range(4 * k, min(4 * k + 4, 27)):
                 out[tap] = tile[:, C * (tap % 4) : C * (tap % 4) + C]
 
-    store_y.wait()
-    store_dx.wait()
     for halo in halos:
         halo.drain()
     for total in totals:
@@ -810,6 +805,18 @@
         fan_in(chunks, gw_send.at[k])
 
 
+def write_out(*refs):
+    sources, targets, semaphores = refs[:5], refs[5:10], refs[10]
+    copies = [
+        pltpu.make_async_copy(source, target, semaphores.at[index])
+        for index, (source, target) in enumerate(zip(sources, targets))
+    ]
+    for copy in copies:
+        copy.start()
+    for copy in copies:
+        copy.wait()
+
+
 def body(voxels, x_a, x_b, w_first, w_second, gain_first, bias_first, gain_second, bias_second,
          grad_out):
     def sized(*shape, kind=BF16):
@@ -818,7 +825,7 @@
     volumes = (2, 1, 2, 1, 1)
     devices = math.prod(lax.axis_size(axis) for axis in AXES)
     block = (C, SPAN_X, SPAN_Y, LANES)
-    scratch = [sized(*block)] * 5 + [sized(27, C, C)] * 2
+    scratch = [sized(*block)] * 3 + [sized(27, C, C)] * 2 + [sized(1, C, kind=F32)] * 4
     scratch += [
         sized(4, SPAN_X * C, DEPTH), sized(SPAN_X, SPAN_Y, C, LANES, kind=F32)
     ]
@@ -850,30 +857,41 @@
         pltpu.SemaphoreType.DMA((4,)),
         pltpu.SemaphoreType.DMA((3,)),
         pltpu.SemaphoreType.DMA((3,)),
-        pltpu.SemaphoreType.DMA((7,)),
+        pltpu.SemaphoreType.DMA((9,)),
     ]
     in_vmem = pl.BlockSpec(memory_space=pltpu.VMEM)
-    anywhere = pl.BlockSpec(memory_space=pl.ANY)
+    in_hbm = pl.BlockSpec(memory_space=pltpu.HBM)
     taps = jax.ShapeDtypeStruct((27, C, C), F32)
-    y_a, dx_b, grad_first, grad_second, norms = pl.pallas_call(
+    out_shape = (
+        jax.ShapeDtypeStruct(block, BF16),
+        jax.ShapeDtypeStruct(block, BF16),
+        taps,
+        taps,
+        jax.ShapeDtypeStruct((4, C), F32),
+    )
+    results = pl.pallas_call(
         functools.partial(kernel, voxels),
-        out_shape=(
-            jax.ShapeDtypeStruct(block, BF16),
-            jax.ShapeDtypeStruct(block, BF16),
-            taps,
-            taps,
-            jax.ShapeDtypeStruct((4, C), F32),
-        ),
-        in_specs=[anywhere] * 5 + [in_vmem] * 4,
-        out_specs=(anywhere,) * 2 + (in_vmem,) * 3,
+        out_shape=out_shape,
+        in_specs=[in_hbm] * 9,
+        out_specs=(in_vmem,) * 5,
         scratch_shapes=scratch,
         compiler_params=pltpu.CompilerParams(
-            collective_id=0, has_side_effects=True, vmem_limit_bytes=60 * 1024 * 1024
+            collective_id=0, has_side_effects=True, vmem_limit_bytes=28 * 1024 * 1024
         ),
     )(
-        x_a, x_b, grad_out, w_first.reshape(27, C, C), w_second.reshape(27, C, C),
-        *(row.reshape(1, C) for row in (gain_first, bias_first, gain_second, bias_second)),
+        *(pltpu.with_memory_space_constraint(value, pltpu.HBM) for value in (
+            x_a, x_b, grad_out, w_first.reshape(27, C, C), w_second.reshape(27, C, C),
+            *(row.reshape(1, C) for row in (gain_first, bias_first, gain_second, bias_second)),
+        )),
     )
+    y_a, dx_b, grad_first, grad_second, norms = pl.pallas_call(
+        write_out,
+        out_shape=out_shape,
+        in_specs=[in_vmem] * 5,
+        out_specs=(in_hbm,) * 5,
+        scratch_shapes=[pltpu.SemaphoreType.DMA((5,))],
+        compiler_params=pltpu.CompilerParams(vmem_limit_bytes=8 * 1024 * 1024),
+    )(*results)
     return (
         y_a, dx_b, grad_first.reshape(3, 3, 3, C, C), grad_second.reshape(3, 3, 3, C, C), norms
     )

time: 92.4 us -> 86.9 us (0.940)
  local copies, waits for them, and re-layouts: 4.96 us -> 0 us
    unnamed x13 -> x0, local copies, waits for them, and re-layouts: 4.96 us -> none
    pallas_call x1 -> x2, Pallas kernels: 86.5 us -> 86.1 us  [the longest x1 85 us: body(): pl.pallas_call(functools.partial(kernel, voxels), out_shape=out_shape, in...]
where the time goes in v5:
time: 86.9 us; the launch traced here: 86.8 us
  Pallas kernels  86.1 us (99%)
    pallas_call x1, Pallas kernels, body(): pl.pallas_call(functools.partial(kernel, voxels), out_shape=out_shape, in...  85 us

profile of v5, /device:TPU:1, one launch (start us, length us, event | category | flops | bytes accessed | tf_op | source)
XLA Modules:
  0.0 86.8 jit_solution(16510241371399071670)
XLA Ops:
  0.6 85.0 %shard_map.128 = (bf16[32,2,16,128]{3,2,1,0:T(8,128)(2,1)S(1)}, bf16[32,2,16,128]{3,2,1,0:T(8,128)(2,1)S(1)}, f32[27,32,32]{2,1,0:T(8,128)S(1)}, f32[27,32,32]{2,1,0:T(8,128)S(1)}, f32[4,32]{1,0:T(4,128)S(1)}) custom-call(bf16[32,2,16,128]{3,2,1,0:T(8,128)(2,1)} %x_a.1, bf16[32,2,16,128]{3,2,1,0:T(8,128)(2,1)} %x_b.1, bf16[32,2,16,128]{3,2,1,0:T(8,128)(2,1)} %grad.1, ...), custom_call_target="tpu_custom_call" | custom-call | tf_op jit(solution)/shard_map/pallas_call | solution.py:872
  85.6 1.1 %shard_map.129 = (bf16[32,2,16,128]{3,2,1,0:T(8,128)(2,1)}, bf16[32,2,16,128]{3,2,1,0:T(8,128)(2,1)}, f32[27,32,32]{2,1,0:T(8,128)}, f32[27,32,32]{2,1,0:T(8,128)}, f32[4,32]{1,0:T(4,128)}) custom-call(bf16[32,2,16,128]{3,2,1,0:T(8,128)(2,1)S(1)} %get-tuple-element.15.refs_0_, bf16[32,2,16,128]{3,2,1,0:T(8,128)(2,1)S(1)} %get-tuple-element.16.refs_1_, ...), custom_call_target="tpu_custom_call" | custom-call | tf_op jit(solution)/shard_map/pallas_call | solution.py:887

commit v6 on v5

--- a/solution.py
+++ b/solution.py
@@ -33,104 +33,109 @@
 
 
 class Halo:
-    def __init__(
-        self, rows, near, far_y, turn, far_x, edge, side, send, recv, place, volumes
-    ):
-        self.rows, self.near, self.far_y, self.turn, self.far_x = rows, near, far_y, turn, far_x
-        self.side = side
-        self.edge, self.send, self.recv, self.place, self.volumes = edge, send, recv, place, volumes
+    def __init__(self, rows, cols, edge, side, send, recv, place, volumes):
+        self.rows, self.cols, self.edge, self.side = rows, cols, edge, side
+        self.send, self.recv, self.place, self.volumes = send, recv, place, volumes
         self.count = 0
         self.sent = []
 
-    def has(self, axis, step):
-        me, size = self.place[axis]
-        return me > 0 if step < 0 else me < size - 1
-
-    def push(self, source, target, axis, step):
-        me, size = self.place[axis]
+    def has(self, steps):
+        present = None
+        for axis, step in zip(AXES, steps):
+            if step:
+                me, size = self.place[axis]
+                inside = me > 0 if step < 0 else me < size - 1
+                present = inside if present is None else jnp.logical_and(present, inside)
+        return present
+
+    def push(self, source, target, *steps):
         index = self.count
         self.count += 1
+        to = {}
+        for axis, step in zip(AXES, steps):
+            if step:
+                me, size = self.place[axis]
+                to[axis] = lax.rem(me + step + size, size)
         copy = pltpu.make_async_remote_copy(
             src_ref=source,
             dst_ref=target,
             send_sem=self.send.at[index],
             recv_sem=self.recv.at[index],
-            device_id={axis: lax.rem(me + step + size, size)},
+            device_id=to,
             device_id_type=MESH,
         )
-
-        @pl.when(self.has(axis, step))
+        present = self.has(steps)
+
+        @pl.when(present)
         def _():
             copy.start()
 
-        self.sent.append((copy, self.has(axis, step)))
-        return copy, self.has(axis, -step)
+        self.sent.append((copy, present))
+        return copy, self.has([-step for step in steps])
 
     def faces_x(self, volume):
-        rows = self.rows
-        inner = pl.ds(1, SPAN_Y)
-        down = self.push(
-            rows.at[volume, 1, inner], rows.at[volume, PAD_X - 1, inner], "gx", -1
-        )
-        up = self.push(rows.at[volume, SPAN_X, inner], rows.at[volume, 0, inner], "gx", 1)
-        return [down, up]
-
-    def faces_y(self):
-        rows, inner, every = self.rows, pl.ds(1, SPAN_X), pl.ds(0, self.volumes)
-        down = self.push(
-            rows.at[every, inner, 1], rows.at[every, inner, PAD_Y - 1], "gy", -1
-        )
-        up = self.push(rows.at[every, inner, SPAN_Y], rows.at[every, inner, 0], "gy", 1)
-        return [down, up]
-
-    def columns_z(self):
-        down = self.push(self.edge.at[0], self.near.at[1], "gz", -1)
-        up = self.push(self.edge.at[1], self.near.at[0], "gz", 1)
-        return [down, up]
-
-    def columns_y(self):
-        down = self.push(self.near, self.far_y.at[1], "gy", -1)
-        up = self.push(self.near, self.far_y.at[0], "gy", 1)
-        return [down, up]
-
-    def columns_x(self, lane):
+        rows, inner = self.rows, pl.ds(1, SPAN_Y)
+        return [
+            self.push(
+                rows.at[volume, 1 if step < 0 else SPAN_X, inner],
+                rows.at[volume, PAD_X - 1 if step < 0 else 0, inner],
+                step, 0, 0,
+            )
+            for step in (-1, 1)
+        ]
+
+    def columns(self, step_x, step_y):
+        return [
+            self.push(
+                self.edge.at[0 if step < 0 else 1],
+                self.cols.at[1 if step < 0 else 0, 1 - step_x, 1 - step_y],
+                step_x, step_y, step,
+            )
+            for step in (-1, 1)
+        ]
+
+    def small(self):
+        rows, every = self.rows, pl.ds(0, self.volumes)
+        near = self.columns(0, 0)
+        rest = []
+        for step_x in (-1, 0, 1):
+            at_x = (1 if step_x < 0 else SPAN_X) if step_x else pl.ds(1, SPAN_X)
+            to_x = (PAD_X - 1 if step_x < 0 else 0) if step_x else pl.ds(1, SPAN_X)
+            for step_y in (-1, 1):
+                rest.append(
+                    self.push(
+                        rows.at[every, at_x, 1 if step_y < 0 else SPAN_Y],
+                        rows.at[every, to_x, PAD_Y - 1 if step_y < 0 else 0],
+                        step_x, step_y, 0,
+                    )
+                )
+        for step_x, step_y in (
+            (-1, -1), (-1, 1), (1, -1), (1, 1), (-1, 0), (1, 0), (0, -1), (0, 1)
+        ):
+            rest += self.columns(step_x, step_y)
+        return near, rest
+
+    def own(self, side, volume, lane):
+        tile = self.cols[side, 1, 1].astype(F32)
+        at = 32 * volume
+        return jnp.where(lane < 64, rolled(tile, 33 - at), rolled(tile, 49 - at))
+
+    def merged(self, side, volume, lane):
+        at = 32 * volume
         inside = lax.rem(lane, 32)
-        down = jnp.zeros((C, LANES), F32)
-        up = jnp.zeros((C, LANES), F32)
-        for side in range(2):
-            for volume in range(self.volumes):
-                own = self.near[side, volume].astype(F32)
-                low = pltpu.roll(self.far_y[0, side, volume].astype(F32), LANES - 16, 1)
-                high = pltpu.roll(self.far_y[1, side, volume].astype(F32), 16, 1)
-                own = jnp.where(inside == 0, low, jnp.where(inside == PAD_Y - 1, high, own))
-                self.side[volume, side] = own
-                at = 32 * (side * self.volumes + volume)
-                here = lane // 32 == at // 32
-                down = jnp.where(here, rolled(own, at - 32), down)
-                up = jnp.where(here, rolled(own, at - 64), up)
-        self.turn[0] = down.astype(BF16)
-        self.turn[1] = up.astype(BF16)
-        down = self.push(self.turn.at[0], self.far_x.at[1], "gx", -1)
-        up = self.push(self.turn.at[1], self.far_x.at[0], "gx", 1)
-        return [down, up]
-
-    def corners_x(self):
-        rows, every = self.rows, pl.ds(0, self.volumes)
-        result = []
-        for at in (0, PAD_Y - 1):
-            result.append(
-                self.push(rows.at[every, 1, at], rows.at[every, PAD_X - 1, at], "gx", -1)
-            )
-            result.append(
-                self.push(rows.at[every, SPAN_X, at], rows.at[every, 0, at], "gx", 1)
-            )
-        return result
-
-    def merged(self, side, volume, lane):
-        at = 32 * (side * self.volumes + volume)
-        low = rolled(self.far_x[0].astype(F32), -at)
-        high = rolled(self.far_x[1].astype(F32), 96 - at)
-        return jnp.where(lane < 32, low, jnp.where(lane >= 96, high, self.side[volume, side]))
+
+        def strip(index, low, middle, high):
+            low, middle, high = (
+                rolled(self.cols[side, index, k].astype(F32), shift - at)
+                for k, shift in enumerate((low, middle, high))
+            )
+            return jnp.where(inside == 0, low, jnp.where(inside == PAD_Y - 1, high, middle))
+
+        return jnp.where(
+            lane < 64,
+            jnp.where(lane < 32, strip(0, -31, -15, 1), strip(1, 17, 33, 49)),
+            jnp.where(lane < 96, strip(1, 33, 49, 65), strip(2, 81, 97, 113)),
+        )
 
     @staticmethod
     def arrive(pushes):
@@ -154,13 +159,10 @@
     y_out, dx_out, gw_first, gw_second, norm_out,
     block_a, block_b, block_g, kernel_1, kernel_2, row_1, row_2, row_3, row_4, weights, stage,
     taps_x, taps_h, taps_d2, taps_d1,
-    rows_x, rows_g, rows_1, rows_2, rows_e,
-    near_x, near_g, near_1, near_2, near_e,
-    fary_x, fary_g, fary_1, fary_2, fary_e,
-    turn_x, turn_g, turn_1, turn_2, turn_e,
-    farx_x, farx_g, farx_1, farx_2, farx_e,
-    edge_x, edge_g, edge_1, edge_2, edge_e,
-    side_x, side_g, side_1, side_2, side_e,
+    rows_x, rows_1, rows_2, rows_e,
+    cols_x, cols_1, cols_2, cols_e,
+    edge_x, edge_1, edge_2, edge_e,
+    side_x, side_1, side_2, side_e,
     side_h,
     conv_1, conv_2, back_1,
     sums,
@@ -178,8 +180,6 @@
     for load in loads:
         load.start()
     place = {axis: (lax.axis_index(axis), lax.axis_size(axis)) for axis in AXES}
-    for near in (near_x, near_g, near_1, near_2, near_e):
-        near[...] = jnp.zeros_like(near)
     for chunks in (early_out, late_out):
         for j in range(4):
             chunks[32 * j + 28 : 32 * j + 32] = jnp.zeros((4, 4, LANES), F32)
@@ -235,18 +235,16 @@
 
     lane = lax.broadcasted_iota(jnp.int32, (C, LANES), 1)
     halos = []
-    for index, (rows, near, fary, turn, farx, edge, side, volumes) in enumerate((
-        (rows_x, near_x, fary_x, turn_x, farx_x, edge_x, side_x, 2),
-        (rows_g, near_g, fary_g, turn_g, farx_g, edge_g, side_g, 1),
-        (rows_1, near_1, fary_1, turn_1, farx_1, edge_1, side_1, 2),
-        (rows_2, near_2, fary_2, turn_2, farx_2, edge_2, side_2, 1),
-        (rows_e, near_e, fary_e, turn_e, farx_e, edge_e, side_e, 1),
+    for index, (rows, cols, edge, side, volumes) in enumerate((
+        (rows_x, cols_x, edge_x, side_x, 3),
+        (rows_1, cols_1, edge_1, side_1, 2),
+        (rows_2, cols_2, edge_2, side_2, 1),
+        (rows_e, cols_e, edge_e, side_e, 1),
     )):
         halos.append(
-            Halo(rows, near, fary, turn, farx, edge, side, halo_send.at[index],
-                 halo_recv.at[index], place, volumes)
-        )
-    halo_x, halo_g, halo_1, halo_2, halo_e = halos
+            Halo(rows, cols, edge, side, halo_send.at[index], halo_recv.at[index], place, volumes)
+        )
+    halo_x, halo_1, halo_2, halo_e = halos
 
     low_x, high_x = place["gx"][0] > 0, place["gx"][0] < place["gx"][1] - 1
     low_y, high_y = place["gy"][0] > 0, place["gy"][0] < place["gy"][1] - 1
@@ -298,14 +296,8 @@
         taps[volume, at_x, at_y, C : 2 * C] = tile.astype(BF16)
         taps[volume, at_x, at_y, 2 * C : 3 * C] = right.astype(BF16)
 
-    def build(taps, volume, outer, inner, sides):
+    def build_inner(taps, volume, inner, sides):
         low, high = sides
-        zero = jnp.zeros((C, LANES), F32)
-
-        def held(at_x, at_y):
-            tile = outer(at_x, at_y)
-            return jnp.where(keep(at_x, at_y), tile, zero)
-
         for at_x in (1, 2):
 
             def step(block, carry, at_x=at_x):
@@ -317,17 +309,30 @@
                 return carry
 
             lax.fori_loop(0, 2, step, 0)
+
+    def build_outer(taps, volume, outer, sides):
+        low, high = sides
+        zero = jnp.zeros((C, LANES), F32)
+
+        def put(at_x, at_y):
+            tile = jnp.where(keep(at_x, at_y), outer(at_x, at_y), zero)
+            put_taps(taps, volume, at_x, at_y, tile, low[...], high[...])
+
+        for at_x in (1, 2):
             for at_y in (0, PAD_Y - 1):
-                put_taps(taps, volume, at_x, at_y, held(at_x, at_y), low[...], high[...])
+                put(at_x, at_y)
         for at_x in (0, PAD_X - 1):
 
             def step(block, carry, at_x=at_x):
                 for k in range(6):
-                    at_y = block * 6 + k
-                    put_taps(taps, volume, at_x, at_y, held(at_x, at_y), low[...], high[...])
+                    put(at_x, block * 6 + k)
                 return carry
 
             lax.fori_loop(0, 3, step, 0)
+
+    def build(taps, volume, outer, inner, sides):
+        build_inner(taps, volume, inner, sides)
+        build_outer(taps, volume, outer, sides)
 
     def convolve(taps, volume, weight, emit, carry):
         def step(block, carry):
@@ -421,14 +426,6 @@
             fan_in(self.slots, sums_send.at[self.index])
 
     totals = [Total(index) for index in range(4)]
-
-    def second(halo, phase):
-        halo.arrive(phase)
-        return halo.columns_y(), halo.corners_x()
-
-    def third(halo, phase):
-        halo.arrive(phase)
-        return halo.columns_x(lane)
 
     small_lane = lax.broadcasted_iota(jnp.int32, (C, C), 1)
     small_row = lax.broadcasted_iota(jnp.int32, (C, C), 0)
@@ -466,10 +463,10 @@
 
     zero = jnp.zeros((C, LANES), F32)
 
-    def take(load, source, rows, edge, at):
+    def take(load, source, at, carry):
         load.wait()
         for at_x in range(SPAN_X):
-            rows[at, at_x + 1, 1 : SPAN_Y + 1] = jnp.swapaxes(
+            rows_x[at, at_x + 1, 1 : SPAN_Y + 1] = jnp.swapaxes(
                 source[:, at_x].astype(F32), 0, 1
             ).astype(BF16)
         for at_x in range(SPAN_X):
@@ -478,79 +475,77 @@
                 for k in range(8):
                     at_y = block * 8 + k
                     carry = extract(
-                        rows[at, at_x + 1, at_y + 1].astype(F32),
-                        (at_x + 1) * 32 + at_y + 1,
+                        rows_x[at, at_x + 1, at_y + 1].astype(F32),
+                        32 * at + 16 * at_x + at_y,
                         carry,
                     )
                 return carry
 
-            carry = lax.fori_loop(0, 2, step, (zero, zero) if at_x == 0 else carry)
-        edge[0, at] = carry[0].astype(BF16)
-        edge[1, at] = carry[1].astype(BF16)
-
-    take(loads[0], block_a, rows_x, edge_x, 0)
-    take(loads[1], block_b, rows_x, edge_x, 1)
+            carry = lax.fori_loop(0, 2, step, carry)
+        return carry
+
+    carry = (zero, zero)
+    for at, source in enumerate((block_a, block_b, block_g)):
+        carry = take(loads[at], source, at, carry)
+    edge_x[0] = carry[0].astype(BF16)
+    edge_x[1] = carry[1].astype(BF16)
 
     pl.semaphore_wait(barrier, count - 1)
 
-    phase = halo_x.columns_z() + halo_x.faces_y()
-    waits_x = [halo_x.faces_x(0)]
+    near, rest = halo_x.small()
+    waits_x = [halo_x.faces_x(0), halo_x.faces_x(1)]
     loads[3].wait()
     loads[4].wait()
     stack_weights(kernel_1, 0, 3)
     stack_weights(kernel_2, 1, 2)
-    phase, corners = second(halo_x, phase)
-    take(loads[2], block_g, rows_g, edge_g, 0)
-    last = third(halo_x, phase)
-    waits_x.append(halo_x.faces_x(1))
-    halo_x.arrive(corners)
-    halo_x.arrive(last)
     ok = [lane_keep(side) for side in range(2)]
+    halo_x.arrive(near)
+    for volume in range(2):
+        for side in range(2):
+            side_x[volume, side] = jnp.where(ok[side], halo_x.own(side, volume, lane), 0.0)
+        build_inner(
+            taps_x, volume,
+            lambda at_x, at_y, volume=volume: rows_x[volume, at_x + 1, at_y + 1].astype(F32),
+            (side_x.at[volume, 0], side_x.at[volume, 1]),
+        )
+    halo_x.arrive(rest)
     for side in range(2):
-        for volume in range(2):
+        for volume in range(3):
             tile = halo_x.merged(side, volume, lane)
             side_x[volume, side] = jnp.where(ok[side], tile, 0.0)
 
-    def stats_emit(keep_f32, halo, volume):
-        def emit(at_x, at_y, tile, carry):
-            total, squares, first, last = carry
-            keep_f32[volume, at_x, at_y] = tile
-            halo.rows[halo_of[volume], at_x + 1, at_y + 1] = tile.astype(BF16)
-            first, last = extract(tile, (at_x + 1) * 32 + at_y + 1, (first, last))
-            return total + tile, squares + tile * tile, first, last
-
-        halo_of = {0: 0, 1: 1}
-        return emit
-
     columns = []
-    waits = []
+    waits_1 = []
+    carry = (zero,) * 2
     for volume in range(2):
         halo_x.arrive(waits_x[volume])
-        build(
+        build_outer(
             taps_x, volume,
             lambda at_x, at_y, volume=volume: rows_x[volume, at_x, at_y].astype(F32),
-            lambda at_x, at_y, volume=volume: rows_x[volume, at_x + 1, at_y + 1].astype(F32),
             (side_x.at[volume, 0], side_x.at[volume, 1]),
         )
-        total, squares, first, last = convolve(
-            taps_x, volume, 0, stats_emit(conv_1, halo_1, volume), (zero,) * 4
-        )
-        edge_1[0, volume] = first.astype(BF16)
-        edge_1[1, volume] = last.astype(BF16)
+
+        def emit(at_x, at_y, tile, carry, volume=volume):
+            total, squares, first, last = carry
+            conv_1[volume, at_x, at_y] = tile
+            rows_1[volume, at_x + 1, at_y + 1] = tile.astype(BF16)
+            first, last = extract(tile, 32 * volume + 16 * at_x + at_y, (first, last))
+            return total + tile, squares + tile * tile, first, last
+
+        total, squares, *carry = convolve(taps_x, volume, 0, emit, (zero, zero, *carry))
         if volume == 0:
-            waits += halo_1.faces_x(volume)
+            waits_1.append(halo_1.faces_x(0))
         columns += [
             jnp.sum(total, axis=1, keepdims=True), jnp.sum(squares, axis=1, keepdims=True)
         ]
+    edge_1[0] = carry[0].astype(BF16)
+    edge_1[1] = carry[1].astype(BF16)
     totals[0].start(pack(columns))
-    phase = halo_1.columns_z() + halo_1.faces_y()
-    waits += halo_1.faces_x(1)
-    phase, corners = second(halo_1, phase)
-    last = third(halo_1, phase)
+    near, rest = halo_1.small()
+    waits_1.append(halo_1.faces_x(1))
     row = totals[0].finish()
-    halo_1.arrive(waits + corners + last)
-    phase_g = halo_g.columns_z() + halo_g.faces_y()
-    waits_g = halo_g.faces_x(0)
+    halo_1.arrive(near + rest)
+    waits_g = halo_x.faces_x(2)
     stats = unpack(row, 4)
 
     def moments(total, squares):
@@ -559,7 +554,6 @@
         return mean, scale
 
     columns = []
-    affine_1 = None
     for volume in range(2):
         mean, scale = moments(stats[2 * volume], stats[2 * volume + 1])
         slope = jnp.broadcast_to(gain_1 * scale, (C, LANES))
@@ -582,11 +576,15 @@
             tile = halo_1.merged(side, volume, lane)
             side_1[volume, side] = tile
             side_h[volume, side] = jnp.where(ok[side], active(tile), 0.0)
-        build(
+        sides = (side_h.at[volume, 0], side_h.at[volume, 1])
+        build_inner(
+            taps_h, volume, functools.partial(own_row, volume=volume, active=active), sides
+        )
+        halo_1.arrive(waits_1[volume])
+        build_outer(
             taps_h, volume,
             lambda at_x, at_y, volume=volume: active(rows_1[volume, at_x, at_y].astype(F32)),
-            functools.partial(own_row, volume=volume, active=active),
-            (side_h.at[volume, 0], side_h.at[volume, 1]),
+            sides,
         )
         if volume == 0:
 
@@ -596,27 +594,25 @@
                 return total + tile, squares + tile * tile
 
             total, squares = convolve(taps_h, 0, 1, emit, (zero,) * 2)
-            phase_g, corners_g = second(halo_g, phase_g)
         else:
 
             def emit(at_x, at_y, tile, carry):
                 total, squares, first, last = carry
                 conv_2[1, at_x, at_y] = tile
                 rows_2[0, at_x + 1, at_y + 1] = tile.astype(BF16)
-                first, last = extract(tile, (at_x + 1) * 32 + at_y + 1, (first, last))
+                first, last = extract(tile, 16 * at_x + at_y, (first, last))
                 return total + tile, squares + tile * tile, first, last
 
             total, squares, first, last = convolve(taps_h, 1, 1, emit, (zero,) * 4)
-            edge_2[0, 0] = first.astype(BF16)
-            edge_2[1, 0] = last.astype(BF16)
+            edge_2[0] = first.astype(BF16)
+            edge_2[1] = last.astype(BF16)
         columns += [
             jnp.sum(total, axis=1, keepdims=True), jnp.sum(squares, axis=1, keepdims=True)
         ]
     mean_1, scale_1 = mean, scale
     totals[1].start(pack(columns))
-    phase = halo_2.columns_z() + halo_2.faces_y()
-    waits = halo_2.faces_x(0)
-    last_g = third(halo_g, phase_g)
+    near, rest = halo_2.small()
+    waits = near + rest + halo_2.faces_x(0)
     kernel_grad(taps_x, 1, lambda at_x, at_y: norms[at_x, at_y], early_out, 0, plain=True)
     fan_out(
         lambda to: early_out.at[to], early_in.at[flat], gw_send.at[0], gw_recv.at[0]
@@ -671,10 +667,9 @@
     columns = sum_rows(
         slope_2,
         lambda at_x, at_y: conv_2[1, at_x, at_y],
-        lambda at_x, at_y: rows_g[0, at_x + 1, at_y + 1].astype(F32),
+        lambda at_x, at_y: rows_x[2, at_x + 1, at_y + 1].astype(F32),
     )
     totals[2].start(pack(columns))
-    phase, corners = second(halo_2, phase)
 
     mean_a, scale_a = moments(stats[0], stats[1])
     slope_a = jnp.broadcast_to(gain_2 * scale_a, (C, LANES))
@@ -691,22 +686,21 @@
         lax.fori_loop(0, 2, step, 0)
         y_out[:, at_x] = jnp.swapaxes(stage[at_x], 0, 1).astype(BF16)
 
-    last = third(halo_2, phase)
-    halo_g.arrive(waits_g + corners_g + last_g)
-    halo_2.arrive(waits + corners + last)
+    halo_x.arrive(waits_g)
+    halo_2.arrive(waits)
     sum_d2, sum_x2 = unpack(totals[2].finish(), 2)
 
     delta_2 = delta_of(slope_2, sum_d2, sum_x2, gain_2, scale_2)
     for side in range(2):
-        tile = delta_2(halo_2.merged(side, 0, lane), halo_g.merged(side, 0, lane))
+        tile = delta_2(halo_2.merged(side, 0, lane), side_x[2, side])
         side_2[0, side] = jnp.where(ok[side], tile, 0.0)
     build(
         taps_d2, 0,
         lambda at_x, at_y: delta_2(
-            rows_2[0, at_x, at_y].astype(F32), rows_g[0, at_x, at_y].astype(F32)
+            rows_2[0, at_x, at_y].astype(F32), rows_x[2, at_x, at_y].astype(F32)
         ),
         lambda at_x, at_y: delta_2(
-            conv_2[1, at_x, at_y], rows_g[0, at_x + 1, at_y + 1].astype(F32)
+            conv_2[1, at_x, at_y], rows_x[2, at_x + 1, at_y + 1].astype(F32)
         ),
         (side_2.at[0, 0], side_2.at[0, 1]),
     )
@@ -716,30 +710,28 @@
         total, weighted, first, last = carry
         back_1[at_x, at_y] = tile
         rows_e[0, at_x + 1, at_y + 1] = tile.astype(BF16)
-        first, last = extract(tile, (at_x + 1) * 32 + at_y + 1, (first, last))
+        first, last = extract(tile, 16 * at_x + at_y, (first, last))
         slope, normed = slope_1(conv_1[1, at_x, at_y], tile)
         slopes[at_x, at_y] = slope.astype(BF16)
         return total + slope, weighted + slope * normed, first, last
 
     total, weighted, first, last = convolve(taps_d2, 0, 2, emit, (zero,) * 4)
-    edge_e[0, 0] = first.astype(BF16)
-    edge_e[1, 0] = last.astype(BF16)
+    edge_e[0] = first.astype(BF16)
+    edge_e[1] = last.astype(BF16)
     columns = [
         jnp.sum(total, axis=1, keepdims=True), jnp.sum(weighted, axis=1, keepdims=True)
     ]
     totals[3].start(pack(columns))
-    phase = halo_e.columns_z() + halo_e.faces_y()
-    waits = halo_e.faces_x(0)
+    near, rest = halo_e.small()
+    waits = near + rest + halo_e.faces_x(0)
     kernel_grad(taps_x, 1, lambda at_x, at_y: slopes[at_x, at_y], late_out, 0)
-    phase, corners = second(halo_e, phase)
     kernel_grad(
         taps_h, 1, lambda at_x, at_y: taps_d2[0, at_x + 1, at_y + 1, C : 2 * C], late_out, 2
     )
-    last = third(halo_e, phase)
     fan_out(lambda to: late_out.at[to], late_in.at[flat], gw_send.at[1], gw_recv.at[1])
     late_in[flat] = late_out[flat]
     sum_d1, sum_x1 = unpack(totals[3].finish(), 2)
-    halo_e.arrive(waits + corners + last)
+    halo_e.arrive(waits)
 
     delta_1 = delta_of(slope_1, sum_d1, sum_x1, gain_1, scale_1)
     for side in range(2):
@@ -822,7 +814,7 @@
     def sized(*shape, kind=BF16):
         return pltpu.VMEM(shape, kind)
 
-    volumes = (2, 1, 2, 1, 1)
+    volumes = (3, 2, 1, 1)
     devices = math.prod(lax.axis_size(axis) for axis in AXES)
     block = (C, SPAN_X, SPAN_Y, LANES)
     scratch = [sized(*block)] * 3 + [sized(27, C, C)] * 2 + [sized(1, C, kind=F32)] * 4
@@ -831,11 +823,8 @@
     ]
     scratch += [sized(count, PAD_X, PAD_Y, TAPS, LANES) for count in (2, 2, 1, 1)]
     scratch += [sized(count, PAD_X, PAD_Y, C, LANES) for count in volumes]
-    scratch += [sized(2, count, C, LANES) for count in volumes]
-    scratch += [sized(2, 2, count, C, LANES) for count in volumes]
+    scratch += [sized(2, 3, 3, C, LANES) for count in volumes]
     scratch += [sized(2, C, LANES) for count in volumes]
-    scratch += [sized(2, C, LANES) for count in volumes]
-    scratch += [sized(2, count, C, LANES) for count in volumes]
     scratch += [sized(count, 2, C, LANES, kind=F32) for count in volumes]
     scratch += [sized(2, 2, C, LANES, kind=F32)]
     scratch += [
@@ -851,8 +840,8 @@
         sized(devices, 4, LANES, kind=F32),
         sized(devices, 4, LANES, kind=F32),
         sized(3, 16, 2, LANES, kind=F32),
-        pltpu.SemaphoreType.DMA((5, 24)),
-        pltpu.SemaphoreType.DMA((5, 24)),
+        pltpu.SemaphoreType.DMA((4, 32)),
+        pltpu.SemaphoreType.DMA((4, 32)),
         pltpu.SemaphoreType.DMA((4,)),
         pltpu.SemaphoreType.DMA((4,)),
         pltpu.SemaphoreType.DMA((3,)),

time: 86.9 us -> 77.5 us (0.89)
  Pallas kernels: 86.1 us -> 76.8 us
    pallas_call x1, Pallas kernels: 85 us -> 75.7 us  [body(): pl.pallas_call(functools.partial(kernel, voxels), out_shape=out_shape, in...]
where the time goes in v6:
time: 77.5 us; the launch traced here: 77.4 us
  Pallas kernels  76.8 us (99%)
    pallas_call x1, Pallas kernels, body(): pl.pallas_call(functools.partial(kernel, voxels), out_shape=out_shape, in...  75.7 us

profile of v6, /device:TPU:1, one launch (start us, length us, event | category | flops | bytes accessed | tf_op | source)
XLA Modules:
  0.0 77.4 jit_solution(13042456615308387444)
XLA Ops:
  0.6 75.7 %shard_map.128 = (bf16[32,2,16,128]{3,2,1,0:T(8,128)(2,1)S(1)}, bf16[32,2,16,128]{3,2,1,0:T(8,128)(2,1)S(1)}, f32[27,32,32]{2,1,0:T(8,128)S(1)}, f32[27,32,32]{2,1,0:T(8,128)S(1)}, f32[4,32]{1,0:T(4,128)S(1)}) custom-call(bf16[32,2,16,128]{3,2,1,0:T(8,128)(2,1)} %x_a.1, bf16[32,2,16,128]{3,2,1,0:T(8,128)(2,1)} %x_b.1, bf16[32,2,16,128]{3,2,1,0:T(8,128)(2,1)} %grad.1, ...), custom_call_target="tpu_custom_call" | custom-call | tf_op jit(solution)/shard_map/pallas_call | solution.py:861
  76.3 1.1 %shard_map.129 = (bf16[32,2,16,128]{3,2,1,0:T(8,128)(2,1)}, bf16[32,2,16,128]{3,2,1,0:T(8,128)(2,1)}, f32[27,32,32]{2,1,0:T(8,128)}, f32[27,32,32]{2,1,0:T(8,128)}, f32[4,32]{1,0:T(4,128)}) custom-call(bf16[32,2,16,128]{3,2,1,0:T(8,128)(2,1)S(1)} %get-tuple-element.15.refs_0_, bf16[32,2,16,128]{3,2,1,0:T(8,128)(2,1)S(1)} %get-tuple-element.16.refs_1_, ...), custom_call_target="tpu_custom_call" | custom-call | tf_op jit(solution)/shard_map/pallas_call | solution.py:876

commit v7 on v6

--- a/solution.py
+++ b/solution.py
@@ -19,12 +19,20 @@
 DEPTH = PAD_X * 3 * TAPS
 FLAT = 9 * TAPS
 GROUP = 4
+INNER = 16
+OUTER = 18
 AXES = ("gx", "gy", "gz")
 MESH = pl.DeviceIdType.MESH
 
 
 def sigmoid(value):
     return 0.5 + 0.5 * jnp.tanh(0.5 * value)
+
+
+def unrolled(first, last, step, carry):
+    for index in range(first, last):
+        carry = step(index, carry)
+    return carry
 
 
 def rolled(tile, shift):
@@ -116,7 +124,7 @@
         return near, rest
 
     def own(self, side, volume, lane):
-        tile = self.cols[side, 1, 1].astype(F32)
+        tile = self.cols[side, 1, 1]
         at = 32 * volume
         return jnp.where(lane < 64, rolled(tile, 33 - at), rolled(tile, 49 - at))
 
@@ -126,7 +134,7 @@
 
         def strip(index, low, middle, high):
             low, middle, high = (
-                rolled(self.cols[side, index, k].astype(F32), shift - at)
+                rolled(self.cols[side, index, k], shift - at)
                 for k, shift in enumerate((low, middle, high))
             )
             return jnp.where(inside == 0, low, jnp.where(inside == PAD_Y - 1, high, middle))
@@ -210,16 +218,18 @@
                     device_id=to, device_id_type=pl.DeviceIdType.LOGICAL,
                 ).start()
 
-        def most(plane, carry):
-            copies(plane, spots[:-1])
+        def most(block, carry):
+            for k in range(4):
+                copies(block * 4 + k, spots[:-1])
             return carry
 
-        def rest(plane, carry):
-            copies(plane, spots[-1:])
+        def rest(block, carry):
+            for k in range(5):
+                copies(block * 5 + k, spots[-1:])
             return carry
 
-        lax.fori_loop(0, 16, most, 0)
-        lax.fori_loop(0, 15, rest, 0)
+        lax.fori_loop(0, 4, most, 0)
+        lax.fori_loop(0, 3, rest, 0)
 
     def fan_in(slots, semaphore):
         part = slots.at[pl.ds(0, count - 1)]
@@ -276,59 +286,58 @@
 
     def extract(tile, spot, carry):
         first, last = carry
+        tile = tile.astype(BF16)
         first = jnp.where(lane == spot, pltpu.roll(tile, spot, 1), first)
         last = jnp.where(lane == spot, pltpu.roll(tile, lax.rem(spot + 1, LANES), 1), last)
         return first, last
 
-    def put_taps(taps, volume, at_x, at_y, tile, side_lo, side_hi):
-        spot = at_x * 32 + at_y
-        left = jnp.where(
-            lane == 0,
-            pltpu.roll(side_lo, lax.rem(LANES - spot, LANES), 1),
-            pltpu.roll(tile, 1, 1),
-        )
-        right = jnp.where(
-            lane == LANES - 1,
-            pltpu.roll(side_hi, LANES - 1 - spot, 1),
-            pltpu.roll(tile, LANES - 1, 1),
-        )
-        taps[volume, at_x, at_y, 0:C] = left.astype(BF16)
-        taps[volume, at_x, at_y, C : 2 * C] = tile.astype(BF16)
-        taps[volume, at_x, at_y, 2 * C : 3 * C] = right.astype(BF16)
+    def put_taps(taps, volume, spots, tiles, sides):
+        low, high = sides[0][...], sides[1][...]
+        shifted = []
+        for (at_x, at_y), tile in zip(spots, tiles):
+            spot = at_x * 32 + at_y
+            left = jnp.where(
+                lane == 0,
+                pltpu.roll(low, lax.rem(LANES - spot, LANES), 1),
+                pltpu.roll(tile, 1, 1),
+            )
+            right = jnp.where(
+                lane == LANES - 1,
+                pltpu.roll(high, LANES - 1 - spot, 1),
+                pltpu.roll(tile, LANES - 1, 1),
+            )
+            shifted.append((left, tile, right))
+        for (at_x, at_y), rows in zip(spots, shifted):
+            for k, row in enumerate(rows):
+                taps[volume, at_x, at_y, k * C : (k + 1) * C] = row
 
     def build_inner(taps, volume, inner, sides):
-        low, high = sides
-        for at_x in (1, 2):
+        for at_x in range(SPAN_X):
 
             def step(block, carry, at_x=at_x):
-                for k in range(8):
-                    at_y = block * 8 + k
-                    put_taps(
-                        taps, volume, at_x, at_y + 1, inner(at_x - 1, at_y), low[...], high[...]
-                    )
+                rows = [block * INNER + k for k in range(INNER)]
+                tiles = [inner(at_x, at_y).astype(BF16) for at_y in rows]
+                put_taps(taps, volume, [(at_x + 1, at_y + 1) for at_y in rows], tiles, sides)
                 return carry
 
-            lax.fori_loop(0, 2, step, 0)
+            unrolled(0, SPAN_Y // INNER, step, 0)
 
     def build_outer(taps, volume, outer, sides):
-        low, high = sides
-        zero = jnp.zeros((C, LANES), F32)
-
-        def put(at_x, at_y):
-            tile = jnp.where(keep(at_x, at_y), outer(at_x, at_y), zero)
-            put_taps(taps, volume, at_x, at_y, tile, low[...], high[...])
-
-        for at_x in (1, 2):
-            for at_y in (0, PAD_Y - 1):
-                put(at_x, at_y)
+        def put(spots):
+            tiles = [
+                jnp.where(keep(at_x, at_y), outer(at_x, at_y).astype(BF16), none)
+                for at_x, at_y in spots
+            ]
+            put_taps(taps, volume, spots, tiles, sides)
+
+        put([(at_x, at_y) for at_x in (1, 2) for at_y in (0, PAD_Y - 1)])
         for at_x in (0, PAD_X - 1):
 
             def step(block, carry, at_x=at_x):
-                for k in range(6):
-                    put(at_x, block * 6 + k)
+                put([(at_x, block * OUTER + k) for k in range(OUTER)])
                 return carry
 
-            lax.fori_loop(0, 3, step, 0)
+            unrolled(0, PAD_Y // OUTER, step, 0)
 
     def build(taps, volume, outer, inner, sides):
         build_inner(taps, volume, inner, sides)
@@ -351,7 +360,7 @@
                     carry = emit(at_x, first + k, tile, carry)
             return carry
 
-        return lax.fori_loop(0, SPAN_Y // GROUP, step, carry)
+        return unrolled(0, SPAN_Y // GROUP, step, carry)
 
     def kernel_grad(taps, volume, row_of, out, first_row, plain=False):
         high = SPAN_X * C + (16 if plain else 0)
@@ -372,7 +381,7 @@
                 preferred_element_type=F32,
             )
 
-        total = lax.fori_loop(0, SPAN_Y // GROUP, step, jnp.zeros((high, DEPTH), F32))
+        total = unrolled(0, SPAN_Y // GROUP, step, 0.0)
         slab = 3 * TAPS
 
         def wide(value):
@@ -462,6 +471,7 @@
                 weights[index, C : 2 * C, LANES * k : LANES * (k + 1)] = low[k].astype(BF16)
 
     zero = jnp.zeros((C, LANES), F32)
+    none = jnp.zeros((C, LANES), BF16)
 
     def take(load, source, at, carry):
         load.wait()
@@ -475,20 +485,20 @@
                 for k in range(8):
                     at_y = block * 8 + k
                     carry = extract(
-                        rows_x[at, at_x + 1, at_y + 1].astype(F32),
+                        rows_x[at, at_x + 1, at_y + 1],
                         32 * at + 16 * at_x + at_y,
                         carry,
                     )
                 return carry
 
-            carry = lax.fori_loop(0, 2, step, carry)
+            carry = unrolled(0, 2, step, carry)
         return carry
 
-    carry = (zero, zero)
+    carry = (none, none)
     for at, source in enumerate((block_a, block_b, block_g)):
         carry = take(loads[at], source, at, carry)
-    edge_x[0] = carry[0].astype(BF16)
-    edge_x[1] = carry[1].astype(BF16)
+    edge_x[0] = carry[0]
+    edge_x[1] = carry[1]
 
     pl.semaphore_wait(barrier, count - 1)
 
@@ -502,26 +512,26 @@
     halo_x.arrive(near)
     for volume in range(2):
         for side in range(2):
-            side_x[volume, side] = jnp.where(ok[side], halo_x.own(side, volume, lane), 0.0)
+            side_x[volume, side] = jnp.where(ok[side], halo_x.own(side, volume, lane), none)
         build_inner(
             taps_x, volume,
-            lambda at_x, at_y, volume=volume: rows_x[volume, at_x + 1, at_y + 1].astype(F32),
+            lambda at_x, at_y, volume=volume: rows_x[volume, at_x + 1, at_y + 1],
             (side_x.at[volume, 0], side_x.at[volume, 1]),
         )
     halo_x.arrive(rest)
     for side in range(2):
         for volume in range(3):
             tile = halo_x.merged(side, volume, lane)
-            side_x[volume, side] = jnp.where(ok[side], tile, 0.0)
+            side_x[volume, side] = jnp.where(ok[side], tile, none)
 
     columns = []
     waits_1 = []
-    carry = (zero,) * 2
+    carry = (none,) * 2
     for volume in range(2):
         halo_x.arrive(waits_x[volume])
         build_outer(
             taps_x, volume,
-            lambda at_x, at_y, volume=volume: rows_x[volume, at_x, at_y].astype(F32),
+            lambda at_x, at_y, volume=volume: rows_x[volume, at_x, at_y],
             (side_x.at[volume, 0], side_x.at[volume, 1]),
         )
 
@@ -538,8 +548,8 @@
         columns += [
             jnp.sum(total, axis=1, keepdims=True), jnp.sum(squares, axis=1, keepdims=True)
         ]
-    edge_1[0] = carry[0].astype(BF16)
-    edge_1[1] = carry[1].astype(BF16)
+    edge_1[0] = carry[0]
+    edge_1[1] = carry[1]
     totals[0].start(pack(columns))
     near, rest = halo_1.small()
     waits_1.append(halo_1.faces_x(1))
@@ -575,7 +585,9 @@
         for side in range(2):
             tile = halo_1.merged(side, volume, lane)
             side_1[volume, side] = tile
-            side_h[volume, side] = jnp.where(ok[side], active(tile), 0.0)
+            side_h[volume, side] = jnp.where(
+                ok[side], active(tile.astype(F32)), 0.0
+            ).astype(BF16)
         sides = (side_h.at[volume, 0], side_h.at[volume, 1])
         build_inner(
             taps_h, volume, functools.partial(own_row, volume=volume, active=active), sides
@@ -603,9 +615,9 @@
                 first, last = extract(tile, 16 * at_x + at_y, (first, last))
                 return total + tile, squares + tile * tile, first, last
 
-            total, squares, first, last = convolve(taps_h, 1, 1, emit, (zero,) * 4)
-            edge_2[0] = first.astype(BF16)
-            edge_2[1] = last.astype(BF16)
+            total, squares, first, last = convolve(taps_h, 1, 1, emit, (zero, zero, none, none))
+            edge_2[0] = first
+            edge_2[1] = last
         columns += [
             jnp.sum(total, axis=1, keepdims=True), jnp.sum(squares, axis=1, keepdims=True)
         ]
@@ -661,7 +673,7 @@
                     total, weighted = total + slope, weighted + slope * normed
                 return total, weighted
 
-            carry = lax.fori_loop(0, 2, step, carry)
+            carry = unrolled(0, 2, step, carry)
         return [jnp.sum(part, axis=1, keepdims=True) for part in carry]
 
     columns = sum_rows(
@@ -683,7 +695,7 @@
                 stage[at_x, at_y] = pre * sigmoid(pre)
             return carry
 
-        lax.fori_loop(0, 2, step, 0)
+        unrolled(0, 2, step, 0)
         y_out[:, at_x] = jnp.swapaxes(stage[at_x], 0, 1).astype(BF16)
 
     halo_x.arrive(waits_g)
@@ -692,8 +704,10 @@
 
     delta_2 = delta_of(slope_2, sum_d2, sum_x2, gain_2, scale_2)
     for side in range(2):
-        tile = delta_2(halo_2.merged(side, 0, lane), side_x[2, side])
-        side_2[0, side] = jnp.where(ok[side], tile, 0.0)
+        tile = delta_2(
+            halo_2.merged(side, 0, lane).astype(F32), side_x[2, side].astype(F32)
+        )
+        side_2[0, side] = jnp.where(ok[side], tile, 0.0).astype(BF16)
     build(
         taps_d2, 0,
         lambda at_x, at_y: delta_2(
@@ -715,9 +729,9 @@
         slopes[at_x, at_y] = slope.astype(BF16)
         return total + slope, weighted + slope * normed, first, last
 
-    total, weighted, first, last = convolve(taps_d2, 0, 2, emit, (zero,) * 4)
-    edge_e[0] = first.astype(BF16)
-    edge_e[1] = last.astype(BF16)
+    total, weighted, first, last = convolve(taps_d2, 0, 2, emit, (zero, zero, none, none))
+    edge_e[0] = first
+    edge_e[1] = last
     columns = [
         jnp.sum(total, axis=1, keepdims=True), jnp.sum(weighted, axis=1, keepdims=True)
     ]
@@ -735,8 +749,10 @@
 
     delta_1 = delta_of(slope_1, sum_d1, sum_x1, gain_1, scale_1)
     for side in range(2):
-        tile = delta_1(side_1[1, side], halo_e.merged(side, 0, lane))
-        side_e[0, side] = jnp.where(ok[side], tile, 0.0)
+        tile = delta_1(
+            side_1[1, side].astype(F32), halo_e.merged(side, 0, lane).astype(F32)
+        )
+        side_e[0, side] = jnp.where(ok[side], tile, 0.0).astype(BF16)
     build(
         taps_d1, 0,
         lambda at_x, at_y: delta_1(
@@ -825,8 +841,7 @@
     scratch += [sized(count, PAD_X, PAD_Y, C, LANES) for count in volumes]
     scratch += [sized(2, 3, 3, C, LANES) for count in volumes]
     scratch += [sized(2, C, LANES) for count in volumes]
-    scratch += [sized(count, 2, C, LANES, kind=F32) for count in volumes]
-    scratch += [sized(2, 2, C, LANES, kind=F32)]
+    scratch += [sized(count, 2, C, LANES) for count in volumes] + [sized(2, 2, C, LANES)]
     scratch += [
         sized(2, SPAN_X, SPAN_Y, C, LANES, kind=F32),
         sized(2, SPAN_X, SPAN_Y, C, LANES, kind=F32),

time: 77.5 us -> 67.6 us (0.87)
  Pallas kernels: 76.8 us -> 66.7 us
    pallas_call x1, Pallas kernels: 75.7 us -> 65.6 us  [body(): pl.pallas_call(functools.partial(kernel, voxels), out_shape=out_shape, in...]
where the time goes in v7:
time: 67.6 us; the launch traced here: 67.5 us
  Pallas kernels  66.7 us (99%)
  between operations  0.8 us (1%)
    pallas_call x1, Pallas kernels, body(): pl.pallas_call(functools.partial(kernel, voxels), out_shape=out_shape, in...  65.6 us

profile of v7, /device:TPU:1, one launch (start us, length us, event | category | flops | bytes accessed | tf_op | source)
XLA Modules:
  0.0 67.5 jit_solution(4109967310696806791)
XLA Ops:
  0.6 65.6 %shard_map.128 = (bf16[32,2,16,128]{3,2,1,0:T(8,128)(2,1)S(1)}, bf16[32,2,16,128]{3,2,1,0:T(8,128)(2,1)S(1)}, f32[27,32,32]{2,1,0:T(8,128)S(1)}, f32[27,32,32]{2,1,0:T(8,128)S(1)}, f32[4,32]{1,0:T(4,128)S(1)}) custom-call(bf16[32,2,16,128]{3,2,1,0:T(8,128)(2,1)} %x_a.1, bf16[32,2,16,128]{3,2,1,0:T(8,128)(2,1)} %x_b.1, bf16[32,2,16,128]{3,2,1,0:T(8,128)(2,1)} %grad.1, ...), custom_call_target="tpu_custom_call" | custom-call | tf_op jit(solution)/shard_map/pallas_call | solution.py:876
  66.2 1.1 %shard_map.129 = (bf16[32,2,16,128]{3,2,1,0:T(8,128)(2,1)}, bf16[32,2,16,128]{3,2,1,0:T(8,128)(2,1)}, f32[27,32,32]{2,1,0:T(8,128)}, f32[27,32,32]{2,1,0:T(8,128)}, f32[4,32]{1,0:T(4,128)}) custom-call(bf16[32,2,16,128]{3,2,1,0:T(8,128)(2,1)S(1)} %get-tuple-element.15.refs_0_, bf16[32,2,16,128]{3,2,1,0:T(8,128)(2,1)S(1)} %get-tuple-element.16.refs_1_, ...), custom_call_target="tpu_custom_call" | custom-call | tf_op jit(solution)/shard_map/pallas_call | solution.py:891

commit v8 on v7

--- a/solution.py
+++ b/solution.py
@@ -174,7 +174,8 @@
     side_h,
     conv_1, conv_2, back_1,
     sums,
-    norms, slopes, early_out, early_in, late_out, late_in, gathered, pairs,
+    norms, slopes, norms_2, slopes_2,
+    early_out, early_in, mid_out, mid_in, late_out, late_in, gathered, pairs,
     halo_send, halo_recv, sums_send, sums_recv, gw_send, gw_recv, local,
 ):
     loads = [
@@ -188,9 +189,13 @@
     for load in loads:
         load.start()
     place = {axis: (lax.axis_index(axis), lax.axis_size(axis)) for axis in AXES}
-    for chunks in (early_out, late_out):
+    for chunks in (early_out, mid_out, late_out):
         for j in range(4):
-            chunks[32 * j + 28 : 32 * j + 32] = jnp.zeros((4, 4, LANES), F32)
+            at = slice(32 * j + 28, 32 * j + 32)
+            chunks[at] = jnp.zeros((4, chunks.shape[1], LANES), F32)
+    for rows in (norms, slopes, norms_2, slopes_2):
+        for at in (0, SPAN_Y + 2):
+            rows[:, at : at + 2] = jnp.zeros((SPAN_X, 2, C, LANES), BF16)
     barrier = pltpu.get_barrier_semaphore()
     count = place["gx"][1] * place["gy"][1] * place["gz"][1]
     flat = (place["gx"][0] * place["gy"][1] + place["gy"][0]) * place["gz"][1] + place["gz"][0]
@@ -362,44 +367,61 @@
 
         return unrolled(0, SPAN_Y // GROUP, step, carry)
 
-    def kernel_grad(taps, volume, row_of, out, first_row, plain=False):
-        high = SPAN_X * C + (16 if plain else 0)
-
-        def step(block, total):
-            first = block * GROUP
-            left, right = [], []
-            for k in range(GROUP):
-                rows = [row_of(at_x, first + k) for at_x in range(SPAN_X)]
-                if plain:
-                    rows.append(jnp.ones((16, LANES), BF16))
-                left.append(jnp.concatenate(rows, axis=0))
-                right.append(taps[volume, :, pl.ds(first + k, 3)].reshape(DEPTH, LANES))
-            return total + lax.dot_general(
-                jnp.concatenate(left, axis=1),
-                jnp.concatenate(right, axis=1),
-                (((1,), (1,)), ((), ())),
-                preferred_element_type=F32,
-            )
-
-        total = unrolled(0, SPAN_Y // GROUP, step, 0.0)
-        slab = 3 * TAPS
-
-        def wide(value):
+    def kernel_grad(taps, volume, buffers, out, plain):
+        tap_row = lax.broadcasted_iota(jnp.int32, (16, LANES), 0)
+        left, right = [], []
+        for at_y in range(PAD_Y):
+            parts = [
+                rows[at_x, at_y - tap + 2]
+                for rows in buffers for tap in range(3) for at_x in range(SPAN_X)
+            ]
+            if plain:
+                inside = [0 <= at_y - tap < SPAN_Y for tap in range(3)]
+                first = inside.index(True)
+                mine = jnp.logical_and(tap_row >= first, tap_row < first + sum(inside))
+                parts.append(jnp.where(mine, 1.0, 0.0).astype(BF16))
+            left.append(jnp.concatenate(parts, axis=0))
+            right.append(taps[volume, :, at_y].reshape(PAD_X * TAPS, LANES))
+        total = lax.dot_general(
+            jnp.concatenate(left, axis=1),
+            jnp.concatenate(right, axis=1),
+            (((1,), (1,)), ((), ())),
+            preferred_element_type=F32,
+        )
+
+        def wide(pieces):
+            height = pieces[0].shape[0]
             return jnp.concatenate(
-                [value, jnp.zeros((value.shape[0], 7 * LANES - FLAT), F32)], axis=1
-            )
-
-        both = wide(total[0:C, 0:FLAT] + total[C : 2 * C, slab : slab + FLAT])
+                pieces + [jnp.zeros((height, 7 * LANES - FLAT), F32)], axis=1
+            )
+
+        def slab(row, height, at_x):
+            return total[row : row + height, TAPS * at_x : TAPS * (at_x + 1)]
+
+        blocks = []
+        for index in range(len(buffers)):
+            first = 6 * C * index
+            pieces = []
+            for tap_x in range(3):
+                for tap_y in range(3):
+                    row = first + 2 * C * tap_y
+                    pieces.append(slab(row, C, tap_x) + slab(row + C, C, tap_x + 1))
+            blocks.append(wide(pieces))
         if plain:
-            alone = total[2 * C : 2 * C + 1]
-            alone = wide(alone[:, 0:FLAT] + alone[:, slab : slab + FLAT])
+            first = 6 * C * len(buffers)
+            alone = wide([
+                slab(first + tap_y, 1, tap_x) + slab(first + tap_y, 1, tap_x + 1)
+                for tap_x in range(3) for tap_y in range(3)
+            ])
         for k in range(7):
             lanes = slice(LANES * k, LANES * (k + 1))
             for pair in range(16):
                 spot = (pair // 4 * 8 + k) * 4 + pair % 4
-                out[spot, first_row : first_row + 2] = both[2 * pair : 2 * pair + 2, lanes]
+                for index, block in enumerate(blocks):
+                    out[spot, 2 * index : 2 * index + 2] = block[2 * pair : 2 * pair + 2, lanes]
                 if plain:
-                    out[spot, 2:3] = alone[:, lanes]
+                    last = 2 * len(blocks)
+                    out[spot, last : last + 1] = alone[:, lanes]
 
     channel = lax.broadcasted_iota(jnp.int32, (C, LANES), 0)
 
@@ -579,7 +601,7 @@
         def own_row(at_x, at_y, volume, active, norm_slope=norm_slope, norm_shift=norm_shift):
             value = conv_1[volume, at_x, at_y]
             if volume == 1:
-                norms[at_x, at_y] = (value * norm_slope + norm_shift).astype(BF16)
+                norms[at_x, at_y + 2] = (value * norm_slope + norm_shift).astype(BF16)
             return active(value)
 
         for side in range(2):
@@ -625,7 +647,7 @@
     totals[1].start(pack(columns))
     near, rest = halo_2.small()
     waits = near + rest + halo_2.faces_x(0)
-    kernel_grad(taps_x, 1, lambda at_x, at_y: norms[at_x, at_y], early_out, 0, plain=True)
+    kernel_grad(taps_x, 1, [norms], early_out, True)
     fan_out(
         lambda to: early_out.at[to], early_in.at[flat], gw_send.at[0], gw_recv.at[0]
     )
@@ -670,6 +692,8 @@
                 for k in range(8):
                     at_y = block * 8 + k
                     slope, normed = slope_of(value_of(at_x, at_y), upstream_of(at_x, at_y))
+                    slopes_2[at_x, at_y + 2] = slope.astype(BF16)
+                    norms_2[at_x, at_y + 2] = normed.astype(BF16)
                     total, weighted = total + slope, weighted + slope * normed
                 return total, weighted
 
@@ -698,6 +722,9 @@
         unrolled(0, 2, step, 0)
         y_out[:, at_x] = jnp.swapaxes(stage[at_x], 0, 1).astype(BF16)
 
+    kernel_grad(taps_h, 1, [slopes_2, norms_2], mid_out, True)
+    fan_out(lambda to: mid_out.at[to], mid_in.at[flat], gw_send.at[1], gw_recv.at[1])
+    mid_in[flat] = mid_out[flat]
     halo_x.arrive(waits_g)
     halo_2.arrive(waits)
     sum_d2, sum_x2 = unpack(totals[2].finish(), 2)
@@ -726,7 +753,7 @@
         rows_e[0, at_x + 1, at_y + 1] = tile.astype(BF16)
         first, last = extract(tile, 16 * at_x + at_y, (first, last))
         slope, normed = slope_1(conv_1[1, at_x, at_y], tile)
-        slopes[at_x, at_y] = slope.astype(BF16)
+        slopes[at_x, at_y + 2] = slope.astype(BF16)
         return total + slope, weighted + slope * normed, first, last
 
     total, weighted, first, last = convolve(taps_d2, 0, 2, emit, (zero, zero, none, none))
@@ -738,15 +765,38 @@
     totals[3].start(pack(columns))
     near, rest = halo_e.small()
     waits = near + rest + halo_e.faces_x(0)
-    kernel_grad(taps_x, 1, lambda at_x, at_y: slopes[at_x, at_y], late_out, 0)
-    kernel_grad(
-        taps_h, 1, lambda at_x, at_y: taps_d2[0, at_x + 1, at_y + 1, C : 2 * C], late_out, 2
-    )
-    fan_out(lambda to: late_out.at[to], late_in.at[flat], gw_send.at[1], gw_recv.at[1])
+    kernel_grad(taps_x, 1, [slopes], late_out, False)
+    fan_out(lambda to: late_out.at[to], late_in.at[flat], gw_send.at[2], gw_recv.at[2])
     late_in[flat] = late_out[flat]
     sum_d1, sum_x1 = unpack(totals[3].finish(), 2)
+
+    whole = 1.0 / math.sqrt(voxels)
+    for k, factor in enumerate(
+        (
+            gain_1 * scale_1 * whole, sum_d1 / voxels, sum_x1 / voxels,
+            gain_2 * scale_2 * whole, sum_d2 / voxels, sum_x2 / voxels,
+        )
+    ):
+        tile = jnp.broadcast_to(factor, (C, LANES))
+        for pair in range(16):
+            pairs[k, pair] = tile[2 * pair : 2 * pair + 2]
+    fan_in(early_in, gw_recv.at[0])
+    early = jnp.sum(early_in[...], axis=0)
+    fan_in(mid_in, gw_recv.at[1])
+    mid = jnp.sum(mid_in[...], axis=0)
+    at = flat // 32 * 4 + lax.rem(flat, 4)
+    fan_in(late_in, gw_recv.at[2])
+    late = jnp.sum(late_in[...], axis=0)
+    gathered[flat, 0:2] = pairs[0, at] * (
+        late[0:2] - pairs[1, at] * early[2:3] - pairs[2, at] * early[0:2]
+    )
+    gathered[flat, 2:4] = pairs[3, at] * (
+        mid[0:2] - pairs[4, at] * mid[4:5] - pairs[5, at] * mid[2:4]
+    )
+    mine = gathered.at[flat]
+    fan_out(lambda to: mine, mine, gw_send.at[3], gw_recv.at[3])
+
     halo_e.arrive(waits)
-
     delta_1 = delta_of(slope_1, sum_d1, sum_x1, gain_1, scale_1)
     for side in range(2):
         tile = delta_1(
@@ -761,25 +811,6 @@
         lambda at_x, at_y: delta_1(conv_1[1, at_x, at_y], back_1[at_x, at_y]),
         (side_e.at[0, 0], side_e.at[0, 1]),
     )
-    whole = 1.0 / math.sqrt(voxels)
-    for k, factor in enumerate(
-        (gain_1 * scale_1 * whole, sum_d1 / voxels, sum_x1 / voxels)
-    ):
-        tile = jnp.broadcast_to(factor, (C, LANES))
-        for pair in range(16):
-            pairs[k, pair] = tile[2 * pair : 2 * pair + 2]
-    fan_in(early_in, gw_recv.at[0])
-    early = jnp.sum(early_in[...], axis=0)
-    at = flat // 32 * 4 + lax.rem(flat, 4)
-    fan_in(late_in, gw_recv.at[1])
-    late = jnp.sum(late_in[...], axis=0)
-    gathered[flat, 0:2] = pairs[0, at] * (
-        late[0:2] - pairs[1, at] * early[2:3] - pairs[2, at] * early[0:2]
-    )
-    gathered[flat, 2:4] = late[2:4] * whole
-    mine = gathered.at[flat]
-    fan_out(lambda to: mine, mine, gw_send.at[2], gw_recv.at[2])
-
     def emit(at_x, at_y, tile, carry):
         stage[at_x, at_y] = tile
         return carry
@@ -792,7 +823,7 @@
         norm_out[k : k + 1] = whole * jnp.sum(
             jnp.where(small_lane == small_row, total, 0.0), axis=0, keepdims=True
         )
-    fan_in(gathered, gw_recv.at[2])
+    fan_in(gathered, gw_recv.at[3])
     for member, out in ((0, gw_first), (1, gw_second)):
         for k in range(7):
             tile = jnp.concatenate(
@@ -809,7 +840,7 @@
         halo.drain()
     for total in totals:
         total.drain()
-    for k, chunks in enumerate((early_out, late_out, gathered)):
+    for k, chunks in enumerate((early_out, mid_out, late_out, gathered)):
         fan_in(chunks, gw_send.at[k])
 
 
@@ -847,20 +878,18 @@
         sized(2, SPAN_X, SPAN_Y, C, LANES, kind=F32),
         sized(SPAN_X, SPAN_Y, C, LANES, kind=F32),
         sized(4, devices, 1, LANES, kind=F32),
-        sized(SPAN_X, SPAN_Y, C, LANES),
-        sized(SPAN_X, SPAN_Y, C, LANES),
+        *[sized(SPAN_X, SPAN_Y + 4, C, LANES)] * 4,
+        *[sized(devices, 3, LANES, kind=F32)] * 2,
+        *[sized(devices, 5, LANES, kind=F32)] * 2,
+        *[sized(devices, 2, LANES, kind=F32)] * 2,
         sized(devices, 4, LANES, kind=F32),
-        sized(devices, 4, LANES, kind=F32),
-        sized(devices, 4, LANES, kind=F32),
-        sized(devices, 4, LANES, kind=F32),
-        sized(devices, 4, LANES, kind=F32),
-        sized(3, 16, 2, LANES, kind=F32),
+        sized(6, 16, 2, LANES, kind=F32),
         pltpu.SemaphoreType.DMA((4, 32)),
         pltpu.SemaphoreType.DMA((4, 32)),
         pltpu.SemaphoreType.DMA((4,)),
         pltpu.SemaphoreType.DMA((4,)),
-        pltpu.SemaphoreType.DMA((3,)),
-        pltpu.SemaphoreType.DMA((3,)),
+        pltpu.SemaphoreType.DMA((4,)),
+        pltpu.SemaphoreType.DMA((4,)),
         pltpu.SemaphoreType.DMA((9,)),
     ]
     in_vmem = pl.BlockSpec(memory_space=pltpu.VMEM)

time: 67.6 us -> 66.5 us (0.984)
  Pallas kernels: 66.7 us -> 65.6 us
    pallas_call x1, Pallas kernels: 65.6 us -> 64.4 us  [body(): pl.pallas_call(functools.partial(kernel, voxels), out_shape=out_shape, in...]
where the time goes in v8:
time: 66.5 us; the launch traced here: 66.4 us
  Pallas kernels  65.6 us (99%)
  between operations  0.8 us (1%)
    pallas_call x1, Pallas kernels, body(): pl.pallas_call(functools.partial(kernel, voxels), out_shape=out_shape, in...  64.4 us

profile of v8, /device:TPU:1, one launch (start us, length us, event | category | flops | bytes accessed | tf_op | source)
XLA Modules:
  0.0 66.4 jit_solution(17490303531824549293)
XLA Ops:
  0.6 64.4 %shard_map.128 = (bf16[32,2,16,128]{3,2,1,0:T(8,128)(2,1)S(1)}, bf16[32,2,16,128]{3,2,1,0:T(8,128)(2,1)S(1)}, f32[27,32,32]{2,1,0:T(8,128)S(1)}, f32[27,32,32]{2,1,0:T(8,128)S(1)}, f32[4,32]{1,0:T(4,128)S(1)}) custom-call(bf16[32,2,16,128]{3,2,1,0:T(8,128)(2,1)} %x_a.1, bf16[32,2,16,128]{3,2,1,0:T(8,128)(2,1)} %x_b.1, bf16[32,2,16,128]{3,2,1,0:T(8,128)(2,1)} %grad.1, ...), custom_call_target="tpu_custom_call" | custom-call | tf_op jit(solution)/shard_map/pallas_call | solution.py:905
  65.1 1.1 %shard_map.129 = (bf16[32,2,16,128]{3,2,1,0:T(8,128)(2,1)}, bf16[32,2,16,128]{3,2,1,0:T(8,128)(2,1)}, f32[27,32,32]{2,1,0:T(8,128)}, f32[27,32,32]{2,1,0:T(8,128)}, f32[4,32]{1,0:T(4,128)}) custom-call(bf16[32,2,16,128]{3,2,1,0:T(8,128)(2,1)S(1)} %get-tuple-element.15.refs_0_, bf16[32,2,16,128]{3,2,1,0:T(8,128)(2,1)S(1)} %get-tuple-element.16.refs_1_, ...), custom_call_target="tpu_custom_call" | custom-call | tf_op jit(solution)/shard_map/pallas_call | solution.py:920

commit v9 on v8

--- a/solution.py
+++ b/solution.py
@@ -16,9 +16,10 @@
 SPAN_X, SPAN_Y = 2, 16
 PAD_X, PAD_Y = SPAN_X + 2, SPAN_Y + 2
 TAPS = 3 * C
-DEPTH = PAD_X * 3 * TAPS
+DEPTH = PAD_X * TAPS
+HEIGHT = 3 * SPAN_X * C
 FLAT = 9 * TAPS
-GROUP = 4
+GROUP = 2
 INNER = 16
 OUTER = 18
 AXES = ("gx", "gy", "gz")
@@ -123,8 +124,20 @@
             rest += self.columns(step_x, step_y)
         return near, rest
 
+    def put_edge(self, first, last, lane):
+        for index, tile in enumerate((first, last)):
+            if self.volumes < 3:
+                tile = jnp.where(lane[:16] < 64, tile[:16], pltpu.roll(tile[16:], 64, 1))
+            self.edge[index] = tile
+
+    def tile(self, side, index_x, index_y):
+        tile = self.cols[side, index_x, index_y]
+        if self.volumes < 3:
+            tile = jnp.concatenate([tile, pltpu.roll(tile, 64, 1)], axis=0)
+        return tile
+
     def own(self, side, volume, lane):
-        tile = self.cols[side, 1, 1]
+        tile = self.tile(side, 1, 1)
         at = 32 * volume
         return jnp.where(lane < 64, rolled(tile, 33 - at), rolled(tile, 49 - at))
 
@@ -134,7 +147,7 @@
 
         def strip(index, low, middle, high):
             low, middle, high = (
-                rolled(self.cols[side, index, k], shift - at)
+                rolled(self.tile(side, index, k), shift - at)
                 for k, shift in enumerate((low, middle, high))
             )
             return jnp.where(inside == 0, low, jnp.where(inside == PAD_Y - 1, high, middle))
@@ -224,17 +237,17 @@
                 ).start()
 
         def most(block, carry):
-            for k in range(4):
-                copies(block * 4 + k, spots[:-1])
+            for k in range(8):
+                copies(block * 8 + k, spots[:-1])
             return carry
 
         def rest(block, carry):
-            for k in range(5):
-                copies(block * 5 + k, spots[-1:])
+            for k in range(15):
+                copies(block * 15 + k, spots[-1:])
             return carry
 
-        lax.fori_loop(0, 4, most, 0)
-        lax.fori_loop(0, 3, rest, 0)
+        lax.fori_loop(0, 2, most, 0)
+        rest(0, 0)
 
     def fan_in(slots, semaphore):
         part = slots.at[pl.ds(0, count - 1)]
@@ -349,23 +362,27 @@
         build_outer(taps, volume, outer, sides)
 
     def convolve(taps, volume, weight, emit, carry):
-        def step(block, carry):
-            first = block * GROUP
+        parts = {}
+        for block in range(PAD_Y // GROUP):
             columns = [
-                taps[volume, :, pl.ds(first + k, 3)].reshape(DEPTH, LANES) for k in range(GROUP)
+                taps[volume, :, block * GROUP + k].reshape(DEPTH, LANES) for k in range(GROUP)
             ]
             total = jnp.dot(
-                weights[weight],
-                jnp.concatenate(columns, axis=1),
-                preferred_element_type=F32,
+                weights[weight], jnp.concatenate(columns, axis=1), preferred_element_type=F32
             )
             for k in range(GROUP):
+                parts[block * GROUP + k] = total[:, k * LANES : (k + 1) * LANES]
+            for at_y in range((block - 1) * GROUP, block * GROUP):
+                if at_y < 0 or at_y + 2 not in parts:
+                    continue
                 for at_x in range(SPAN_X):
-                    tile = total[at_x * C : (at_x + 1) * C, k * LANES : (k + 1) * LANES]
-                    carry = emit(at_x, first + k, tile, carry)
-            return carry
-
-        return unrolled(0, SPAN_Y // GROUP, step, carry)
+                    low = at_x * C
+                    tile = parts[at_y][low : low + C]
+                    for tap in (1, 2):
+                        first = tap * SPAN_X * C + low
+                        tile = tile + parts[at_y + tap][first : first + C]
+                    carry = emit(at_x, at_y, tile, carry)
+        return carry
 
     def kernel_grad(taps, volume, buffers, out, plain):
         tap_row = lax.broadcasted_iota(jnp.int32, (16, LANES), 0)
@@ -381,7 +398,7 @@
                 mine = jnp.logical_and(tap_row >= first, tap_row < first + sum(inside))
                 parts.append(jnp.where(mine, 1.0, 0.0).astype(BF16))
             left.append(jnp.concatenate(parts, axis=0))
-            right.append(taps[volume, :, at_y].reshape(PAD_X * TAPS, LANES))
+            right.append(taps[volume, :, at_y].reshape(DEPTH, LANES))
         total = lax.dot_general(
             jnp.concatenate(left, axis=1),
             jnp.concatenate(right, axis=1),
@@ -478,19 +495,21 @@
             for k in range(7)
         ]
         turned = [tile.T for tile in tiles]
-        pieces = [turned[tap // 4][C * (tap % 4) : C * (tap % 4) + C] for tap in range(26, -1, -1)]
-        back = [jnp.concatenate((pieces + pieces[:1])[4 * k : 4 * k + 4], axis=1) for k in range(7)]
-        for index, parts in ((forward, tiles), (backward, back)):
-            last = jnp.where(lane < 96, parts[6], 0.0)
-            empty = jnp.zeros((C, LANES), F32)
-            top = parts[:6] + [last, empty, empty]
-            moved = [pltpu.roll(part, 32, 1) for part in parts[:6] + [last]]
-            low = [empty, empty]
-            for k in range(7):
-                low.append(jnp.where(lane < 32, moved[k - 1] if k else empty, moved[k]))
-            for k in range(9):
-                weights[index, 0:C, LANES * k : LANES * (k + 1)] = top[k].astype(BF16)
-                weights[index, C : 2 * C, LANES * k : LANES * (k + 1)] = low[k].astype(BF16)
+        empty = jnp.zeros((C, C), F32)
+        ahead = [source[tap].astype(F32) for tap in range(27)]
+        back = [turned[tap // 4][C * (tap % 4) : C * (tap % 4) + C] for tap in range(26, -1, -1)]
+        for index, pieces in ((forward, ahead), (backward, back)):
+            for tap_y in range(3):
+                line = [
+                    pieces[(tap_x * 3 + tap_y) * 3 + tap_z]
+                    for tap_x in range(3) for tap_z in range(3)
+                ]
+                for at_x, row in ((0, line + [empty] * 3), (1, [empty] * 3 + line)):
+                    first = (tap_y * SPAN_X + at_x) * C
+                    for k in range(3):
+                        weights[index, first : first + C, LANES * k : LANES * (k + 1)] = (
+                            jnp.concatenate(row[4 * k : 4 * k + 4], axis=1).astype(BF16)
+                        )
 
     zero = jnp.zeros((C, LANES), F32)
     none = jnp.zeros((C, LANES), BF16)
@@ -519,8 +538,7 @@
     carry = (none, none)
     for at, source in enumerate((block_a, block_b, block_g)):
         carry = take(loads[at], source, at, carry)
-    edge_x[0] = carry[0]
-    edge_x[1] = carry[1]
+    halo_x.put_edge(*carry, lane)
 
     pl.semaphore_wait(barrier, count - 1)
 
@@ -570,8 +588,7 @@
         columns += [
             jnp.sum(total, axis=1, keepdims=True), jnp.sum(squares, axis=1, keepdims=True)
         ]
-    edge_1[0] = carry[0]
-    edge_1[1] = carry[1]
+    halo_1.put_edge(*carry, lane)
     totals[0].start(pack(columns))
     near, rest = halo_1.small()
     waits_1.append(halo_1.faces_x(1))
@@ -638,8 +655,7 @@
                 return total + tile, squares + tile * tile, first, last
 
             total, squares, first, last = convolve(taps_h, 1, 1, emit, (zero, zero, none, none))
-            edge_2[0] = first
-            edge_2[1] = last
+            halo_2.put_edge(first, last, lane)
         columns += [
             jnp.sum(total, axis=1, keepdims=True), jnp.sum(squares, axis=1, keepdims=True)
         ]
@@ -757,16 +773,15 @@
         return total + slope, weighted + slope * normed, first, last
 
     total, weighted, first, last = convolve(taps_d2, 0, 2, emit, (zero, zero, none, none))
-    edge_e[0] = first
-    edge_e[1] = last
+    halo_e.put_edge(first, last, lane)
     columns = [
         jnp.sum(total, axis=1, keepdims=True), jnp.sum(weighted, axis=1, keepdims=True)
     ]
     totals[3].start(pack(columns))
     near, rest = halo_e.small()
-    waits = near + rest + halo_e.faces_x(0)
     kernel_grad(taps_x, 1, [slopes], late_out, False)
     fan_out(lambda to: late_out.at[to], late_in.at[flat], gw_send.at[2], gw_recv.at[2])
+    waits = near + rest + halo_e.faces_x(0)
     late_in[flat] = late_out[flat]
     sum_d1, sum_x1 = unpack(totals[3].finish(), 2)
 
@@ -866,12 +881,13 @@
     block = (C, SPAN_X, SPAN_Y, LANES)
     scratch = [sized(*block)] * 3 + [sized(27, C, C)] * 2 + [sized(1, C, kind=F32)] * 4
     scratch += [
-        sized(4, SPAN_X * C, DEPTH), sized(SPAN_X, SPAN_Y, C, LANES, kind=F32)
+        sized(4, HEIGHT, DEPTH), sized(SPAN_X, SPAN_Y, C, LANES, kind=F32)
     ]
     scratch += [sized(count, PAD_X, PAD_Y, TAPS, LANES) for count in (2, 2, 1, 1)]
     scratch += [sized(count, PAD_X, PAD_Y, C, LANES) for count in volumes]
-    scratch += [sized(2, 3, 3, C, LANES) for count in volumes]
-    scratch += [sized(2, C, LANES) for count in volumes]
+    heights = [C if count == 3 else C // 2 for count in volumes]
+    scratch += [sized(2, 3, 3, height, LANES) for height in heights]
+    scratch += [sized(2, height, LANES) for height in heights]
     scratch += [sized(count, 2, C, LANES) for count in volumes] + [sized(2, 2, C, LANES)]
     scratch += [
         sized(2, SPAN_X, SPAN_Y, C, LANES, kind=F32),

time: 66.5 us -> 64.3 us (0.967)
  Pallas kernels: 65.6 us -> 63.4 us
    pallas_call x1, Pallas kernels: 64.4 us -> 62.3 us  [body(): pl.pallas_call(functools.partial(kernel, voxels), out_shape=out_shape, in...]
where the time goes in v9:
time: 64.3 us; the launch traced here: 64.2 us
  Pallas kernels  63.4 us (99%)
  between operations  0.8 us (1%)
    pallas_call x1, Pallas kernels, body(): pl.pallas_call(functools.partial(kernel, voxels), out_shape=out_shape, in...  62.3 us

profile of v9, /device:TPU:1, one launch (start us, length us, event | category | flops | bytes accessed | tf_op | source)
XLA Modules:
  0.0 64.2 jit_solution(10862921202187333220)
XLA Ops:
  0.6 62.3 %shard_map.128 = (bf16[32,2,16,128]{3,2,1,0:T(8,128)(2,1)S(1)}, bf16[32,2,16,128]{3,2,1,0:T(8,128)(2,1)S(1)}, f32[27,32,32]{2,1,0:T(8,128)S(1)}, f32[27,32,32]{2,1,0:T(8,128)S(1)}, f32[4,32]{1,0:T(4,128)S(1)}) custom-call(bf16[32,2,16,128]{3,2,1,0:T(8,128)(2,1)} %x_a.1, bf16[32,2,16,128]{3,2,1,0:T(8,128)(2,1)} %x_b.1, bf16[32,2,16,128]{3,2,1,0:T(8,128)(2,1)} %grad.1, ...), custom_call_target="tpu_custom_call" | custom-call | tf_op jit(solution)/shard_map/pallas_call | solution.py:921
  62.9 1.1 %shard_map.129 = (bf16[32,2,16,128]{3,2,1,0:T(8,128)(2,1)}, bf16[32,2,16,128]{3,2,1,0:T(8,128)(2,1)}, f32[27,32,32]{2,1,0:T(8,128)}, f32[27,32,32]{2,1,0:T(8,128)}, f32[4,32]{1,0:T(4,128)}) custom-call(bf16[32,2,16,128]{3,2,1,0:T(8,128)(2,1)S(1)} %get-tuple-element.15.refs_0_, bf16[32,2,16,128]{3,2,1,0:T(8,128)(2,1)S(1)} %get-tuple-element.16.refs_1_, ...), custom_call_target="tpu_custom_call" | custom-call | tf_op jit(solution)/shard_map/pallas_call | solution.py:936

commit v10 on v9

--- a/solution.py
+++ b/solution.py
@@ -263,16 +263,21 @@
 
     lane = lax.broadcasted_iota(jnp.int32, (C, LANES), 1)
     halos = []
+    def lone(refs, volume):
+        return refs.at[pl.ds(volume, 1)]
+
     for index, (rows, cols, edge, side, volumes) in enumerate((
         (rows_x, cols_x, edge_x, side_x, 3),
-        (rows_1, cols_1, edge_1, side_1, 2),
+        (lone(rows_1, 0), cols_1.at[0], edge_1.at[0], lone(side_1, 0), 1),
+        (lone(rows_1, 1), cols_1.at[1], edge_1.at[1], lone(side_1, 1), 1),
         (rows_2, cols_2, edge_2, side_2, 1),
         (rows_e, cols_e, edge_e, side_e, 1),
     )):
         halos.append(
             Halo(rows, cols, edge, side, halo_send.at[index], halo_recv.at[index], place, volumes)
         )
-    halo_x, halo_1, halo_2, halo_e = halos
+    halo_x, halo_a, halo_b, halo_2, halo_e = halos
+    halo_1 = (halo_a, halo_b)
 
     low_x, high_x = place["gx"][0] > 0, place["gx"][0] < place["gx"][1] - 1
     low_y, high_y = place["gy"][0] > 0, place["gy"][0] < place["gy"][1] - 1
@@ -543,14 +548,14 @@
     pl.semaphore_wait(barrier, count - 1)
 
     near, rest = halo_x.small()
-    waits_x = [halo_x.faces_x(0), halo_x.faces_x(1)]
+    waits_x = {volume: halo_x.faces_x(volume) for volume in (1, 0)}
     loads[3].wait()
     loads[4].wait()
     stack_weights(kernel_1, 0, 3)
     stack_weights(kernel_2, 1, 2)
     ok = [lane_keep(side) for side in range(2)]
     halo_x.arrive(near)
-    for volume in range(2):
+    for volume in (1, 0):
         for side in range(2):
             side_x[volume, side] = jnp.where(ok[side], halo_x.own(side, volume, lane), none)
         build_inner(
@@ -564,103 +569,93 @@
             tile = halo_x.merged(side, volume, lane)
             side_x[volume, side] = jnp.where(ok[side], tile, none)
 
-    columns = []
-    waits_1 = []
-    carry = (none,) * 2
-    for volume in range(2):
-        halo_x.arrive(waits_x[volume])
-        build_outer(
-            taps_x, volume,
-            lambda at_x, at_y, volume=volume: rows_x[volume, at_x, at_y],
-            (side_x.at[volume, 0], side_x.at[volume, 1]),
-        )
-
-        def emit(at_x, at_y, tile, carry, volume=volume):
-            total, squares, first, last = carry
-            conv_1[volume, at_x, at_y] = tile
-            rows_1[volume, at_x + 1, at_y + 1] = tile.astype(BF16)
-            first, last = extract(tile, 32 * volume + 16 * at_x + at_y, (first, last))
-            return total + tile, squares + tile * tile, first, last
-
-        total, squares, *carry = convolve(taps_x, volume, 0, emit, (zero, zero, *carry))
-        if volume == 0:
-            waits_1.append(halo_1.faces_x(0))
-        columns += [
-            jnp.sum(total, axis=1, keepdims=True), jnp.sum(squares, axis=1, keepdims=True)
-        ]
-    halo_1.put_edge(*carry, lane)
-    totals[0].start(pack(columns))
-    near, rest = halo_1.small()
-    waits_1.append(halo_1.faces_x(1))
-    row = totals[0].finish()
-    halo_1.arrive(near + rest)
-    waits_g = halo_x.faces_x(2)
-    stats = unpack(row, 4)
+    def both_sums(total, squares):
+        return [jnp.sum(total, axis=1, keepdims=True), jnp.sum(squares, axis=1, keepdims=True)]
 
     def moments(total, squares):
         mean = total / voxels
         scale = lax.rsqrt(squares / voxels - mean * mean + EPSILON)
         return mean, scale
 
-    columns = []
-    for volume in range(2):
-        mean, scale = moments(stats[2 * volume], stats[2 * volume + 1])
+    def first_layer(volume):
+        halo_x.arrive(waits_x[volume])
+        build_outer(
+            taps_x, volume,
+            lambda at_x, at_y: rows_x[volume, at_x, at_y],
+            (side_x.at[volume, 0], side_x.at[volume, 1]),
+        )
+
+        def emit(at_x, at_y, tile, carry):
+            total, squares, first, last = carry
+            conv_1[volume, at_x, at_y] = tile
+            rows_1[volume, at_x + 1, at_y + 1] = tile.astype(BF16)
+            first, last = extract(tile, 16 * at_x + at_y, (first, last))
+            return total + tile, squares + tile * tile, first, last
+
+        total, squares, first, last = convolve(
+            taps_x, volume, 0, emit, (zero, zero, none, none)
+        )
+        halo_1[volume].put_edge(first, last, lane)
+        return both_sums(total, squares)
+
+    def second_layer(volume, mean, scale, waits):
+        halo = halo_1[volume]
         slope = jnp.broadcast_to(gain_1 * scale, (C, LANES))
         shift = jnp.broadcast_to(bias_1 - mean * gain_1 * scale, (C, LANES))
-
-        def active(value, slope=slope, shift=shift):
+        norm_slope = jnp.broadcast_to(scale, (C, LANES))
+        norm_shift = jnp.broadcast_to(-mean * scale, (C, LANES))
+
+        def active(value):
             pre = value * slope + shift
             return pre * sigmoid(pre)
 
-        norm_slope = jnp.broadcast_to(scale, (C, LANES))
-        norm_shift = jnp.broadcast_to(-mean * scale, (C, LANES))
-
-        def own_row(at_x, at_y, volume, active, norm_slope=norm_slope, norm_shift=norm_shift):
+        def own_row(at_x, at_y):
             value = conv_1[volume, at_x, at_y]
             if volume == 1:
                 norms[at_x, at_y + 2] = (value * norm_slope + norm_shift).astype(BF16)
             return active(value)
 
         for side in range(2):
-            tile = halo_1.merged(side, volume, lane)
+            tile = halo.merged(side, 0, lane)
             side_1[volume, side] = tile
             side_h[volume, side] = jnp.where(
                 ok[side], active(tile.astype(F32)), 0.0
             ).astype(BF16)
         sides = (side_h.at[volume, 0], side_h.at[volume, 1])
-        build_inner(
-            taps_h, volume, functools.partial(own_row, volume=volume, active=active), sides
-        )
-        halo_1.arrive(waits_1[volume])
+        build_inner(taps_h, volume, own_row, sides)
+        halo.arrive(waits)
         build_outer(
             taps_h, volume,
-            lambda at_x, at_y, volume=volume: active(rows_1[volume, at_x, at_y].astype(F32)),
+            lambda at_x, at_y: active(rows_1[volume, at_x, at_y].astype(F32)),
             sides,
         )
-        if volume == 0:
-
-            def emit(at_x, at_y, tile, carry):
-                total, squares = carry
-                conv_2[0, at_x, at_y] = tile
-                return total + tile, squares + tile * tile
-
-            total, squares = convolve(taps_h, 0, 1, emit, (zero,) * 2)
-        else:
-
-            def emit(at_x, at_y, tile, carry):
-                total, squares, first, last = carry
-                conv_2[1, at_x, at_y] = tile
+
+        def emit(at_x, at_y, tile, carry):
+            conv_2[volume, at_x, at_y] = tile
+            total, squares, *columns = carry
+            if volume == 1:
                 rows_2[0, at_x + 1, at_y + 1] = tile.astype(BF16)
-                first, last = extract(tile, 16 * at_x + at_y, (first, last))
-                return total + tile, squares + tile * tile, first, last
-
-            total, squares, first, last = convolve(taps_h, 1, 1, emit, (zero, zero, none, none))
-            halo_2.put_edge(first, last, lane)
-        columns += [
-            jnp.sum(total, axis=1, keepdims=True), jnp.sum(squares, axis=1, keepdims=True)
-        ]
-    mean_1, scale_1 = mean, scale
-    totals[1].start(pack(columns))
+                columns = extract(tile, 16 * at_x + at_y, columns)
+            return total + tile, squares + tile * tile, *columns
+
+        start = (zero, zero) + ((none, none) if volume == 1 else ())
+        total, squares, *columns = convolve(taps_h, volume, 1, emit, start)
+        if volume == 1:
+            halo_2.put_edge(*columns, lane)
+        return both_sums(total, squares)
+
+    sums_b = first_layer(1)
+    totals[0].start(pack(sums_b))
+    near, rest = halo_b.small()
+    face_b = halo_b.faces_x(0)
+    sums_a = first_layer(0)
+    near_a, rest_a = halo_a.small()
+    face_a = halo_a.faces_x(0)
+    mean_1, scale_1 = moments(*unpack(totals[0].finish(), 2))
+    halo_b.arrive(near + rest)
+    waits_g = halo_x.faces_x(2)
+    sums_b = second_layer(1, mean_1, scale_1, face_b)
+    totals[1].start(pack(sums_b + sums_a))
     near, rest = halo_2.small()
     waits = near + rest + halo_2.faces_x(0)
     kernel_grad(taps_x, 1, [norms], early_out, True)
@@ -670,7 +665,7 @@
     early_in[flat] = early_out[flat]
     stats = unpack(totals[1].finish(), 4)
 
-    mean_2, scale_2 = moments(stats[2], stats[3])
+    mean_2, scale_2 = moments(stats[0], stats[1])
 
     def layer_of(mean, scale, gain, bias):
         norm_slope = jnp.broadcast_to(scale, (C, LANES))
@@ -723,24 +718,11 @@
     )
     totals[2].start(pack(columns))
 
-    mean_a, scale_a = moments(stats[0], stats[1])
-    slope_a = jnp.broadcast_to(gain_2 * scale_a, (C, LANES))
-    shift_a = jnp.broadcast_to(bias_2 - mean_a * gain_2 * scale_a, (C, LANES))
-    for at_x in range(SPAN_X):
-
-        def step(block, carry, at_x=at_x):
-            for k in range(8):
-                at_y = block * 8 + k
-                pre = conv_2[0, at_x, at_y] * slope_a + shift_a
-                stage[at_x, at_y] = pre * sigmoid(pre)
-            return carry
-
-        unrolled(0, 2, step, 0)
-        y_out[:, at_x] = jnp.swapaxes(stage[at_x], 0, 1).astype(BF16)
-
     kernel_grad(taps_h, 1, [slopes_2, norms_2], mid_out, True)
     fan_out(lambda to: mid_out.at[to], mid_in.at[flat], gw_send.at[1], gw_recv.at[1])
     mid_in[flat] = mid_out[flat]
+    halo_a.arrive(near_a + rest_a)
+    sums_a = second_layer(0, *moments(stats[2], stats[3]), face_a)
     halo_x.arrive(waits_g)
     halo_2.arrive(waits)
     sum_d2, sum_x2 = unpack(totals[2].finish(), 2)
@@ -777,13 +759,13 @@
     columns = [
         jnp.sum(total, axis=1, keepdims=True), jnp.sum(weighted, axis=1, keepdims=True)
     ]
-    totals[3].start(pack(columns))
+    totals[3].start(pack(columns + sums_a))
     near, rest = halo_e.small()
     kernel_grad(taps_x, 1, [slopes], late_out, False)
     fan_out(lambda to: late_out.at[to], late_in.at[flat], gw_send.at[2], gw_recv.at[2])
     waits = near + rest + halo_e.faces_x(0)
     late_in[flat] = late_out[flat]
-    sum_d1, sum_x1 = unpack(totals[3].finish(), 2)
+    sum_d1, sum_x1, *sums_a = unpack(totals[3].finish(), 4)
 
     whole = 1.0 / math.sqrt(voxels)
     for k, factor in enumerate(
@@ -834,6 +816,21 @@
     for at_x in range(SPAN_X):
         dx_out[:, at_x] = jnp.swapaxes(stage[at_x], 0, 1).astype(BF16)
 
+    mean_a, scale_a = moments(*sums_a)
+    slope_a = jnp.broadcast_to(gain_2 * scale_a, (C, LANES))
+    shift_a = jnp.broadcast_to(bias_2 - mean_a * gain_2 * scale_a, (C, LANES))
+    for at_x in range(SPAN_X):
+
+        def step(block, carry, at_x=at_x):
+            for k in range(8):
+                at_y = block * 8 + k
+                pre = conv_2[0, at_x, at_y] * slope_a + shift_a
+                stage[at_x, at_y] = pre * sigmoid(pre)
+            return carry
+
+        unrolled(0, 2, step, 0)
+        y_out[:, at_x] = jnp.swapaxes(stage[at_x], 0, 1).astype(BF16)
+
     for k, total in enumerate((sum_x1, sum_d1, sum_x2, sum_d2)):
         norm_out[k : k + 1] = whole * jnp.sum(
             jnp.where(small_lane == small_row, total, 0.0), axis=0, keepdims=True
@@ -886,8 +883,11 @@
     scratch += [sized(count, PAD_X, PAD_Y, TAPS, LANES) for count in (2, 2, 1, 1)]
     scratch += [sized(count, PAD_X, PAD_Y, C, LANES) for count in volumes]
     heights = [C if count == 3 else C // 2 for count in volumes]
-    scratch += [sized(2, 3, 3, height, LANES) for height in heights]
-    scratch += [sized(2, height, LANES) for height in heights]
+    pairs = [(2,) if count == 2 else () for count in volumes]
+    scratch += [
+        sized(*pair, 2, 3, 3, height, LANES) for pair, height in zip(pairs, heights)
+    ]
+    scratch += [sized(*pair, 2, height, LANES) for pair, height in zip(pairs, heights)]
     scratch += [sized(count, 2, C, LANES) for count in volumes] + [sized(2, 2, C, LANES)]
     scratch += [
         sized(2, SPAN_X, SPAN_Y, C, LANES, kind=F32),
@@ -900,8 +900,8 @@
         *[sized(devices, 2, LANES, kind=F32)] * 2,
         sized(devices, 4, LANES, kind=F32),
         sized(6, 16, 2, LANES, kind=F32),
-        pltpu.SemaphoreType.DMA((4, 32)),
-        pltpu.SemaphoreType.DMA((4, 32)),
+        pltpu.SemaphoreType.DMA((5, 32)),
+        pltpu.SemaphoreType.DMA((5, 32)),
         pltpu.SemaphoreType.DMA((4,)),
         pltpu.SemaphoreType.DMA((4,)),
         pltpu.SemaphoreType.DMA((4,)),

time: 64.3 us -> 62.5 us (0.972)
  Pallas kernels: 63.4 us -> 61.6 us
    pallas_call x1, Pallas kernels: 62.3 us -> 60.4 us  [body(): pl.pallas_call(functools.partial(kernel, voxels), out_shape=out_shape, in...]
where the time goes in v10:
time: 62.5 us; the launch traced here: 62.4 us
  Pallas kernels  61.6 us (99%)
  between operations  0.8 us (1%)
    pallas_call x1, Pallas kernels, body(): pl.pallas_call(functools.partial(kernel, voxels), out_shape=out_shape, in...  60.4 us

profile of v10, /device:TPU:1, one launch (start us, length us, event | category | flops | bytes accessed | tf_op | source)
XLA Modules:
  0.0 62.4 jit_solution(12492515879670437440)
XLA Ops:
  0.6 60.4 %shard_map.128 = (bf16[32,2,16,128]{3,2,1,0:T(8,128)(2,1)S(1)}, bf16[32,2,16,128]{3,2,1,0:T(8,128)(2,1)S(1)}, f32[27,32,32]{2,1,0:T(8,128)S(1)}, f32[27,32,32]{2,1,0:T(8,128)S(1)}, f32[4,32]{1,0:T(4,128)S(1)}) custom-call(bf16[32,2,16,128]{3,2,1,0:T(8,128)(2,1)} %x_a.1, bf16[32,2,16,128]{3,2,1,0:T(8,128)(2,1)} %x_b.1, bf16[32,2,16,128]{3,2,1,0:T(8,128)(2,1)} %grad.1, ...), custom_call_target="tpu_custom_call" | custom-call | tf_op jit(solution)/shard_map/pallas_call | solution.py:921
  61.1 1.1 %shard_map.129 = (bf16[32,2,16,128]{3,2,1,0:T(8,128)(2,1)}, bf16[32,2,16,128]{3,2,1,0:T(8,128)(2,1)}, f32[27,32,32]{2,1,0:T(8,128)}, f32[27,32,32]{2,1,0:T(8,128)}, f32[4,32]{1,0:T(4,128)}) custom-call(bf16[32,2,16,128]{3,2,1,0:T(8,128)(2,1)S(1)} %get-tuple-element.15.refs_0_, bf16[32,2,16,128]{3,2,1,0:T(8,128)(2,1)S(1)} %get-tuple-element.16.refs_1_, ...), custom_call_target="tpu_custom_call" | custom-call | tf_op jit(solution)/shard_map/pallas_call | solution.py:936

commit v11 on v10

--- a/solution.py
+++ b/solution.py
@@ -835,6 +835,12 @@
         norm_out[k : k + 1] = whole * jnp.sum(
             jnp.where(small_lane == small_row, total, 0.0), axis=0, keepdims=True
         )
+    for halo in halos:
+        halo.drain()
+    for total in totals:
+        total.drain()
+    for k, chunks in enumerate((early_out, mid_out, late_out)):
+        fan_in(chunks, gw_send.at[k])
     fan_in(gathered, gw_recv.at[3])
     for member, out in ((0, gw_first), (1, gw_second)):
         for k in range(7):
@@ -848,12 +854,7 @@
             for tap in range(4 * k, min(4 * k + 4, 27)):
                 out[tap] = tile[:, C * (tap % 4) : C * (tap % 4) + C]
 
-    for halo in halos:
-        halo.drain()
-    for total in totals:
-        total.drain()
-    for k, chunks in enumerate((early_out, mid_out, late_out, gathered)):
-        fan_in(chunks, gw_send.at[k])
+    fan_in(gathered, gw_send.at[3])
 
 
 def write_out(*refs):

time: 62.5 us -> 62.3 us (level)
  no operation moved by 1% of the time
where the time goes in v11:
time: 62.3 us; the launch traced here: 62.2 us
  Pallas kernels  61.4 us (99%)
  between operations  0.8 us (1%)
    pallas_call x1, Pallas kernels, body(): pl.pallas_call(functools.partial(kernel, voxels), out_shape=out_shape, in...  60.3 us

profile of v11, /device:TPU:1, one launch (start us, length us, event | category | flops | bytes accessed | tf_op | source)
XLA Modules:
  0.0 62.2 jit_solution(9963563402386110905)
XLA Ops:
  0.6 60.3 %shard_map.128 = (bf16[32,2,16,128]{3,2,1,0:T(8,128)(2,1)S(1)}, bf16[32,2,16,128]{3,2,1,0:T(8,128)(2,1)S(1)}, f32[27,32,32]{2,1,0:T(8,128)S(1)}, f32[27,32,32]{2,1,0:T(8,128)S(1)}, f32[4,32]{1,0:T(4,128)S(1)}) custom-call(bf16[32,2,16,128]{3,2,1,0:T(8,128)(2,1)} %x_a.1, bf16[32,2,16,128]{3,2,1,0:T(8,128)(2,1)} %x_b.1, bf16[32,2,16,128]{3,2,1,0:T(8,128)(2,1)} %grad.1, ...), custom_call_target="tpu_custom_call" | custom-call | tf_op jit(solution)/shard_map/pallas_call | solution.py:922
  60.9 1.1 %shard_map.129 = (bf16[32,2,16,128]{3,2,1,0:T(8,128)(2,1)}, bf16[32,2,16,128]{3,2,1,0:T(8,128)(2,1)}, f32[27,32,32]{2,1,0:T(8,128)}, f32[27,32,32]{2,1,0:T(8,128)}, f32[4,32]{1,0:T(4,128)}) custom-call(bf16[32,2,16,128]{3,2,1,0:T(8,128)(2,1)S(1)} %get-tuple-element.15.refs_0_, bf16[32,2,16,128]{3,2,1,0:T(8,128)(2,1)S(1)} %get-tuple-element.16.refs_1_, ...), custom_call_target="tpu_custom_call" | custom-call | tf_op jit(solution)/shard_map/pallas_call | solution.py:937
